TPU v7x, 128 devices: a whole 4x4x4 slice. The times are simulated.
128 devices in a mesh: dp: 16 (over x, z), mp: 8 (over y, core).
Axes of the slice: x: 4, y: 4, z: 4, core: 2. Of those that a mesh axis runs over, the one named last changes fastest.
Arguments:
- hidden_in: bfloat16 [2, 2048, 3584], P(None, 'dp', 'mp'), may hold values from -6 to 6
- out_grad: bfloat16 [2, 2048, 3584], P(None, 'dp', 'mp'), may hold values from -3072 to 3072
- pack_fill: int32 [2, 16], P(None, 'dp'), may hold values from 1 to 128, as said below
- norm_gain: float32 [3584], P('mp'), may hold values from 0.5 to 1.5
- up_weight: bfloat16 [3584, 7168], P(None, 'mp'), may hold values from -0.09375 to 0.09375
- down_weight: bfloat16 [7168, 3584], P('mp'), may hold values from -0.0625 to 0.0625
Outputs:
- in_grad: bfloat16 [2, 2048, 3584], P(None, 'dp', 'mp')
- up_grad: float32 [3584, 7168], P('dp', 'mp')
- down_grad: float32 [7168, 3584], P('mp', 'dp')
- gain_grad: float32 [3584], P('mp')
Inputs may be any that keep to these rules, and one draw needn't show every extreme that they name: pack_fill[m, p] real tokens stand at the start of pack p of microbatch m (positions p * 128 onward); the other positions of the pack are padding and carry no loss. In every draw the last pack of the first microbatch is full.
All inputs are finite; a program needn't handle non-finite values.
Results may differ from a plain program's by a relative error of at most 0.014.
Values may be sent and summed in bfloat16 or wider, within the bound.
No kernel may reach another device: no remote copies, remote signals or barrier semaphores. Data moves between devices by JAX's collectives and lax.ppermute only.
A program may use at most 128 MiB of HBM per device.

v0:
```python
import functools

import jax
import jax.numpy as jnp
from jax import lax
from jax.sharding import Mesh
from jax.sharding import PartitionSpec as P

TOK_DEV = 128
MICRO = 2
BLOCK = 128
DP = ("dp_0", "dp_1")


epsilon = 1e-06


def gather_turned(arrays, axis, dims):
    turned = [jnp.moveaxis(a, dim, 0) for a, dim in zip(arrays, dims)]
    widths = [t[0].size for t in turned]
    both = jnp.concatenate([t.reshape(-1, w) for t, w in zip(turned, widths)], axis=1)
    out = lax.all_gather(both, axis, axis=0, tiled=True)
    parts = jnp.split(out, [sum(widths[:k]) for k in range(1, len(widths))], axis=1)
    return tuple(
        (
            jnp.moveaxis(b.reshape(-1, *t.shape[1:]), 0, dim)
            for b, t, dim in zip(parts, turned, dims)
        )
    )


def cut_along(shard, dim, length):
    lengths = shard.shape
    parts = shard.reshape(*lengths[:dim], length, lengths[dim] // length, *lengths[dim + 1 :])
    return jnp.moveaxis(parts, dim, 0)


def sum_at_owner(shard, axis, dim):
    parts = cut_along(shard, dim, lax.axis_size(axis))
    arrived = lax.all_to_all(parts, axis, split_axis=0, concat_axis=0, tiled=True)
    return arrived.astype(jnp.float32).sum(axis=0)


def copy_for_each(shard, axis):
    copies = jnp.broadcast_to(shard, (lax.axis_size(axis), *shard.shape))
    return lax.all_to_all(copies, axis, split_axis=0, concat_axis=0, tiled=True)


def over_copies(shard, axis):
    return copy_for_each(shard, axis).sum(axis=0)


def by_axis(shard, axes):
    return functools.reduce(lax.psum, axes, shard)


def gelu_tanh(value):
    return jax.nn.gelu(value, approximate=True)


def contract_rows(left, right):
    return lax.dot_general(
        left, right, (((0,), (0,)), ((), ())), preferred_element_type=jnp.float32
    )


def contract_cols(left, right):
    return lax.dot_general(
        left, right, (((1,), (1,)), ((), ())), preferred_element_type=jnp.float32
    )


def block_grads(tok_rows, grad_rows, live_mask, inv_count, weights):
    norm_gain, up_weight, down_weight = weights
    model_width = up_weight.shape[0]
    values = tok_rows.astype(jnp.float32)
    squares = lax.psum(jnp.sum(values * values, axis=1), "mp")
    inv_rms = lax.rsqrt(squares / model_width + epsilon)[:, None]
    normed = (values * inv_rms * norm_gain[None, :]).astype(jnp.bfloat16)
    scaled = (grad_rows.astype(jnp.float32) * live_mask[:, None] * inv_count).astype(jnp.bfloat16)
    normed_full, scaled_full = gather_turned((normed, scaled), "mp", (1, 1))
    pre_act = jnp.dot(normed_full, up_weight, preferred_element_type=jnp.float32)
    activated = gelu_tanh(pre_act).astype(jnp.bfloat16)
    grad_act = contract_cols(scaled_full, down_weight)
    grad_pre = jax.vjp(gelu_tanh, pre_act)[1](grad_act)[0].astype(jnp.bfloat16)
    grad_normed = sum_at_owner(contract_cols(grad_pre, up_weight).astype(jnp.bfloat16), "mp", 1)
    row_dot = (
        over_copies(jnp.sum(grad_pre.astype(jnp.float32) * pre_act, axis=1), "mp")[:, None]
        / inv_rms
    )
    cubed = inv_rms * inv_rms * inv_rms
    in_rows = (
        scaled.astype(jnp.float32)
        + norm_gain[None, :] * grad_normed * inv_rms
        - values * cubed * row_dot / model_width
    )
    gain_term = jnp.sum(grad_normed * values * inv_rms, axis=0)
    return (in_rows.astype(jnp.bfloat16), normed_full, grad_pre, activated, scaled_full, gain_term)


def run_rows(tok_rows, grad_rows, live_count, count_blocks, inv_count, weights, carried):
    out_rows = jnp.zeros(tok_rows.shape, jnp.bfloat16)

    def block_step(block_index, current):
        out_rows, down_acc, gain_acc, kept_terms = current
        row_start = block_index * BLOCK
        live_mask = (row_start + jnp.arange(BLOCK, dtype=jnp.int32) < live_count).astype(
            jnp.float32
        )
        in_rows, normed_full, grad_pre, activated, scaled_full, gain_term = block_grads(
            tok_rows, grad_rows, live_mask, inv_count, weights
        )
        out_rows = in_rows
        down_acc = down_acc + contract_rows(activated, scaled_full)
        gain_acc = gain_acc + gain_term
        kept_terms = (kept_terms[0] + contract_rows(normed_full, grad_pre),)
        return (out_rows, down_acc, gain_acc, kept_terms)

    out_rows, down_acc, gain_acc, kept_terms = lax.fori_loop(
        0, count_blocks, block_step, (out_rows,) + carried
    )
    return (out_rows, (down_acc, gain_acc, kept_terms))


def on_device(hidden_in, out_grad, pack_fill, norm_gain, up_weight, down_weight):
    weights = (norm_gain, up_weight, down_weight)
    shard_width = hidden_in.shape[2]
    ff_shard = up_weight.shape[1]
    model_width = up_weight.shape[0]
    down_acc = jnp.zeros((ff_shard, model_width), jnp.float32)
    gain_acc = jnp.zeros((shard_width,), jnp.float32)
    kept_terms = (jnp.zeros((model_width, ff_shard), jnp.float32),)
    carried = (down_acc, gain_acc, kept_terms)
    results = []
    token_total = over_copies(jnp.sum(pack_fill), DP)
    inv_count = 1.0 / jnp.asarray(token_total).astype(jnp.float32)
    for micro_index in range(MICRO):
        out_rows, carried = run_rows(
            hidden_in[micro_index],
            out_grad[micro_index],
            pack_fill[micro_index, 0],
            TOK_DEV // BLOCK,
            inv_count,
            weights,
            carried,
        )
        results.append(out_rows)
    in_grad = jnp.stack(results)
    down_acc, gain_acc, kept_terms = carried
    up_grad, down_grad = (
        lax.psum_scatter(
            kept_terms[0].astype(jnp.bfloat16), DP, scatter_dimension=0, tiled=True
        ).astype(jnp.float32),
        lax.psum_scatter(down_acc.astype(jnp.bfloat16), DP, scatter_dimension=1, tiled=True).astype(
            jnp.float32
        ),
    )
    gain_grad = by_axis(gain_acc, DP)
    return (in_grad, up_grad, down_grad, gain_grad)


def solution(mesh):
    split = Mesh(mesh.devices.reshape(4, 4, mesh.shape["mp"]), ("dp_0", "dp_1", "mp"))
    in_specs = (
        P(None, DP, "mp"),
        P(None, DP, "mp"),
        P(None, DP),
        P("mp"),
        P(None, "mp"),
        P("mp", None),
    )
    out_specs = (P(None, DP, "mp"), P(DP, "mp"), P("mp", DP), P("mp"))
    return jax.shard_map(
        on_device, mesh=split, in_specs=in_specs, out_specs=out_specs, check_vma=False
    )
```

profile of v0, /device:TPU:0, one launch (start us, length us, event | category | flops | bytes accessed | tf_op | source)
XLA Modules:
  0.0 278.4 jit_solution(17550048841849903523)
XLA Ops:
  7.2 1.3 reduce_sum.122
  8.5 1.2 broadcast_in_dim.32
  9.7 8.0 %all-to-all-start = ((s32[16,1,1]{2,1,0:T(1,128)}), s32[16,1,1]{2,1,0:T(1,128)S(1)}, u32[]{:S(2)}, u32[]{:S(2)}) async-start(s32[16,1,1]{2,1,0:T(1,128)} %broadcast_in_dim.32), calls=%async_computation | async-start | bytes 16384 | tf_op jit(solution)/shard_map/all_to_all | solution.py:46
  17.7 0.0 all-gather.5.cloned.1.call-start
  17.8 1.3 fusion.92
  19.1 1.0 fusion.48
  20.1 14.7 %all-reduce = (f32[128]{0:T(128)S(1)}, f32[128]{0:T(128)S(1)}) all-reduce(f32[128]{0:T(128)S(1)} %get-tuple-element.57, f32[128]{0:T(128)S(1)} %get-tuple-element.56), channel_id=1, replica_groups=mesh['dp_0'=4,'dp_1'=4,'mp'=8] {'mp'}, use_global_device_ids=true, to_apply=%region_8.9 | all-reduce | flops 256 | bytes 2048 | tf_op jit(solution)/shard_map/while/body/eval_jaxpr/psum | solution.py:77
  34.8 1.1 fusion.79
  35.9 1.3 compare_convert_fusion
  37.3 0.7 reduce_sum.123
  38.6 1.0 fusion.81
  39.6 0.7 pad_maximum_fusion.1
  40.3 0.0 all-gather.5.cloned.1.call-update
  40.4 0.0 all-gather.3.cloned.1.call-start
  40.4 0.7 pad_maximum_fusion
  41.2 0.0 reduce-scatter.5.cloned.1.call-start
  41.2 22.9 %all-gather.5.cloned.1.call-done = bf16[3584,256]{1,0:T(8,128)(2,1)} async-done(((bf16[448,256]{1,0:T(8,128)(2,1)}), bf16[3584,256]{1,0:T(8,128)(2,1)}) %all-gather.5.cloned.1.call-update) | async-done | bytes 1835024 | tf_op jit(solution)/shard_map/while/body/eval_jaxpr/all_gather | solution.py:22
  64.1 4.3 %fusion.1 = f32[128,896]{1,0:T(8,128)S(1)} fusion(bf16[3584,896]{1,0:T(8,128)(2,1)} %param.10, bf16[3584,256]{1,0:T(8,128)(2,1)} %all-gather.5.cloned.1.call-done), kind=kOutput, calls=%fused_computation.7 | convolution fusion | flops 822083584 | bytes 7798784 | tf_op jit(solution)/shard_map/while/body/eval_jaxpr/dot_general | solution.py:82
  68.3 23.2 %all-gather.3.cloned.1.call-done = bf16[3584,256]{1,0:T(8,128)(2,1)} async-done(((bf16[448,256]{1,0:T(8,128)(2,1)}), bf16[3584,256]{1,0:T(8,128)(2,1)}) %all-gather.3.cloned.1.call-update) | async-done | bytes 1835024 | tf_op jit(solution)/shard_map/while/body/eval_jaxpr/all_gather | solution.py:22
  91.5 4.4 %fusion.8 = f32[128,896]{1,0:T(8,128)S(1)} fusion(bf16[3584,896]{1,0:T(8,128)(2,1)} %param.10, bf16[3584,256]{1,0:T(8,128)(2,1)} %all-gather.3.cloned.1.call-done), kind=kOutput, calls=%fused_computation.14 | convolution fusion | flops 822083584 | bytes 7798784 | tf_op jit(solution)/shard_map/while/body/eval_jaxpr/dot_general | solution.py:82
  95.9 1.9 fusion.10
  97.8 4.6 %add_convert_fusion = bf16[896,3584]{0,1:T(8,128)(2,1)} fusion(f32[896,3584]{0,1:T(8,128)S(1)} %fusion.10, bf16[3584,256]{1,0:T(8,128)(2,1)S(1)} %copy-done.1, f32[128,896]{1,0:T(8,128)S(1)} %fusion.1), kind=kOutput, calls=%fused_computation | convolution fusion | flops 829538304 | bytes 20643840 | tf_op jit(solution)/shard_map/while/body/eval_jaxpr/dot_general | solution.py:62
  102.4 0.2 reduce-scatter.3.cloned.1.call-start
  102.6 5.1 %multiply_reduce_fusion = (f32[128]{0:T(128)S(1)}, bf16[128,896]{1,0:T(8,128)(2,1)S(1)}) fusion(f32[128,896]{1,0:T(8,128)S(1)} %fusion.1, bf16[896,3584]{1,0:T(8,128)(2,1)} %param.11, bf16[3584,256]{1,0:T(8,128)(2,1)} %all-gather.5.cloned.1.call-done), kind=kOutput, calls=%fused_computation.40 | convolution fusion | flops 824721280 | bytes 8028672 | tf_op jit(solution)/shard_map/while/body/eval_jaxpr/dot_general | solution.py:68
  107.8 4.9 %multiply_reduce_fusion.1 = (f32[128]{0:T(128)S(1)}, bf16[128,896]{1,0:T(8,128)(2,1)S(1)}) fusion(f32[128,896]{1,0:T(8,128)S(1)} %fusion.8, bf16[896,3584]{1,0:T(8,128)(2,1)} %param.11, bf16[3584,256]{1,0:T(8,128)(2,1)S(1)} %copy-done), kind=kOutput, calls=%fused_computation.41 | convolution fusion | flops 824721280 | bytes 8028672 | tf_op jit(solution)/shard_map/while/body/eval_jaxpr/dot_general | solution.py:68
  112.6 1.8 fusion.6
  114.5 4.5 %add_convert_fusion.1 = bf16[3584,896]{1,0:T(8,128)(2,1)} fusion(f32[3584,896]{1,0:T(8,128)S(1)} %fusion.6, bf16[128,896]{1,0:T(8,128)(2,1)S(1)} %get-tuple-element.88, bf16[3584,256]{1,0:T(8,128)(2,1)S(1)} %copy-done.2), kind=kOutput, calls=%fused_computation.1 | convolution fusion | flops 828506112 | bytes 20414464 | tf_op jit(solution)/shard_map/while/body/eval_jaxpr/dot_general | solution.py:62
  119.0 8.4 %all_to_all.32 = f32[8,1,128]{2,1,0:T(1,128)S(1)} all-to-all(f32[8,1,128]{2,1,0:T(1,128)S(1)} %broadcast_in_dim.34), channel_id=1, replica_groups=mesh['dp_0'=4,'dp_1'=4,'mp'=8] {'mp'}, dimensions={0} | all-to-all | bytes 8192 | tf_op jit(solution)/shard_map/while/body/eval_jaxpr/all_to_all | solution.py:46
  127.4 0.6 broadcast_in_dim.33
  128.0 3.3 %all-to-all-start.2 = ((f32[8,1,128]{2,1,0:T(1,128)}), f32[8,1,128]{2,1,0:T(1,128)S(1)}, u32[]{:S(2)}, u32[]{:S(2)}) async-start(f32[8,1,128]{2,1,0:T(1,128)} %broadcast_in_dim.33), calls=%async_computation.2 | async-start | bytes 8192 | tf_op jit(solution)/shard_map/while/body/eval_jaxpr/all_to_all | solution.py:46
  131.3 5.1 %convolution_convert_fusion.1 = bf16[128,3584]{1,0:T(8,128)(2,1)S(1)} fusion(bf16[128,896]{1,0:T(8,128)(2,1)S(1)} %get-tuple-element.86, bf16[3584,896]{1,0:T(8,128)(2,1)} %param.10), kind=kOutput, calls=%fused_computation.3 | convolution fusion | flops 822542336 | bytes 7569408 | tf_op jit(solution)/shard_map/while/body/eval_jaxpr/dot_general | solution.py:68
  136.4 1.3 copy.15
  137.7 4.7 %all-to-all-start.1 = ((bf16[8,128,448]{1,2,0:T(8,128)(2,1)}), bf16[8,128,448]{1,2,0:T(8,128)(2,1)S(1)}, u32[]{:S(2)}, u32[]{:S(2)}) async-start(bf16[8,128,448]{1,2,0:T(8,128)(2,1)} %bitcast.6), calls=%async_computation.1 | async-start | bytes 1835008 | tf_op jit(solution)/shard_map/while/body/eval_jaxpr/all_to_all | solution.py:40
  142.4 5.1 %convolution_convert_fusion = bf16[128,3584]{1,0:T(8,128)(2,1)S(1)} fusion(bf16[128,896]{1,0:T(8,128)(2,1)S(1)} %get-tuple-element.88, bf16[3584,896]{1,0:T(8,128)(2,1)} %param.10), kind=kOutput, calls=%fused_computation.2 | convolution fusion | flops 822542336 | bytes 7569408 | tf_op jit(solution)/shard_map/while/body/eval_jaxpr/dot_general | solution.py:68
  147.6 1.3 copy.17
  148.8 8.1 %all-to-all-done.1 = bf16[8,128,448]{1,2,0:T(8,128)(2,1)S(1)} async-done(((bf16[8,128,448]{1,2,0:T(8,128)(2,1)}), bf16[8,128,448]{1,2,0:T(8,128)(2,1)S(1)}, u32[]{:S(2)}, u32[]{:S(2)}) %all-to-all-start.1) | async-done | bytes 917536 | tf_op jit(solution)/shard_map/while/body/eval_jaxpr/all_to_all | solution.py:40
  156.9 3.6 %all-to-all-start.3 = ((bf16[8,128,448]{1,2,0:T(8,128)(2,1)}), bf16[8,128,448]{1,2,0:T(8,128)(2,1)S(1)}, u32[]{:S(2)}, u32[]{:S(2)}) async-start(bf16[8,128,448]{1,2,0:T(8,128)(2,1)} %bitcast.15), calls=%async_computation.3 | async-start | bytes 1835008 | tf_op jit(solution)/shard_map/while/body/eval_jaxpr/all_to_all | solution.py:40
  160.6 0.1 convert_reduce_fusion.1
  160.7 14.3 %all-to-all-done.3 = bf16[8,128,448]{1,2,0:T(8,128)(2,1)S(1)} async-done(((bf16[8,128,448]{1,2,0:T(8,128)(2,1)}), bf16[8,128,448]{1,2,0:T(8,128)(2,1)S(1)}, u32[]{:S(2)}, u32[]{:S(2)}) %all-to-all-start.3) | async-done | bytes 917536 | tf_op jit(solution)/shard_map/while/body/eval_jaxpr/all_to_all | solution.py:40
  175.0 0.1 convert_reduce_fusion
  175.1 0.2 fusion.61
  175.3 10.4 %psum.32 = f32[448]{0:T(512)S(1)} all-reduce(f32[448]{0:T(512)S(1)} %add.96), channel_id=1, replica_groups=mesh['dp_0'=4,'dp_1'=4,'mp'=8] {'dp_0'}, use_global_device_ids=true, to_apply=%region_16.17 | all-reduce | flops 448 | bytes 3584 | tf_op jit(solution)/shard_map/psum | solution.py:54
  185.7 11.2 %psum.33 = f32[448]{0:T(512)} all-reduce(f32[448]{0:T(512)S(1)} %psum.32), channel_id=1, replica_groups=mesh['dp_0'=4,'dp_1'=4,'mp'=8] {'dp_1'}, use_global_device_ids=true, to_apply=%region_17.0 | all-reduce | flops 448 | bytes 3584 | tf_op jit(solution)/shard_map/psum | solution.py:54
  196.9 0.2 fusion.56
  197.1 0.7 pad_maximum_fusion.2
  197.9 1.9 convert_element_type.191
  199.8 70.1 %reduce-scatter.3.cloned.1.call-done = bf16[224,896]{1,0:T(8,128)(2,1)} async-done(((bf16[3584,896]{1,0:T(8,128)(2,1)}), bf16[224,896]{1,0:T(8,128)(2,1)}) %reduce-scatter.3.cloned.1.call-update) | async-done | bytes 401424 | tf_op jit(solution)/shard_map/reduce_scatter | solution.py:151
  269.9 1.9 convert_element_type.187
  (25 shorter events, 0.2 us)
Async XLA Ops:
  9.7 27.5 %all-to-all-start = ((s32[16,1,1]{2,1,0:T(1,128)}), s32[16,1,1]{2,1,0:T(1,128)S(1)}, u32[]{:S(2)}, u32[]{:S(2)}) async-start(s32[16,1,1]{2,1,0:T(1,128)} %broadcast_in_dim.32), calls=%async_computation | async-start | bytes 16384 | tf_op jit(solution)/shard_map/all_to_all | solution.py:46
  17.7 46.4 %all-gather.5.cloned.1.call-start = ((), (), s32[]{:S(2)}) async-start(), calls=%async_computation.8 | async-start | bytes 2064384 | tf_op jit(solution)/shard_map/while/body/eval_jaxpr/all_gather | solution.py:22
  40.4 51.1 %all-gather.3.cloned.1.call-start = ((), (), s32[]{:S(2)}) async-start(), calls=%async_computation.7 | async-start | bytes 2064384 | tf_op jit(solution)/shard_map/while/body/eval_jaxpr/all_gather | solution.py:22
  41.2 156.7 %reduce-scatter.5.cloned.1.call-start = ((), (), s32[]{:S(2)}) async-start(), calls=%async_computation.10 | async-start | bytes 6823936 | tf_op jit(solution)/shard_map/reduce_scatter | solution.py:154
  91.5 4.4 %copy-start = (bf16[3584,256]{1,0:T(8,128)(2,1)S(1)}, bf16[3584,256]{1,0:T(8,128)(2,1)}, u32[]{:S(2)}) copy-start(bf16[3584,256]{1,0:T(8,128)(2,1)} %all-gather.3.cloned.1.call-done) | copy-start | bytes 5505028
  95.9 1.9 copy-start.1
  102.4 167.5 %reduce-scatter.3.cloned.1.call-start = ((), (), s32[]{:S(2)}) async-start(), calls=%async_computation.9 | async-start | bytes 6823936 | tf_op jit(solution)/shard_map/reduce_scatter | solution.py:151
  112.6 1.8 copy-start.2
  128.0 9.7 %all-to-all-start.2 = ((f32[8,1,128]{2,1,0:T(1,128)}), f32[8,1,128]{2,1,0:T(1,128)S(1)}, u32[]{:S(2)}, u32[]{:S(2)}) async-start(f32[8,1,128]{2,1,0:T(1,128)} %broadcast_in_dim.33), calls=%async_computation.2 | async-start | bytes 8192 | tf_op jit(solution)/shard_map/while/body/eval_jaxpr/all_to_all | solution.py:46
  137.7 19.2 %all-to-all-start.1 = ((bf16[8,128,448]{1,2,0:T(8,128)(2,1)}), bf16[8,128,448]{1,2,0:T(8,128)(2,1)S(1)}, u32[]{:S(2)}, u32[]{:S(2)}) async-start(bf16[8,128,448]{1,2,0:T(8,128)(2,1)} %bitcast.6), calls=%async_computation.1 | async-start | bytes 1835008 | tf_op jit(solution)/shard_map/while/body/eval_jaxpr/all_to_all | solution.py:40
  142.4 32.7 %copy-start.3 = (bf16[2,128,448]{1,2,0:T(8,128)(2,1)S(1)}, bf16[2,128,448]{1,2,0:T(8,128)(2,1)}, u32[]{:S(2)}) copy-start(bf16[2,128,448]{1,2,0:T(8,128)(2,1)} %param.6) | copy-start | bytes 688132
  142.4 54.5 %copy-start.4 = (bf16[2,128,448]{1,2,0:T(8,128)(2,1)S(1)}, bf16[2,128,448]{1,2,0:T(8,128)(2,1)}, u32[]{:S(2)}) copy-start(bf16[2,128,448]{1,2,0:T(8,128)(2,1)} %param.7) | copy-start | bytes 688132
  142.4 54.5 %copy-start.5 = (f32[448]{0:T(512)S(1)}, f32[448]{0:T(512)}, u32[]{:S(2)}) copy-start(f32[448]{0:T(512)} %param.9) | copy-start | bytes 5380
  156.9 18.0 %all-to-all-start.3 = ((bf16[8,128,448]{1,2,0:T(8,128)(2,1)}), bf16[8,128,448]{1,2,0:T(8,128)(2,1)S(1)}, u32[]{:S(2)}, u32[]{:S(2)}) async-start(bf16[8,128,448]{1,2,0:T(8,128)(2,1)} %bitcast.15), calls=%async_computation.3 | async-start | bytes 1835008 | tf_op jit(solution)/shard_map/while/body/eval_jaxpr/all_to_all | solution.py:40
Sparse Core Ops, SparseCore 0:
  40.5 23.5 all-gather.4
  66.3 25.1 all-gather.2
  102.5 82.6 reduce-scatter.4
  188.5 81.3 reduce-scatter.2
where the time goes:
time: 279 us; the launch traced here: 278 us
  waiting for transfers between devices  139 us (50%)
  blocking collectives  44.7 us (16%)
  matrix products  41.6 us (15%)
  starting transfers between devices  19.9 us (7%)
  between operations  14.6 us (5%)
  other arithmetic  13.1 us (5%)
  local copies, waits for them, and re-layouts  5.77 us (2%)
    reduce_scatter x1, waiting for transfers between devices, on_device(): lax.psum_scatter(kept_terms[0].astype(jnp.bfloat16), DP, scatter_dimensio...  70.1 us
    all_gather x2, waiting for transfers between devices, gather_turned(): out = lax.all_gather(both, axis, axis=0, tiled=True)  46 us
    all_to_all x2, waiting for transfers between devices, sum_at_owner(): lax.all_to_all(parts, axis, split_axis=0, concat_axis=0, tiled=True)  22.4 us
    psum x2, blocking collectives, by_axis(): return functools.reduce(lax.psum, axes, shard)  21.6 us
    dot_general x4, matrix products, contract_cols(): lax.dot_general(left, right, (((1,), (1,)), ((), ())), preferred_element_...  20.2 us
    psum x1, blocking collectives, block_grads(): squares = lax.psum(jnp.sum(values * values, axis=1), 'mp')  14.7 us
    dot_general x4, matrix products, contract_rows(): lax.dot_general(left, right, (((0,), (0,)), ((), ())), preferred_element_...  12.8 us
    all_to_all x2, starting transfers between devices, copy_for_each(): return lax.all_to_all(copies, axis, split_axis=0, concat_axis=0, tiled=True)  11.3 us
  transfers between devices with their start and end apart: 8, of which 5 were waited for; matrix products, arithmetic and copies ran while one was open for 15% of the time, Pallas kernels for 0%

commit v1 on v0

v1 whole, which is shorter than its diff:
```python
import jax
import jax.numpy as jnp
from jax import lax
from jax.experimental import pallas as pl
from jax.experimental.pallas import tpu as pltpu
from jax.sharding import Mesh
from jax.sharding import PartitionSpec as P

INTERPRET = False
EPS = 1e-06
EXTRA = 16
GELU_A = 0.7978845608028654
GELU_B = 0.044715

F32 = jnp.float32
BF16 = jnp.bfloat16


def moved(value, axis, step):
    size = lax.axis_size(axis)
    return lax.ppermute(value, axis, [(i, (i + step) % size) for i in range(size)])


def ring_of(value, axis):
    return tuple(moved(value, axis, step) for step in (1, 2, 3))


def total_over(value, axes):
    for axis in axes:
        a, b, c = ring_of(value, axis)
        value = (value + b) + (a + c)
    return value


def spec(space=pltpu.VMEM):
    return pl.BlockSpec(memory_space=space)


def call(body, outs, ins, scratch=(), flops=0, moved_bytes=0, name="local"):
    return pl.pallas_call(
        body,
        out_shape=[jax.ShapeDtypeStruct(s, d) for s, d in outs],
        in_specs=[spec(space) for _, space in ins],
        out_specs=[spec() for _ in outs],
        scratch_shapes=list(scratch),
        cost_estimate=pl.CostEstimate(flops=flops, bytes_accessed=moved_bytes, transcendentals=0),
        compiler_params=pltpu.CompilerParams(vmem_limit_bytes=48 * 1024 * 1024),
        interpret=INTERPRET,
        name=name,
    )(*[a for a, _ in ins])


V, S, H = pltpu.VMEM, pltpu.SMEM, pl.ANY


def split3(value):
    hi = value.astype(BF16)
    rest = value - hi.astype(F32)
    mid = rest.astype(BF16)
    return hi, mid, (rest - mid.astype(F32)).astype(BF16)


def extra_rows(value):
    parts = [p.astype(F32) for p in split3(value)]
    row = lax.broadcasted_iota(jnp.int32, (EXTRA, value.shape[-1]), 0)
    out = jnp.where(row == 0, parts[0], 0.0)
    out = jnp.where(row == 1, parts[1], out)
    return jnp.where(row == 2, parts[2], out).astype(BF16)


def sum_extra(rows):
    return jnp.sum(rows.astype(F32), axis=0, keepdims=True)


def dot(left, right, dims):
    return lax.dot_general(left, right, (dims, ((), ())), preferred_element_type=F32)


def live_row(sc, tok):
    pos = lax.broadcasted_iota(jnp.int32, (1, 2 * tok), 1)
    in_first = pos < tok
    limit = jnp.where(in_first, sc[4], sc[5] + tok)
    return (pos < limit).astype(F32)


def prepare(hidden_t, gain_mat):
    micro, width, tok = hidden_t.shape

    def body(h_ref, g_ref, out_ref):
        for m in range(micro):
            h = h_ref[m].astype(F32)
            out_ref[m, :width, :] = (h * g_ref[...]).astype(BF16)
            out_ref[m, width:, :] = extra_rows(jnp.sum(h * h, axis=0, keepdims=True))

    return call(body, [((micro, width + EXTRA, tok), BF16)], [(hidden_t, V), (gain_mat, V)], name="prepare")[0]


def forward_part(sc, up, own, other):
    micro, padded, tok = own[0].shape
    width = padded - EXTRA
    ff = up.shape[1]
    d = up.shape[0]
    pair = 2 * width
    cols = micro * tok

    def body(sc, up_ref, *refs):
        r, s = refs[0:4], refs[4:8]
        act_ref, pre_ref, inv_ref, hown_ref, h1, h2, h3, wbuf, hbuf, sem = refs[8:]
        x, y, c = sc[0], sc[1], sc[3]

        def fetch(k):
            start = pl.multiple_of(((y + 4 - k) % 4) * pair, pair)
            return pltpu.make_async_copy(up_ref.at[pl.ds(start, pair), :], wbuf.at[k], sem.at[k])

        for k in range(4):
            fetch(k).start()
        mine = pl.multiple_of(c * width, width)
        its = pl.multiple_of((1 - c) * width, width)
        squares = []
        for m in range(micro):
            total = jnp.zeros((1, tok), F32)
            for k in range(4):
                hbuf[k, pl.ds(mine, width), m * tok : (m + 1) * tok] = r[k][m, :width, :]
                hbuf[k, pl.ds(its, width), m * tok : (m + 1) * tok] = s[k][m, :width, :]
                total = total + sum_extra(r[k][m, width:, :]) + sum_extra(s[k][m, width:, :])
            squares.append(total)
        inv = lax.rsqrt(jnp.concatenate(squares, axis=1) / d + EPS)
        inv_ref[...] = jnp.broadcast_to(inv, inv_ref.shape)
        hown_ref[...] = hbuf[(y - x + 4) % 4]
        for k, ref in ((1, h1), (2, h2), (3, h3)):
            ref[...] = hbuf[(y - x - k + 8) % 4, pl.ds(mine, width), :]
        acc = None
        for k in range(4):
            fetch(k).wait()
            part = dot(hbuf[k].T, wbuf[k], ((1,), (0,)))
            acc = part if acc is None else acc + part
        pre = acc.T * inv
        pre_ref[...] = pre
        act = 0.5 * pre * (1.0 + jnp.tanh(GELU_A * (pre + GELU_B * pre * pre * pre)))
        act_ref[...] = (act * live_row(sc, tok)).astype(BF16)

    return call(
        body,
        [
            ((ff, cols), BF16),
            ((ff, cols), F32),
            ((8, cols), F32),
            ((pair, cols), BF16),
        ]
        + [((width, cols), BF16)] * 3,
        [(sc, S), (up, H)] + [(a, V) for a in (*own, *other)],
        [
            pltpu.VMEM((4, pair, ff), BF16),
            pltpu.VMEM((4, pair, cols), BF16),
            pltpu.SemaphoreType.DMA((4,)),
        ],
        flops=2 * d * ff * cols,
        moved_bytes=d * ff * 2,
        name="forward_part",
    )


def backward_part(sc, down, own, other, pre, inv):
    micro, width, tok = own[0].shape
    ff = down.shape[0]
    d = down.shape[1]
    pair = 2 * width
    quarter = pair // 4
    cols = micro * tok

    def body(sc, down_ref, *refs):
        r, s = refs[0:4], refs[4:8]
        pre_ref, inv_ref, gp_ref, rd_ref, oown_ref, o1, o2, o3, wbuf, obuf, sem = refs[8:]
        y, z, c = sc[1], sc[2], sc[3]

        def fetch(k):
            start = pl.multiple_of(((y + 4 - k) % 4) * pair, pair)
            return pltpu.make_async_copy(down_ref.at[:, pl.ds(start, pair)], wbuf.at[k], sem.at[k])

        for k in range(4):
            fetch(k).start()
        mine = pl.multiple_of(c * width, width)
        its = pl.multiple_of((1 - c) * width, width)
        for m in range(micro):
            for k in range(4):
                obuf[k, pl.ds(mine, width), m * tok : (m + 1) * tok] = r[k][m]
                obuf[k, pl.ds(its, width), m * tok : (m + 1) * tok] = s[k][m]
        for k, ref in ((0, oown_ref), (1, o1), (2, o2), (3, o3)):
            row = pl.multiple_of(((z + k) % 4) * quarter, quarter)
            for j in range(4):
                block = obuf[j, pl.ds(row, quarter), :]
                ref[j] = block if k == 0 else jnp.where(c == 0, block[:, :tok], block[:, tok:])
        acc = None
        for k in range(4):
            fetch(k).wait()
            part = dot(wbuf[k], obuf[k], ((1,), (0,)))
            acc = part if acc is None else acc + part
        pre = pre_ref[...]
        cube = GELU_B * pre * pre
        t = jnp.tanh(GELU_A * (pre + cube * pre))
        slope = 0.5 * (1.0 + t) + 0.5 * pre * (1.0 - t * t) * (GELU_A * (1.0 + 3.0 * cube))
        gp = (acc * slope * (inv_ref[0:1, :] * live_row(sc, tok))).astype(BF16)
        gp_ref[...] = gp
        rd = jnp.sum(gp.astype(F32) * pre, axis=0, keepdims=True)
        rd_ref[...] = jnp.broadcast_to(rd, rd_ref.shape)

    return call(
        body,
        [
            ((ff, cols), BF16),
            ((8, cols), F32),
            ((4, quarter, cols), BF16),
        ]
        + [((4, quarter, tok), BF16)] * 3,
        [(sc, S), (down, H)] + [(a, V) for a in (*own, *other)] + [(pre, V), (inv, V)],
        [
            pltpu.VMEM((4, ff, pair), BF16),
            pltpu.VMEM((4, pair, cols), BF16),
            pltpu.SemaphoreType.DMA((4,)),
        ],
        flops=2 * d * ff * cols,
        moved_bytes=d * ff * 2,
        name="backward_part",
    )


def normed_part(sc, up, gp, rd):
    d, ff = up.shape
    pair = d // 4
    width = pair // 2
    cols = gp.shape[1]

    def body(sc, up_ref, gp_ref, rd_ref, pown_ref, psib_ref, wbuf, sem):
        y, c = sc[1], sc[3]

        def fetch(k):
            start = pl.multiple_of(((y + k) % 4) * pair, pair)
            return pltpu.make_async_copy(up_ref.at[pl.ds(start, pair), :], wbuf.at[k], sem.at[k])

        for k in range(4):
            fetch(k).start()
        mine = pl.multiple_of(c * width, width)
        its = pl.multiple_of((1 - c) * width, width)
        gp = gp_ref[...]
        for k in range(4):
            fetch(k).wait()
            psib_ref[k, :width, :] = dot(wbuf[k, pl.ds(its, width), :], gp, ((1,), (0,))).astype(BF16)
            pown_ref[k] = dot(wbuf[k, pl.ds(mine, width), :], gp, ((1,), (0,)))
            psib_ref[k, width:, :] = extra_rows(rd_ref[0:1, :])

    return call(
        body,
        [((4, width, cols), F32), ((4, width + EXTRA, cols), BF16)],
        [(sc, S), (up, H), (gp, V), (rd, V)],
        [pltpu.VMEM((4, pair, ff), BF16), pltpu.SemaphoreType.DMA((4,))],
        flops=2 * d * ff * cols,
        moved_bytes=d * ff * 2,
        name="normed_part",
    )


def pair_sum(pown, psib, rd):
    width, cols = pown.shape[1:]

    def body(p_ref, s_ref, rd_ref, q0, rd0, q1, q2, q3):
        total = rd_ref[0:1, :] + sum_extra(s_ref[0, width:, :])
        q0[...] = p_ref[0] + s_ref[0, :width, :].astype(F32)
        rd0[...] = jnp.broadcast_to(total, rd0.shape)
        tail = extra_rows(total)
        for k, ref in ((1, q1), (2, q2), (3, q3)):
            ref[:width, :] = (p_ref[k] + s_ref[k, :width, :].astype(F32)).astype(BF16)
            ref[width:, :] = tail

    return call(
        body,
        [((width, cols), F32), ((8, cols), F32)] + [((width + EXTRA, cols), BF16)] * 3,
        [(pown, V), (psib, V), (rd, V)],
        name="pair_sum",
    )


def input_grad(sc, q0, rd0, recv, hidden_t, out_t, gain_mat, inv, inv_count):
    micro, width, tok = hidden_t.shape

    def body(sc, q0, rd0, r1, r2, r3, h_ref, o_ref, g_ref, inv_ref, ic_ref, out_ref, gain_ref):
        d = 8 * width
        grad = q0[...]
        rd = rd0[0:1, :]
        for ref in (r1, r2, r3):
            grad = grad + ref[:width, :].astype(F32)
            rd = rd + sum_extra(ref[width:, :])
        live = live_row(sc, tok)
        ic = ic_ref[0:1, :]
        factor = inv_ref[0:1, :] * rd / d
        gain = jnp.zeros((width, tok), F32)
        for m in range(micro):
            cut = slice(m * tok, (m + 1) * tok)
            h = h_ref[m].astype(F32)
            scaled = (o_ref[m].astype(F32) * (live[:, cut] * ic)).astype(BF16).astype(F32)
            rest = g_ref[...] * grad[:, cut] - h * factor[:, cut]
            out_ref[m] = (scaled + rest * ic).astype(BF16)
            gain = gain + grad[:, cut] * h
        gain_ref[...] = jnp.sum(gain, axis=1, keepdims=True) * ic[:, :1]

    return call(
        body,
        [((micro, width, tok), BF16), ((width, 1), F32)],
        [(sc, S)] + [(a, V) for a in (q0, rd0, *recv, hidden_t, out_t, gain_mat, inv, inv_count)],
        name="input_grad",
    )


def up_part(sc, hown, mine, its, gps):
    pair, cols = hown.shape
    width = pair // 2
    ff = gps[0].shape[0]
    rows = pair // 4

    def body(sc, hown_ref, m1, m2, m3, i1, i2, i3, g0, g1, g2, g3, b0, b1, b2, b3, hbuf, gbuf, acc):
        z, c = sc[2], sc[3]
        lo = pl.multiple_of(c * width, width)
        hi = pl.multiple_of((1 - c) * width, width)
        hbuf[:, :cols] = hown_ref[...]
        for k, (a, b) in enumerate(((m1, i1), (m2, i2), (m3, i3)), 1):
            hbuf[pl.ds(lo, width), k * cols : (k + 1) * cols] = a[...]
            hbuf[pl.ds(hi, width), k * cols : (k + 1) * cols] = b[...]
        for k, g in enumerate((g0, g1, g2, g3)):
            gbuf[:, k * cols : (k + 1) * cols] = g[...]
        acc[...] = dot(hbuf[...], gbuf[...], ((1,), (1,)))
        for k, ref in enumerate((b0, b1, b2, b3)):
            start = pl.multiple_of(((z + k) % 4) * rows, rows)
            ref[...] = acc[pl.ds(start, rows), :].astype(ref.dtype)

    return call(
        body,
        [((rows, ff), F32)] + [((rows, ff), BF16)] * 3,
        [(sc, S)] + [(a, V) for a in (hown, *mine, *its, *gps)],
        [
            pltpu.VMEM((pair, 4 * cols), BF16),
            pltpu.VMEM((ff, 4 * cols), BF16),
            pltpu.VMEM((pair, ff), F32),
        ],
        flops=2 * pair * ff * cols * 4,
        name="up_part",
    )


def down_part(sc, oown, mine, its, acts):
    _, rows, cols = oown.shape
    tok = cols // 2
    ff = acts[0].shape[0]
    pair = 4 * rows

    def body(sc, oown_ref, m1, m2, m3, i1, i2, i3, a0, a1, a2, a3, b0, b1, b2, b3, obuf, abuf, acc):
        x, y, c = sc[0], sc[1], sc[3]
        for j in range(4):
            cut = slice(j * rows, (j + 1) * rows)
            obuf[cut, :cols] = oown_ref[j]
            for k, (a, b) in enumerate(((m1, i1), (m2, i2), (m3, i3)), 1):
                left, right = a[j], b[j]
                obuf[cut, k * cols : k * cols + tok] = jnp.where(c == 0, left, right)
                obuf[cut, k * cols + tok : (k + 1) * cols] = jnp.where(c == 0, right, left)
        for k, a in enumerate((a0, a1, a2, a3)):
            abuf[:, k * cols : (k + 1) * cols] = a[...]
        acc[...] = dot(obuf[...], abuf[...], ((1,), (1,)))
        for k, ref in enumerate((b0, b1, b2, b3)):
            start = pl.multiple_of(((y - x - k + 8) % 4) * rows, rows)
            ref[...] = acc[pl.ds(start, rows), :].astype(ref.dtype)

    return call(
        body,
        [((rows, ff), F32)] + [((rows, ff), BF16)] * 3,
        [(sc, S)] + [(a, V) for a in (oown, *mine, *its, *acts)],
        [
            pltpu.VMEM((pair, 4 * cols), BF16),
            pltpu.VMEM((ff, 4 * cols), BF16),
            pltpu.VMEM((pair, ff), F32),
        ],
        flops=2 * pair * ff * cols * 4,
        name="down_part",
    )


def at_owner(blocks, axis):
    return (blocks[0],) + tuple(moved(blocks[k], axis, k) for k in (1, 2, 3))


def add_up(blocks, inv_count):
    first, *rest = blocks

    def body(own, r1, r2, r3, ic_ref, out_ref):
        total = own[...] + r1[...].astype(F32) + (r2[...].astype(F32) + r3[...].astype(F32))
        out_ref[...] = total * ic_ref[0:1, 0:1]

    return call(body, [(first.shape, F32)], [(a, V) for a in (first, *rest, inv_count)], name="add_up")[0]


def on_device(hidden_in, out_grad, pack_fill, norm_gain, up_weight, down_weight):
    hidden_t = jnp.swapaxes(hidden_in, 1, 2)
    out_t = jnp.swapaxes(out_grad, 1, 2)
    _, width, tok = hidden_t.shape
    fills = pack_fill[:, 0]
    place = [lax.axis_index(a) for a in ("x", "y", "z", "c")]
    sc = jnp.concatenate([jnp.stack(place).astype(jnp.int32), fills, jnp.zeros((2,), jnp.int32)])
    gain_mat = jnp.broadcast_to(norm_gain[:, None], (width, tok))

    payload = prepare(hidden_t, gain_mat)
    h_own = (payload,) + ring_of(payload, "y")
    h_other = tuple(moved(a, "c", 1) for a in h_own)
    o_own = (out_t,) + ring_of(out_t, "y")
    o_other = tuple(moved(a, "c", 1) for a in o_own)

    count = jnp.broadcast_to(jnp.sum(fills).astype(F32), (8, 128))
    inv_count = 1.0 / total_over(count, ("x", "z"))

    act, pre, inv, h_home, *h_send = forward_part(sc, up_weight, h_own, h_other)
    acts = (act,) + ring_of(act, "z")
    h_mine = tuple(moved(a, "x", k) for k, a in enumerate(h_send, 1))
    h_its = tuple(moved(a, "c", 1) for a in h_mine)

    gp, rd, o_home, *o_send = backward_part(sc, down_weight, o_own, o_other, pre, inv)
    gps = (gp,) + ring_of(gp, "x")
    o_mine = tuple(moved(a, "z", k) for k, a in enumerate(o_send, 1))
    o_its = tuple(moved(a, "c", 1) for a in o_mine)

    pown, psib = normed_part(sc, up_weight, gp, rd)
    q0, rd0, *q_send = pair_sum(pown, moved(psib, "c", 1), rd)
    q_recv = tuple(moved(a, "y", k) for k, a in enumerate(q_send, 1))
    in_t, gain = input_grad(sc, q0, rd0, q_recv, hidden_t, out_t, gain_mat, inv, inv_count)
    gain_grad = total_over(gain[:, 0], ("x", "z"))

    down_blocks = at_owner(down_part(sc, o_home, o_mine, o_its, acts), "x")
    up_blocks = at_owner(up_part(sc, h_home, h_mine, h_its, gps), "z")
    down_grad = add_up(down_blocks, inv_count).T
    up_grad = add_up(up_blocks, inv_count)
    return (jnp.swapaxes(in_t, 1, 2), up_grad, down_grad, gain_grad)


def solution(mesh):
    split = Mesh(mesh.devices.reshape(4, 4, 4, 2), ("x", "z", "y", "c"))
    dp, mp = ("x", "z"), ("y", "c")
    in_specs = (
        P(None, dp, mp),
        P(None, dp, mp),
        P(None, dp),
        P(mp),
        P(None, mp),
        P(mp, None),
    )
    out_specs = (P(None, dp, mp), P(dp, mp), P(mp, dp), P(mp))
    return jax.shard_map(
        on_device, mesh=split, in_specs=in_specs, out_specs=out_specs, check_vma=False
    )
```

time: 279 us -> 167 us (0.60)
  waiting for transfers between devices: 139 us -> 59.6 us
  blocking collectives: 44.7 us -> 0 us
  starting transfers between devices: 19.9 us -> 63.4 us
  matrix products: 41.6 us -> 0 us
  Pallas kernels: 0 us -> 30.4 us
  between operations: 14.6 us -> 1.61 us
  other arithmetic: 13.1 us -> 1.38 us
  local copies, waits for them, and re-layouts: 5.77 us -> 10 us
    reduce_scatter x2 -> x0, waiting for transfers between devices: 70.1 us -> none  [the longest x1 70.1 us: on_device(): lax.psum_scatter(kept_terms[0].astype(jnp.bfloat16), DP, scatter_dimensio...]
    ppermute x0 -> x54, starting transfers between devices: none -> 63.4 us  [moved(): lax.ppermute(value, axis, [(i, (i + step) % size) for i in range(size)])]
    ppermute x0 -> x54, waiting for transfers between devices: none -> 59.6 us  [moved(): lax.ppermute(value, axis, [(i, (i + step) % size) for i in range(size)])]
    all_gather x2 -> x0, waiting for transfers between devices: 46 us -> none  [gather_turned(): out = lax.all_gather(both, axis, axis=0, tiled=True)]
    dot_general x10 -> x0, matrix products: 41.6 us -> none  [the longest x4 20.2 us: contract_cols(): lax.dot_general(left, right, (((1,), (1,)), ((), ())), preferred_element_...]
    psum x3 -> x0, blocking collectives: 36.3 us -> none  [the longest x2 21.6 us: by_axis(): return functools.reduce(lax.psum, axes, shard)]
    pallas_call x0 -> x10, Pallas kernels: none -> 30.4 us  [call(): pl.pallas_call(body, out_shape=[jax.ShapeDtypeStruct(s, d) for s, d in ou...]
    all_to_all x4 -> x0, waiting for transfers between devices: 22.4 us -> none  [the longest x2 22.4 us: sum_at_owner(): lax.all_to_all(parts, axis, split_axis=0, concat_axis=0, tiled=True)]
  transfers between devices with their start and end apart: 8 -> 54, of which waited for: 5 -> 17; matrix products, arithmetic and copies ran while one was open for 15% -> 1% of each run, Pallas kernels for 0% -> 10%
where the time goes in v1:
time: 167 us; the launch traced here: 166 us
  starting transfers between devices  63.4 us (38%)
  waiting for transfers between devices  59.6 us (36%)
  Pallas kernels  30.4 us (18%)
  local copies, waits for them, and re-layouts  10 us (6%)
    ppermute x54, starting transfers between devices, moved(): lax.ppermute(value, axis, [(i, (i + step) % size) for i in range(size)])  63.4 us
    ppermute x54, waiting for transfers between devices, moved(): lax.ppermute(value, axis, [(i, (i + step) % size) for i in range(size)])  59.6 us
    pallas_call x10, Pallas kernels, call(): pl.pallas_call(body, out_shape=[jax.ShapeDtypeStruct(s, d) for s, d in ou...  30.4 us
    unnamed x48, local copies, waits for them, and re-layouts  8.42 us
  transfers between devices with their start and end apart: 54, of which 17 were waited for; matrix products, arithmetic and copies ran while one was open for 1% of the time, Pallas kernels for 10%

profile of v1, /device:TPU:0, one launch (start us, length us, event | category | flops | bytes accessed | tf_op | source)
XLA Modules:
  0.0 166.4 jit_solution(11964938766322722035)
XLA Ops:
  2.5 1.8 %collective-permute-start.7 = (bf16[2,464,128]{2,1,0:T(8,128)(2,1)S(1)}, bf16[2,464,128]{2,1,0:T(8,128)(2,1)S(1)}, u32[]{:S(2)}, u32[]{:S(2)}) collective-permute-start(bf16[2,464,128]{2,1,0:T(8,128)(2,1)S(1)} %prepare.1.refs_0_), channel_id=1, source_target_pairs={{0,2},{2,4},{4,6},{6,0},{1,3},{3,5},{5,7},{7,1},{8,10},{10,12},{12... | collective-permute-start | bytes 712712 | tf_op jit(solution)/shard_map/ppermute | solution.py:21
  4.3 2.9 %collective-permute-start.8 = (bf16[2,464,128]{2,1,0:T(8,128)(2,1)S(1)}, bf16[2,464,128]{2,1,0:T(8,128)(2,1)S(1)}, u32[]{:S(2)}, u32[]{:S(2)}) collective-permute-start(bf16[2,464,128]{2,1,0:T(8,128)(2,1)S(1)} %prepare.1.refs_0_), channel_id=1, source_target_pairs={{0,4},{2,6},{4,0},{6,2},{1,5},{3,7},{5,1},{7,3},{8,12},{10,14},{12... | collective-permute-start | bytes 712712 | tf_op jit(solution)/shard_map/ppermute | solution.py:21
  7.2 2.8 %collective-permute-start.1 = (bf16[2,448,128]{2,1,0:T(8,128)(2,1)}, bf16[2,448,128]{2,1,0:T(8,128)(2,1)S(1)}, u32[]{:S(2)}, u32[]{:S(2)}) collective-permute-start(bf16[2,448,128]{2,1,0:T(8,128)(2,1)} %bitcast.10), channel_id=1, source_target_pairs={{0,4},{2,6},{4,0},{6,2},{1,5},{3,7},{5,1},{7,3},{8,12},{10,14},{12... | collective-permute-start | bytes 688136 | tf_op jit(solution)/shard_map/ppermute | solution.py:21
  10.4 11.1 %collective-permute-done.refs_1_ = bf16[2,448,128]{2,1,0:T(8,128)(2,1)S(1)} collective-permute-done((bf16[2,448,128]{2,1,0:T(8,128)(2,1)}, bf16[2,448,128]{2,1,0:T(8,128)(2,1)S(1)}, u32[]{:S(2)}, u32[]{:S(2)}) %collective-permute-start) | collective-permute-done | bytes 229408 | tf_op jit(solution)/shard_map/ppermute | solution.py:21
  22.1 5.5 %collective-permute-done.1.refs_2_ = bf16[2,448,128]{2,1,0:T(8,128)(2,1)S(1)} collective-permute-done((bf16[2,448,128]{2,1,0:T(8,128)(2,1)}, bf16[2,448,128]{2,1,0:T(8,128)(2,1)S(1)}, u32[]{:S(2)}, u32[]{:S(2)}) %collective-permute-start.1) | collective-permute-done | bytes 229408 | tf_op jit(solution)/shard_map/ppermute | solution.py:21
  27.7 6.7 %collective-permute-done.2.refs_3_ = bf16[2,448,128]{2,1,0:T(8,128)(2,1)S(1)} collective-permute-done((bf16[2,448,128]{2,1,0:T(8,128)(2,1)}, bf16[2,448,128]{2,1,0:T(8,128)(2,1)S(1)}, u32[]{:S(2)}, u32[]{:S(2)}) %collective-permute-start.2) | collective-permute-done | bytes 229408 | tf_op jit(solution)/shard_map/ppermute | solution.py:21
  36.1 5.3 %forward_part.1 = (bf16[896,256]{1,0:T(8,128)(2,1)S(1)}, f32[896,256]{1,0:T(8,128)S(1)}, f32[8,256]{1,0:T(8,128)S(1)}, bf16[896,256]{1,0:T(8,128)(2,1)S(1)}, bf1...) custom-call(s32[8]{0:T(128)S(1)} %concatenate.3.sc, ...), custom_call_target="tpu_custom_call" | custom-call | flops 1644167168 | bytes 6422528 | tf_op jit(solution)/shard_map/forward_part/pallas_call | solution.py:40
  42.3 7.6 %backward_part.1 = (bf16[896,256]{1,0:T(8,128)(2,1)S(1)}, f32[8,256]{1,0:T(8,128)S(1)}, bf16[4,224,256]{2,1,0:T(8,128)(2,1)S(1)}, bf16[4,224,128]{2,1,0:T(8,128)...) custom-call(s32[8]{0:T(128)S(1)} %concatenate.3.sc, bf16[896,3584]{1,0:T(8,128)(2,1)} %down_ref.1, ...), custom_call_target="tpu_custom_call" | custom-call | flops 1644167168 | bytes 6422528 | tf_op jit(solution)/shard_map/backward_part/pallas_call | solution.py:40
  52.7 5.5 %normed_part.1 = (f32[4,448,256]{2,1,0:T(8,128)S(1)}, bf16[4,464,256]{2,1,0:T(8,128)(2,1)}) custom-call(s32[8]{0:T(128)S(1)} %concatenate.3.sc, bf16[3584,896]{1,0:T(8,128)(2,1)} %up_ref.3, bf16[896,256]{1,0:T(8,128)(2,1)S(1)} %get-tuple-element.36.gp_ref.g0, f32[8,256]{1,0:T(8,128)S(1)} %get-tuple-element.37.rd_ref), custom_call_target="tpu_custom_call" | custom-call | flops 1644167168 | bytes 6422528 | tf_op jit(solution)/shard_map/normed_part/pallas_call | solution.py:40
  60.0 3.1 %collective-permute-start.18 = (f32[8,128]{1,0:T(8,128)S(1)}, f32[8,128]{1,0:T(8,128)S(1)}, u32[]{:S(2)}, u32[]{:S(2)}) collective-permute-start(f32[8,128]{1,0:T(8,128)S(1)} %broadcast_in_dim.10), channel_id=1, source_target_pairs={{0,64},{32,96},{64,0},{96,32},{1,65},{33,97},{65,1},{97,33},{2,66}... | collective-permute-start | bytes 12296 | tf_op jit(solution)/shard_map/ppermute | solution.py:21
  63.7 2.6 %collective-permute-start.20 = (f32[8,128]{1,0:T(8,128)S(1)}, f32[8,128]{1,0:T(8,128)S(1)}, u32[]{:S(2)}, u32[]{:S(2)}) collective-permute-start(f32[8,128]{1,0:T(8,128)S(1)} %broadcast_in_dim.10), channel_id=1, source_target_pairs={{0,96},{32,0},{64,32},{96,64},{1,97},{33,1},{65,33},{97,65},{2,98}... | collective-permute-start | bytes 12296 | tf_op jit(solution)/shard_map/ppermute | solution.py:21
  66.3 1.9 %collective-permute-start.36 = (bf16[4,224,128]{2,1,0:T(8,128)(2,1)}, bf16[4,224,128]{2,1,0:T(8,128)(2,1)S(1)}, u32[]{:S(2)}, u32[]{:S(2)}) collective-permute-start(bf16[4,224,128]{2,1,0:T(8,128)(2,1)} %copy-done.22), channel_id=1, source_target_pairs={{0,8},{8,16},{16,24},{24,0},{1,9},{9,17},{17,25},{25,1},{2,10},{10... | collective-permute-start | bytes 688136 | tf_op jit(solution)/shard_map/ppermute | solution.py:21
  68.3 3.7 %collective-permute-start.21 = (f32[8,128]{1,0:T(8,128)S(1)}, f32[8,128]{1,0:T(8,128)S(1)}, u32[]{:S(2)}, u32[]{:S(2)}) collective-permute-start(f32[8,128]{1,0:T(8,128)S(1)} %add_add_fusion), channel_id=1, source_target_pairs={{0,16},{8,24},{16,0},{24,8},{1,17},{9,25},{17,1},{25,9},{2,18},{10... | collective-permute-start | bytes 12296 | tf_op jit(solution)/shard_map/ppermute | solution.py:21
  72.9 2.3 %collective-permute-start.23 = (f32[8,128]{1,0:T(8,128)S(1)}, f32[8,128]{1,0:T(8,128)S(1)}, u32[]{:S(2)}, u32[]{:S(2)}) collective-permute-start(f32[8,128]{1,0:T(8,128)S(1)} %add_add_fusion), channel_id=1, source_target_pairs={{0,24},{8,0},{16,8},{24,16},{1,25},{9,1},{17,9},{25,17},{2,26},{10... | collective-permute-start | bytes 12296 | tf_op jit(solution)/shard_map/ppermute | solution.py:21
  75.2 1.9 %collective-permute-done.21 = f32[8,128]{1,0:T(8,128)S(1)} collective-permute-done((f32[8,128]{1,0:T(8,128)S(1)}, f32[8,128]{1,0:T(8,128)S(1)}, u32[]{:S(2)}, u32[]{:S(2)}) %collective-permute-start.21) | collective-permute-done | bytes 4128 | tf_op jit(solution)/shard_map/ppermute | solution.py:21
  78.1 4.3 %collective-permute-start.25 = (bf16[448,256]{1,0:T(8,128)(2,1)}, bf16[448,256]{1,0:T(8,128)(2,1)}, u32[]{:S(2)}, u32[]{:S(2)}) collective-permute-start(bf16[448,256]{1,0:T(8,128)(2,1)} %copy-done.18), channel_id=1, source_target_pairs={{0,64},{32,96},{64,0},{96,32},{1,65},{33,97},{65,1},{97,33},{2,66}... | collective-permute-start | bytes 688136 | tf_op jit(solution)/shard_map/ppermute | solution.py:21
  82.3 2.5 %collective-permute-done.37.m2 = bf16[4,224,128]{2,1,0:T(8,128)(2,1)S(1)} collective-permute-done((bf16[4,224,128]{2,1,0:T(8,128)(2,1)}, bf16[4,224,128]{2,1,0:T(8,128)(2,1)S(1)}, u32[]{:S(2)}, u32[]{:S(2)}) %collective-permute-start.37) | collective-permute-done | bytes 229408 | tf_op jit(solution)/shard_map/ppermute | solution.py:21
  84.8 1.2 collective-permute-start.26
  86.3 1.3 collective-permute-done.24.m1
  87.6 2.5 %collective-permute-done.25.m2 = bf16[448,256]{1,0:T(8,128)(2,1)} collective-permute-done((bf16[448,256]{1,0:T(8,128)(2,1)}, bf16[448,256]{1,0:T(8,128)(2,1)}, u32[]{:S(2)}, u32[]{:S(2)}) %collective-permute-start.25) | collective-permute-done | bytes 229408 | tf_op jit(solution)/shard_map/ppermute | solution.py:21
  90.1 1.3 collective-permute-done.26.m3
  91.8 3.0 %collective-permute-start.43 = (bf16[896,256]{1,0:T(8,128)(2,1)}, bf16[896,256]{1,0:T(8,128)(2,1)S(1)}, u32[]{:S(2)}, u32[]{:S(2)}) collective-permute-start(bf16[896,256]{1,0:T(8,128)(2,1)} %copy-done.7), channel_id=1, source_target_pairs={{0,16},{8,24},{16,0},{24,8},{1,17},{9,25},{17,1},{25,9},{2,18},{10... | collective-permute-start | bytes 1376264 | tf_op jit(solution)/shard_map/ppermute | solution.py:21
  94.8 1.0 collective-permute-start.44
  96.1 3.9 %collective-permute-start.31 = (bf16[896,256]{1,0:T(8,128)(2,1)}, bf16[896,256]{1,0:T(8,128)(2,1)S(1)}, u32[]{:S(2)}, u32[]{:S(2)}) collective-permute-start(bf16[896,256]{1,0:T(8,128)(2,1)} %copy-done.3), channel_id=1, source_target_pairs={{0,64},{32,96},{64,0},{96,32},{1,65},{33,97},{65,1},{97,33},{2,66}... | collective-permute-start | bytes 1376264 | tf_op jit(solution)/shard_map/ppermute | solution.py:21
  100.2 4.3 %collective-permute-done.42.a1 = bf16[896,256]{1,0:T(8,128)(2,1)S(1)} collective-permute-done((bf16[896,256]{1,0:T(8,128)(2,1)}, bf16[896,256]{1,0:T(8,128)(2,1)S(1)}, u32[]{:S(2)}, u32[]{:S(2)}) %collective-permute-start.42) | collective-permute-done | bytes 458784 | tf_op jit(solution)/shard_map/ppermute | solution.py:21
  104.4 10.8 %collective-permute-done.43.a2 = bf16[896,256]{1,0:T(8,128)(2,1)S(1)} collective-permute-done((bf16[896,256]{1,0:T(8,128)(2,1)}, bf16[896,256]{1,0:T(8,128)(2,1)S(1)}, u32[]{:S(2)}, u32[]{:S(2)}) %collective-permute-start.43) | collective-permute-done | bytes 458784 | tf_op jit(solution)/shard_map/ppermute | solution.py:21
  115.9 1.7 %collective-permute-start.17 = (bf16[464,256]{1,0:T(8,128)(2,1)S(1)}, bf16[464,256]{1,0:T(8,128)(2,1)S(1)}, u32[]{:S(2)}, u32[]{:S(2)}) collective-permute-start(bf16[464,256]{1,0:T(8,128)(2,1)S(1)} %get-tuple-element.44), channel_id=1, source_target_pairs={{0,6},{2,0},{4,2},{6,4},{1,7},{3,1},{5,3},{7,5},{8,14},{10,8},{12,... | collective-permute-start | bytes 712712 | tf_op jit(solution)/shard_map/ppermute | solution.py:21
  117.6 1.0 collective-permute-done.30.g1
  119.4 1.0 copy-done.8
  120.4 1.0 copy-done.10
  121.5 3.6 %down_part.1 = (f32[224,896]{1,0:T(8,128)S(1)}, bf16[224,896]{1,0:T(8,128)(2,1)}, bf16[224,896]{1,0:T(8,128)(2,1)S(1)}, bf16[224,896]{1,0:T(8,128)(2,1)S(1)}) custom-call(s32[8]{0:T(128)S(1)} %concatenate.3.sc, bf16[4,224,256]{2,1,0:T(8,128)(2,1)S(1)} %copy-done.10, bf16[4,224,128]{2,1,0:T(8,128)(2,1)S(1)} %collective-permute-done.36.m1, ...), custom_call_target="tpu_custom_call" | custom-call | flops 1644167168 | tf_op jit(solution)/shard_map/down_part/pallas_call | solution.py:40
  125.0 2.1 %collective-permute-start.45 = (bf16[224,896]{1,0:T(8,128)(2,1)}, bf16[224,896]{1,0:T(8,128)(2,1)S(1)}, u32[]{:S(2)}, u32[]{:S(2)}) collective-permute-start(bf16[224,896]{1,0:T(8,128)(2,1)} %get-tuple-element.60), channel_id=1, source_target_pairs={{0,32},{32,64},{64,96},{96,0},{1,33},{33,65},{65,97},{97,1},{2,34}... | collective-permute-start | bytes 1204232 | tf_op jit(solution)/shard_map/ppermute | solution.py:21
  127.7 1.5 input_grad.1
  130.1 3.2 %collective-permute-start.48 = (f32[448]{0:T(512)S(1)}, f32[448]{0:T(512)S(1)}, u32[]{:S(2)}, u32[]{:S(2)}) collective-permute-start(f32[448]{0:T(512)S(1)} %reduce.1), channel_id=1, source_target_pairs={{0,64},{32,96},{64,0},{96,32},{1,65},{33,97},{65,1},{97,33},{2,66}... | collective-permute-start | bytes 5384 | tf_op jit(solution)/shard_map/ppermute | solution.py:21
  133.3 1.0 copy-done.14
  134.3 4.1 %up_part.1 = (f32[224,896]{1,0:T(8,128)S(1)}, bf16[224,896]{1,0:T(8,128)(2,1)S(1)}, bf16[224,896]{1,0:T(8,128)(2,1)S(1)}, bf16[224,896]{1,0:T(8,128)(2,1)S(1)}) custom-call(s32[8]{0:T(128)S(1)} %concatenate.3.sc, bf16[896,256]{1,0:T(8,128)(2,1)S(1)} %copy-done.6, bf16[448,256]{1,0:T(8,128)(2,1)} %collective-permute-done.24.m1, ...), custom_call_target="tpu_custom_call" | custom-call | flops 1644167168 | tf_op jit(solution)/shard_map/up_part/pallas_call | solution.py:40
  138.4 3.3 %collective-permute-start.50 = (f32[448]{0:T(512)S(1)}, f32[448]{0:T(512)S(1)}, u32[]{:S(2)}, u32[]{:S(2)}) collective-permute-start(f32[448]{0:T(512)S(1)} %reduce.1), channel_id=1, source_target_pairs={{0,96},{32,0},{64,32},{96,64},{1,97},{33,1},{65,33},{97,65},{2,98}... | collective-permute-start | bytes 5384 | tf_op jit(solution)/shard_map/ppermute | solution.py:21
  141.7 2.6 %collective-permute-done.45.r1 = bf16[224,896]{1,0:T(8,128)(2,1)S(1)} collective-permute-done((bf16[224,896]{1,0:T(8,128)(2,1)}, bf16[224,896]{1,0:T(8,128)(2,1)S(1)}, u32[]{:S(2)}, u32[]{:S(2)}) %collective-permute-start.45) | collective-permute-done | bytes 401440 | tf_op jit(solution)/shard_map/ppermute | solution.py:21
  144.2 2.0 %collective-permute-start.33 = (bf16[224,896]{1,0:T(8,128)(2,1)S(1)}, bf16[224,896]{1,0:T(8,128)(2,1)S(1)}, u32[]{:S(2)}, u32[]{:S(2)}) collective-permute-start(bf16[224,896]{1,0:T(8,128)(2,1)S(1)} %get-tuple-element.51), channel_id=1, source_target_pairs={{0,8},{8,16},{16,24},{24,0},{1,9},{9,17},{17,25},{25,1},{2,10},{10... | collective-permute-start | bytes 1204232 | tf_op jit(solution)/shard_map/ppermute | solution.py:21
  146.2 3.1 %collective-permute-start.34 = (bf16[224,896]{1,0:T(8,128)(2,1)S(1)}, bf16[224,896]{1,0:T(8,128)(2,1)S(1)}, u32[]{:S(2)}, u32[]{:S(2)}) collective-permute-start(bf16[224,896]{1,0:T(8,128)(2,1)S(1)} %get-tuple-element.52), channel_id=1, source_target_pairs={{0,16},{8,24},{16,0},{24,8},{1,17},{9,25},{17,1},{25,9},{2,18},{10... | collective-permute-start | bytes 1204232 | tf_op jit(solution)/shard_map/ppermute | solution.py:21
  149.3 1.6 collective-permute-start.51
  150.9 1.4 collective-permute-done.47.r3
  152.3 2.0 %collective-permute-start.52 = (f32[448]{0:T(512)S(1)}, f32[448]{0:T(512)S(1)}, u32[]{:S(2)}, u32[]{:S(2)}) collective-permute-start(f32[448]{0:T(512)S(1)} %add_add_fusion.2), channel_id=1, source_target_pairs={{0,8},{8,16},{16,24},{24,0},{1,9},{9,17},{17,25},{25,1},{2,10},{10... | collective-permute-start | bytes 5384 | tf_op jit(solution)/shard_map/ppermute | solution.py:21
  154.3 2.8 %collective-permute-done.33.r1 = bf16[224,896]{1,0:T(8,128)(2,1)S(1)} collective-permute-done((bf16[224,896]{1,0:T(8,128)(2,1)S(1)}, bf16[224,896]{1,0:T(8,128)(2,1)S(1)}, u32[]{:S(2)}, u32[]{:S(2)}) %collective-permute-start.33) | collective-permute-done | bytes 401440 | tf_op jit(solution)/shard_map/ppermute | solution.py:21
  157.1 2.9 %collective-permute-start.53 = (f32[448]{0:T(512)S(1)}, f32[448]{0:T(512)S(1)}, u32[]{:S(2)}, u32[]{:S(2)}) collective-permute-start(f32[448]{0:T(512)S(1)} %add_add_fusion.2), channel_id=1, source_target_pairs={{0,24},{8,0},{16,8},{24,16},{1,25},{9,1},{17,9},{25,17},{2,26},{10... | collective-permute-start | bytes 5384 | tf_op jit(solution)/shard_map/ppermute | solution.py:21
  160.0 1.2 add_up.3
  161.2 3.3 %collective-permute-done.34.r2 = bf16[224,896]{1,0:T(8,128)(2,1)S(1)} collective-permute-done((bf16[224,896]{1,0:T(8,128)(2,1)S(1)}, bf16[224,896]{1,0:T(8,128)(2,1)S(1)}, u32[]{:S(2)}, u32[]{:S(2)}) %collective-permute-start.34) | collective-permute-done | bytes 401440 | tf_op jit(solution)/shard_map/ppermute | solution.py:21
  164.5 1.2 add_up.2
  (128 shorter events, 16.6 us)
Async XLA Ops:
  2.5 19.0 %collective-permute-start.7 = (bf16[2,464,128]{2,1,0:T(8,128)(2,1)S(1)}, bf16[2,464,128]{2,1,0:T(8,128)(2,1)S(1)}, u32[]{:S(2)}, u32[]{:S(2)}) collective-permute-start(bf16[2,464,128]{2,1,0:T(8,128)(2,1)S(1)} %prepare.1.refs_0_), channel_id=1, source_target_pairs={{0,2},{2,4},{4,6},{6,0},{1,3},{3,5},{5,7},{7,1},{8,10},{10,12},{12... | collective-permute-start | bytes 712712 | tf_op jit(solution)/shard_map/ppermute | solution.py:21
  4.3 17.7 %collective-permute-start.8 = (bf16[2,464,128]{2,1,0:T(8,128)(2,1)S(1)}, bf16[2,464,128]{2,1,0:T(8,128)(2,1)S(1)}, u32[]{:S(2)}, u32[]{:S(2)}) collective-permute-start(bf16[2,464,128]{2,1,0:T(8,128)(2,1)S(1)} %prepare.1.refs_0_), channel_id=1, source_target_pairs={{0,4},{2,6},{4,0},{6,2},{1,5},{3,7},{5,1},{7,3},{8,12},{10,14},{12... | collective-permute-start | bytes 712712 | tf_op jit(solution)/shard_map/ppermute | solution.py:21
  7.2 14.3 %collective-permute-start = (bf16[2,448,128]{2,1,0:T(8,128)(2,1)}, bf16[2,448,128]{2,1,0:T(8,128)(2,1)S(1)}, u32[]{:S(2)}, u32[]{:S(2)}) collective-permute-start(bf16[2,448,128]{2,1,0:T(8,128)(2,1)} %bitcast.9), channel_id=1, source_target_pairs={{0,2},{2,4},{4,6},{6,0},{1,3},{3,5},{5,7},{7,1},{8,10},{10,12},{12... | collective-permute-start | bytes 688136 | tf_op jit(solution)/shard_map/ppermute | solution.py:21
  7.2 20.5 %collective-permute-start.1 = (bf16[2,448,128]{2,1,0:T(8,128)(2,1)}, bf16[2,448,128]{2,1,0:T(8,128)(2,1)S(1)}, u32[]{:S(2)}, u32[]{:S(2)}) collective-permute-start(bf16[2,448,128]{2,1,0:T(8,128)(2,1)} %bitcast.10), channel_id=1, source_target_pairs={{0,4},{2,6},{4,0},{6,2},{1,5},{3,7},{5,1},{7,3},{8,12},{10,14},{12... | collective-permute-start | bytes 688136 | tf_op jit(solution)/shard_map/ppermute | solution.py:21
  10.0 17.7 %collective-permute-start.9 = (bf16[2,464,128]{2,1,0:T(8,128)(2,1)S(1)}, bf16[2,464,128]{2,1,0:T(8,128)(2,1)S(1)}, u32[]{:S(2)}, u32[]{:S(2)}) collective-permute-start(bf16[2,464,128]{2,1,0:T(8,128)(2,1)S(1)} %prepare.1.refs_0_), channel_id=1, source_target_pairs={{0,6},{2,0},{4,2},{6,4},{1,7},{3,1},{5,3},{7,5},{8,14},{10,8},{12,... | collective-permute-start | bytes 712712 | tf_op jit(solution)/shard_map/ppermute | solution.py:21
  21.5 12.8 %collective-permute-start.10 = (bf16[2,464,128]{2,1,0:T(8,128)(2,1)S(1)}, bf16[2,464,128]{2,1,0:T(8,128)(2,1)S(1)}, u32[]{:S(2)}, u32[]{:S(2)}) collective-permute-start(bf16[2,464,128]{2,1,0:T(8,128)(2,1)S(1)} %prepare.1.refs_0_), channel_id=1, source_target_pairs={{0,1},{1,0},{2,3},{3,2},{4,5},{5,4},{6,7},{7,6},{8,9},{9,8},{10,11... | collective-permute-start | bytes 712712 | tf_op jit(solution)/shard_map/ppermute | solution.py:21
  21.5 13.3 %collective-permute-start.11 = (bf16[2,464,128]{2,1,0:T(8,128)(2,1)S(1)}, bf16[2,464,128]{2,1,0:T(8,128)(2,1)S(1)}, u32[]{:S(2)}, u32[]{:S(2)}) collective-permute-start(bf16[2,464,128]{2,1,0:T(8,128)(2,1)S(1)} %collective-permute-done.7.refs_1_), channel_id=1, source_target_pairs={{0,1},{1,0},{2,3},{3,2},{4,5},{5,4},{6,7},{7,6},{8,9},{9,8},{10,11... | collective-permute-start | bytes 712712 | tf_op jit(solution)/shard_map/ppermute | solution.py:21
  22.0 12.9 %collective-permute-start.12 = (bf16[2,464,128]{2,1,0:T(8,128)(2,1)S(1)}, bf16[2,464,128]{2,1,0:T(8,128)(2,1)S(1)}, u32[]{:S(2)}, u32[]{:S(2)}) collective-permute-start(bf16[2,464,128]{2,1,0:T(8,128)(2,1)S(1)} %collective-permute-done.8.refs_2_), channel_id=1, source_target_pairs={{0,1},{1,0},{2,3},{3,2},{4,5},{5,4},{6,7},{7,6},{8,9},{9,8},{10,11... | collective-permute-start | bytes 712712 | tf_op jit(solution)/shard_map/ppermute | solution.py:21
  27.6 6.7 %collective-permute-start.2 = (bf16[2,448,128]{2,1,0:T(8,128)(2,1)}, bf16[2,448,128]{2,1,0:T(8,128)(2,1)S(1)}, u32[]{:S(2)}, u32[]{:S(2)}) collective-permute-start(bf16[2,448,128]{2,1,0:T(8,128)(2,1)} %bitcast.11), channel_id=1, source_target_pairs={{0,6},{2,0},{4,2},{6,4},{1,7},{3,1},{5,3},{7,5},{8,14},{10,8},{12,... | collective-permute-start | bytes 688136 | tf_op jit(solution)/shard_map/ppermute | solution.py:21
  27.7 8.5 %collective-permute-start.13 = (bf16[2,464,128]{2,1,0:T(8,128)(2,1)S(1)}, bf16[2,464,128]{2,1,0:T(8,128)(2,1)S(1)}, u32[]{:S(2)}, u32[]{:S(2)}) collective-permute-start(bf16[2,464,128]{2,1,0:T(8,128)(2,1)S(1)} %collective-permute-done.9.refs_3_), channel_id=1, source_target_pairs={{0,1},{1,0},{2,3},{3,2},{4,5},{5,4},{6,7},{7,6},{8,9},{9,8},{10,11... | collective-permute-start | bytes 712712 | tf_op jit(solution)/shard_map/ppermute | solution.py:21
  34.3 7.9 %collective-permute-start.3 = (bf16[2,448,128]{2,1,0:T(8,128)(2,1)}, bf16[2,448,128]{2,1,0:T(8,128)(2,1)S(1)}, u32[]{:S(2)}, u32[]{:S(2)}) collective-permute-start(bf16[2,448,128]{2,1,0:T(8,128)(2,1)} %bitcast.12), channel_id=1, source_target_pairs={{0,1},{1,0},{2,3},{3,2},{4,5},{5,4},{6,7},{7,6},{8,9},{9,8},{10,11... | collective-permute-start | bytes 688136 | tf_op jit(solution)/shard_map/ppermute | solution.py:21
  34.4 7.9 %collective-permute-start.4 = (bf16[2,448,128]{2,1,0:T(8,128)(2,1)S(1)}, bf16[2,448,128]{2,1,0:T(8,128)(2,1)S(1)}, u32[]{:S(2)}, u32[]{:S(2)}) collective-permute-start(bf16[2,448,128]{2,1,0:T(8,128)(2,1)S(1)} %collective-permute-done.refs_1_), channel_id=1, source_target_pairs={{0,1},{1,0},{2,3},{3,2},{4,5},{5,4},{6,7},{7,6},{8,9},{9,8},{10,11... | collective-permute-start | bytes 688136 | tf_op jit(solution)/shard_map/ppermute | solution.py:21
  34.9 7.4 %collective-permute-start.5 = (bf16[2,448,128]{2,1,0:T(8,128)(2,1)S(1)}, bf16[2,448,128]{2,1,0:T(8,128)(2,1)}, u32[]{:S(2)}, u32[]{:S(2)}) collective-permute-start(bf16[2,448,128]{2,1,0:T(8,128)(2,1)S(1)} %collective-permute-done.1.refs_2_), channel_id=1, source_target_pairs={{0,1},{1,0},{2,3},{3,2},{4,5},{5,4},{6,7},{7,6},{8,9},{9,8},{10,11... | collective-permute-start | bytes 688136 | tf_op jit(solution)/shard_map/ppermute | solution.py:21
  35.0 7.3 %collective-permute-start.6 = (bf16[2,448,128]{2,1,0:T(8,128)(2,1)S(1)}, bf16[2,448,128]{2,1,0:T(8,128)(2,1)}, u32[]{:S(2)}, u32[]{:S(2)}) collective-permute-start(bf16[2,448,128]{2,1,0:T(8,128)(2,1)S(1)} %collective-permute-done.2.refs_3_), channel_id=1, source_target_pairs={{0,1},{1,0},{2,3},{3,2},{4,5},{5,4},{6,7},{7,6},{8,9},{9,8},{10,11... | collective-permute-start | bytes 688136 | tf_op jit(solution)/shard_map/ppermute | solution.py:21
  58.3 37.7 %collective-permute-start.14 = (bf16[4,464,256]{2,1,0:T(8,128)(2,1)}, bf16[4,464,256]{2,1,0:T(8,128)(2,1)S(1)}, u32[]{:S(2)}, u32[]{:S(2)}) collective-permute-start(bf16[4,464,256]{2,1,0:T(8,128)(2,1)} %get-tuple-element.39), channel_id=1, source_target_pairs={{0,1},{1,0},{2,3},{3,2},{4,5},{5,4},{6,7},{7,6},{8,9},{9,8},{10,11... | collective-permute-start | bytes 2850824 | tf_op jit(solution)/shard_map/ppermute | solution.py:21
  60.0 8.3 %collective-permute-start.18 = (f32[8,128]{1,0:T(8,128)S(1)}, f32[8,128]{1,0:T(8,128)S(1)}, u32[]{:S(2)}, u32[]{:S(2)}) collective-permute-start(f32[8,128]{1,0:T(8,128)S(1)} %broadcast_in_dim.10), channel_id=1, source_target_pairs={{0,64},{32,96},{64,0},{96,32},{1,65},{33,97},{65,1},{97,33},{2,66}... | collective-permute-start | bytes 12296 | tf_op jit(solution)/shard_map/ppermute | solution.py:21
  66.3 11.7 %collective-permute-start.36 = (bf16[4,224,128]{2,1,0:T(8,128)(2,1)}, bf16[4,224,128]{2,1,0:T(8,128)(2,1)S(1)}, u32[]{:S(2)}, u32[]{:S(2)}) collective-permute-start(bf16[4,224,128]{2,1,0:T(8,128)(2,1)} %copy-done.22), channel_id=1, source_target_pairs={{0,8},{8,16},{16,24},{24,0},{1,9},{9,17},{17,25},{25,1},{2,10},{10... | collective-permute-start | bytes 688136 | tf_op jit(solution)/shard_map/ppermute | solution.py:21
  68.3 8.8 %collective-permute-start.21 = (f32[8,128]{1,0:T(8,128)S(1)}, f32[8,128]{1,0:T(8,128)S(1)}, u32[]{:S(2)}, u32[]{:S(2)}) collective-permute-start(f32[8,128]{1,0:T(8,128)S(1)} %add_add_fusion), channel_id=1, source_target_pairs={{0,16},{8,24},{16,0},{24,8},{1,17},{9,25},{17,1},{25,9},{2,18},{10... | collective-permute-start | bytes 12296 | tf_op jit(solution)/shard_map/ppermute | solution.py:21
  77.1 7.7 %collective-permute-start.37 = (bf16[4,224,128]{2,1,0:T(8,128)(2,1)}, bf16[4,224,128]{2,1,0:T(8,128)(2,1)S(1)}, u32[]{:S(2)}, u32[]{:S(2)}) collective-permute-start(bf16[4,224,128]{2,1,0:T(8,128)(2,1)} %copy-done.21), channel_id=1, source_target_pairs={{0,16},{8,24},{16,0},{24,8},{1,17},{9,25},{17,1},{25,9},{2,18},{10... | collective-permute-start | bytes 688136 | tf_op jit(solution)/shard_map/ppermute | solution.py:21
  77.1 9.2 %collective-permute-start.38 = (bf16[4,224,128]{2,1,0:T(8,128)(2,1)}, bf16[4,224,128]{2,1,0:T(8,128)(2,1)S(1)}, u32[]{:S(2)}, u32[]{:S(2)}) collective-permute-start(bf16[4,224,128]{2,1,0:T(8,128)(2,1)} %copy-done.20), channel_id=1, source_target_pairs={{0,24},{8,0},{16,8},{24,16},{1,25},{9,1},{17,9},{25,17},{2,26},{10... | collective-permute-start | bytes 688136 | tf_op jit(solution)/shard_map/ppermute | solution.py:21
  78.1 9.6 %collective-permute-start.24 = (bf16[448,256]{1,0:T(8,128)(2,1)}, bf16[448,256]{1,0:T(8,128)(2,1)}, u32[]{:S(2)}, u32[]{:S(2)}) collective-permute-start(bf16[448,256]{1,0:T(8,128)(2,1)} %copy-done.19), channel_id=1, source_target_pairs={{0,32},{32,64},{64,96},{96,0},{1,33},{33,65},{65,97},{97,1},{2,34}... | collective-permute-start | bytes 688136 | tf_op jit(solution)/shard_map/ppermute | solution.py:21
  78.1 12.0 %collective-permute-start.25 = (bf16[448,256]{1,0:T(8,128)(2,1)}, bf16[448,256]{1,0:T(8,128)(2,1)}, u32[]{:S(2)}, u32[]{:S(2)}) collective-permute-start(bf16[448,256]{1,0:T(8,128)(2,1)} %copy-done.18), channel_id=1, source_target_pairs={{0,64},{32,96},{64,0},{96,32},{1,65},{33,97},{65,1},{97,33},{2,66}... | collective-permute-start | bytes 688136 | tf_op jit(solution)/shard_map/ppermute | solution.py:21
  84.8 6.6 %collective-permute-start.26 = (bf16[448,256]{1,0:T(8,128)(2,1)}, bf16[448,256]{1,0:T(8,128)(2,1)}, u32[]{:S(2)}, u32[]{:S(2)}) collective-permute-start(bf16[448,256]{1,0:T(8,128)(2,1)} %copy-done.17), channel_id=1, source_target_pairs={{0,96},{32,0},{64,32},{96,64},{1,97},{33,1},{65,33},{97,65},{2,98}... | collective-permute-start | bytes 688136 | tf_op jit(solution)/shard_map/ppermute | solution.py:21
  87.6 7.2 %collective-permute-start.40 = (bf16[4,224,128]{2,1,0:T(8,128)(2,1)S(1)}, bf16[4,224,128]{2,1,0:T(8,128)(2,1)S(1)}, u32[]{:S(2)}, u32[]{:S(2)}) collective-permute-start(bf16[4,224,128]{2,1,0:T(8,128)(2,1)S(1)} %collective-permute-done.37.m2), channel_id=1, source_target_pairs={{0,1},{1,0},{2,3},{3,2},{4,5},{5,4},{6,7},{7,6},{8,9},{9,8},{10,11... | collective-permute-start | bytes 688136 | tf_op jit(solution)/shard_map/ppermute | solution.py:21
  90.1 5.7 %collective-permute-start.41 = (bf16[4,224,128]{2,1,0:T(8,128)(2,1)S(1)}, bf16[4,224,128]{2,1,0:T(8,128)(2,1)S(1)}, u32[]{:S(2)}, u32[]{:S(2)}) collective-permute-start(bf16[4,224,128]{2,1,0:T(8,128)(2,1)S(1)} %collective-permute-done.38.m3), channel_id=1, source_target_pairs={{0,1},{1,0},{2,3},{3,2},{4,5},{5,4},{6,7},{7,6},{8,9},{9,8},{10,11... | collective-permute-start | bytes 688136 | tf_op jit(solution)/shard_map/ppermute | solution.py:21
  91.4 13.1 %collective-permute-start.42 = (bf16[896,256]{1,0:T(8,128)(2,1)}, bf16[896,256]{1,0:T(8,128)(2,1)S(1)}, u32[]{:S(2)}, u32[]{:S(2)}) collective-permute-start(bf16[896,256]{1,0:T(8,128)(2,1)} %copy-done.7), channel_id=1, source_target_pairs={{0,8},{8,16},{16,24},{24,0},{1,9},{9,17},{17,25},{25,1},{2,10},{10... | collective-permute-start | bytes 1376264 | tf_op jit(solution)/shard_map/ppermute | solution.py:21
  91.8 23.5 %collective-permute-start.43 = (bf16[896,256]{1,0:T(8,128)(2,1)}, bf16[896,256]{1,0:T(8,128)(2,1)S(1)}, u32[]{:S(2)}, u32[]{:S(2)}) collective-permute-start(bf16[896,256]{1,0:T(8,128)(2,1)} %copy-done.7), channel_id=1, source_target_pairs={{0,16},{8,24},{16,0},{24,8},{1,17},{9,25},{17,1},{25,9},{2,18},{10... | collective-permute-start | bytes 1376264 | tf_op jit(solution)/shard_map/ppermute | solution.py:21
  94.8 21.1 %collective-permute-start.44 = (bf16[896,256]{1,0:T(8,128)(2,1)}, bf16[896,256]{1,0:T(8,128)(2,1)S(1)}, u32[]{:S(2)}, u32[]{:S(2)}) collective-permute-start(bf16[896,256]{1,0:T(8,128)(2,1)} %copy-done.7), channel_id=1, source_target_pairs={{0,24},{8,0},{16,8},{24,16},{1,25},{9,1},{17,9},{25,17},{2,26},{10... | collective-permute-start | bytes 1376264 | tf_op jit(solution)/shard_map/ppermute | solution.py:21
  95.8 22.8 %collective-permute-start.30 = (bf16[896,256]{1,0:T(8,128)(2,1)}, bf16[896,256]{1,0:T(8,128)(2,1)S(1)}, u32[]{:S(2)}, u32[]{:S(2)}) collective-permute-start(bf16[896,256]{1,0:T(8,128)(2,1)} %copy-done.3), channel_id=1, source_target_pairs={{0,32},{32,64},{64,96},{96,0},{1,33},{33,65},{65,97},{97,1},{2,34}... | collective-permute-start | bytes 1376264 | tf_op jit(solution)/shard_map/ppermute | solution.py:21
  96.1 29.0 %collective-permute-start.31 = (bf16[896,256]{1,0:T(8,128)(2,1)}, bf16[896,256]{1,0:T(8,128)(2,1)S(1)}, u32[]{:S(2)}, u32[]{:S(2)}) collective-permute-start(bf16[896,256]{1,0:T(8,128)(2,1)} %copy-done.3), channel_id=1, source_target_pairs={{0,64},{32,96},{64,0},{96,32},{1,65},{33,97},{65,1},{97,33},{2,66}... | collective-permute-start | bytes 1376264 | tf_op jit(solution)/shard_map/ppermute | solution.py:21
  104.4 22.7 %collective-permute-start.15 = (bf16[464,256]{1,0:T(8,128)(2,1)S(1)}, bf16[464,256]{1,0:T(8,128)(2,1)S(1)}, u32[]{:S(2)}, u32[]{:S(2)}) collective-permute-start(bf16[464,256]{1,0:T(8,128)(2,1)S(1)} %get-tuple-element.42), channel_id=1, source_target_pairs={{0,2},{2,4},{4,6},{6,0},{1,3},{3,5},{5,7},{7,1},{8,10},{10,12},{12... | collective-permute-start | bytes 712712 | tf_op jit(solution)/shard_map/ppermute | solution.py:21
  115.3 11.9 %collective-permute-start.16 = (bf16[464,256]{1,0:T(8,128)(2,1)S(1)}, bf16[464,256]{1,0:T(8,128)(2,1)S(1)}, u32[]{:S(2)}, u32[]{:S(2)}) collective-permute-start(bf16[464,256]{1,0:T(8,128)(2,1)S(1)} %get-tuple-element.43), channel_id=1, source_target_pairs={{0,4},{2,6},{4,0},{6,2},{1,5},{3,7},{5,1},{7,3},{8,12},{10,14},{12... | collective-permute-start | bytes 712712 | tf_op jit(solution)/shard_map/ppermute | solution.py:21
  115.9 11.7 %collective-permute-start.17 = (bf16[464,256]{1,0:T(8,128)(2,1)S(1)}, bf16[464,256]{1,0:T(8,128)(2,1)S(1)}, u32[]{:S(2)}, u32[]{:S(2)}) collective-permute-start(bf16[464,256]{1,0:T(8,128)(2,1)S(1)} %get-tuple-element.44), channel_id=1, source_target_pairs={{0,6},{2,0},{4,2},{6,4},{1,7},{3,1},{5,3},{7,5},{8,14},{10,8},{12,... | collective-permute-start | bytes 712712 | tf_op jit(solution)/shard_map/ppermute | solution.py:21
  119.4 10.3 %collective-permute-start.32 = (bf16[896,256]{1,0:T(8,128)(2,1)}, bf16[896,256]{1,0:T(8,128)(2,1)}, u32[]{:S(2)}, u32[]{:S(2)}) collective-permute-start(bf16[896,256]{1,0:T(8,128)(2,1)} %copy-done.3), channel_id=1, source_target_pairs={{0,96},{32,0},{64,32},{96,64},{1,97},{33,1},{65,33},{97,65},{2,98}... | collective-permute-start | bytes 1376264 | tf_op jit(solution)/shard_map/ppermute | solution.py:21
  125.0 19.2 %collective-permute-start.45 = (bf16[224,896]{1,0:T(8,128)(2,1)}, bf16[224,896]{1,0:T(8,128)(2,1)S(1)}, u32[]{:S(2)}, u32[]{:S(2)}) collective-permute-start(bf16[224,896]{1,0:T(8,128)(2,1)} %get-tuple-element.60), channel_id=1, source_target_pairs={{0,32},{32,64},{64,96},{96,0},{1,33},{33,65},{65,97},{97,1},{2,34}... | collective-permute-start | bytes 1204232 | tf_op jit(solution)/shard_map/ppermute | solution.py:21
  127.1 6.1 %collective-permute-start.28 = (bf16[448,256]{1,0:T(8,128)(2,1)}, bf16[448,256]{1,0:T(8,128)(2,1)}, u32[]{:S(2)}, u32[]{:S(2)}) collective-permute-start(bf16[448,256]{1,0:T(8,128)(2,1)} %collective-permute-done.25.m2), channel_id=1, source_target_pairs={{0,1},{1,0},{2,3},{3,2},{4,5},{5,4},{6,7},{7,6},{8,9},{9,8},{10,11... | collective-permute-start | bytes 688136 | tf_op jit(solution)/shard_map/ppermute | solution.py:21
  127.7 5.6 %collective-permute-start.29 = (bf16[448,256]{1,0:T(8,128)(2,1)}, bf16[448,256]{1,0:T(8,128)(2,1)}, u32[]{:S(2)}, u32[]{:S(2)}) collective-permute-start(bf16[448,256]{1,0:T(8,128)(2,1)} %collective-permute-done.26.m3), channel_id=1, source_target_pairs={{0,1},{1,0},{2,3},{3,2},{4,5},{5,4},{6,7},{7,6},{8,9},{9,8},{10,11... | collective-permute-start | bytes 688136 | tf_op jit(solution)/shard_map/ppermute | solution.py:21
  129.7 19.6 %collective-permute-start.46 = (bf16[224,896]{1,0:T(8,128)(2,1)}, bf16[224,896]{1,0:T(8,128)(2,1)S(1)}, u32[]{:S(2)}, u32[]{:S(2)}) collective-permute-start(bf16[224,896]{1,0:T(8,128)(2,1)} %copy-done.16), channel_id=1, source_target_pairs={{0,64},{32,96},{64,0},{96,32},{1,65},{33,97},{65,1},{97,33},{2,66}... | collective-permute-start | bytes 1204232 | tf_op jit(solution)/shard_map/ppermute | solution.py:21
  130.1 14.2 %collective-permute-start.48 = (f32[448]{0:T(512)S(1)}, f32[448]{0:T(512)S(1)}, u32[]{:S(2)}, u32[]{:S(2)}) collective-permute-start(f32[448]{0:T(512)S(1)} %reduce.1), channel_id=1, source_target_pairs={{0,64},{32,96},{64,0},{96,32},{1,65},{33,97},{65,1},{97,33},{2,66}... | collective-permute-start | bytes 5384 | tf_op jit(solution)/shard_map/ppermute | solution.py:21
  133.3 13.0 %collective-permute-start.49 = (f32[448]{0:T(512)S(1)}, f32[448]{0:T(512)S(1)}, u32[]{:S(2)}, u32[]{:S(2)}) collective-permute-start(f32[448]{0:T(512)S(1)} %reduce.1), channel_id=1, source_target_pairs={{0,32},{32,64},{64,96},{96,0},{1,33},{33,65},{65,97},{97,1},{2,34}... | collective-permute-start | bytes 5384 | tf_op jit(solution)/shard_map/ppermute | solution.py:21
  138.4 10.9 %collective-permute-start.50 = (f32[448]{0:T(512)S(1)}, f32[448]{0:T(512)S(1)}, u32[]{:S(2)}, u32[]{:S(2)}) collective-permute-start(f32[448]{0:T(512)S(1)} %reduce.1), channel_id=1, source_target_pairs={{0,96},{32,0},{64,32},{96,64},{1,97},{33,1},{65,33},{97,65},{2,98}... | collective-permute-start | bytes 5384 | tf_op jit(solution)/shard_map/ppermute | solution.py:21
  144.2 8.1 %collective-permute-start.47 = (bf16[224,896]{1,0:T(8,128)(2,1)}, bf16[224,896]{1,0:T(8,128)(2,1)S(1)}, u32[]{:S(2)}, u32[]{:S(2)}) collective-permute-start(bf16[224,896]{1,0:T(8,128)(2,1)} %copy-done.15), channel_id=1, source_target_pairs={{0,96},{32,0},{64,32},{96,64},{1,97},{33,1},{65,33},{97,65},{2,98}... | collective-permute-start | bytes 1204232 | tf_op jit(solution)/shard_map/ppermute | solution.py:21
  144.2 12.9 %collective-permute-start.33 = (bf16[224,896]{1,0:T(8,128)(2,1)S(1)}, bf16[224,896]{1,0:T(8,128)(2,1)S(1)}, u32[]{:S(2)}, u32[]{:S(2)}) collective-permute-start(bf16[224,896]{1,0:T(8,128)(2,1)S(1)} %get-tuple-element.51), channel_id=1, source_target_pairs={{0,8},{8,16},{16,24},{24,0},{1,9},{9,17},{17,25},{25,1},{2,10},{10... | collective-permute-start | bytes 1204232 | tf_op jit(solution)/shard_map/ppermute | solution.py:21
  146.2 18.3 %collective-permute-start.34 = (bf16[224,896]{1,0:T(8,128)(2,1)S(1)}, bf16[224,896]{1,0:T(8,128)(2,1)S(1)}, u32[]{:S(2)}, u32[]{:S(2)}) collective-permute-start(bf16[224,896]{1,0:T(8,128)(2,1)S(1)} %get-tuple-element.52), channel_id=1, source_target_pairs={{0,16},{8,24},{16,0},{24,8},{1,17},{9,25},{17,1},{25,9},{2,18},{10... | collective-permute-start | bytes 1204232 | tf_op jit(solution)/shard_map/ppermute | solution.py:21
  149.3 15.2 %collective-permute-start.35 = (bf16[224,896]{1,0:T(8,128)(2,1)S(1)}, bf16[224,896]{1,0:T(8,128)(2,1)S(1)}, u32[]{:S(2)}, u32[]{:S(2)}) collective-permute-start(bf16[224,896]{1,0:T(8,128)(2,1)S(1)} %get-tuple-element.53), channel_id=1, source_target_pairs={{0,24},{8,0},{16,8},{24,16},{1,25},{9,1},{17,9},{25,17},{2,26},{10... | collective-permute-start | bytes 1204232 | tf_op jit(solution)/shard_map/ppermute | solution.py:21
  149.3 16.5 %collective-permute-start.51 = (f32[448]{0:T(512)S(1)}, f32[448]{0:T(512)S(1)}, u32[]{:S(2)}, u32[]{:S(2)}) collective-permute-start(f32[448]{0:T(512)S(1)} %add_add_fusion.2), channel_id=1, source_target_pairs={{0,16},{8,24},{16,0},{24,8},{1,17},{9,25},{17,1},{25,9},{2,18},{10... | collective-permute-start | bytes 5384 | tf_op jit(solution)/shard_map/ppermute | solution.py:21
  152.3 13.5 %collective-permute-start.52 = (f32[448]{0:T(512)S(1)}, f32[448]{0:T(512)S(1)}, u32[]{:S(2)}, u32[]{:S(2)}) collective-permute-start(f32[448]{0:T(512)S(1)} %add_add_fusion.2), channel_id=1, source_target_pairs={{0,8},{8,16},{16,24},{24,0},{1,9},{9,17},{17,25},{25,1},{2,10},{10... | collective-permute-start | bytes 5384 | tf_op jit(solution)/shard_map/ppermute | solution.py:21
  157.1 8.7 %collective-permute-start.53 = (f32[448]{0:T(512)S(1)}, f32[448]{0:T(512)S(1)}, u32[]{:S(2)}, u32[]{:S(2)}) collective-permute-start(f32[448]{0:T(512)S(1)} %add_add_fusion.2), channel_id=1, source_target_pairs={{0,24},{8,0},{16,8},{24,16},{1,25},{9,1},{17,9},{25,17},{2,26},{10... | collective-permute-start | bytes 5384 | tf_op jit(solution)/shard_map/ppermute | solution.py:21
  (30 other events, 325.3 us)

commit v2 on v1

--- a/solution.py
+++ b/solution.py
@@ -7,6 +7,7 @@
 from jax.sharding import PartitionSpec as P
 
 INTERPRET = False
+MIB = 1024 * 1024
 EPS = 1e-06
 EXTRA = 16
 GELU_A = 0.7978845608028654
@@ -36,7 +37,7 @@
     return pl.BlockSpec(memory_space=space)
 
 
-def call(body, outs, ins, scratch=(), flops=0, moved_bytes=0, name="local"):
+def call(body, outs, ins, scratch=(), flops=0, moved_bytes=0, limit=8):
     return pl.pallas_call(
         body,
         out_shape=[jax.ShapeDtypeStruct(s, d) for s, d in outs],
@@ -44,13 +45,12 @@
         out_specs=[spec() for _ in outs],
         scratch_shapes=list(scratch),
         cost_estimate=pl.CostEstimate(flops=flops, bytes_accessed=moved_bytes, transcendentals=0),
-        compiler_params=pltpu.CompilerParams(vmem_limit_bytes=48 * 1024 * 1024),
+        compiler_params=pltpu.CompilerParams(vmem_limit_bytes=limit * MIB),
         interpret=INTERPRET,
-        name=name,
     )(*[a for a, _ in ins])
 
 
-V, S, H = pltpu.VMEM, pltpu.SMEM, pl.ANY
+V, S, H = pltpu.VMEM, pltpu.SMEM, pltpu.HBM
 
 
 def split3(value):
@@ -92,7 +92,7 @@
             out_ref[m, :width, :] = (h * g_ref[...]).astype(BF16)
             out_ref[m, width:, :] = extra_rows(jnp.sum(h * h, axis=0, keepdims=True))
 
-    return call(body, [((micro, width + EXTRA, tok), BF16)], [(hidden_t, V), (gain_mat, V)], name="prepare")[0]
+    return call(body, [((micro, width + EXTRA, tok), BF16)], [(hidden_t, V), (gain_mat, V)])[0]
 
 
 def forward_part(sc, up, own, other):
@@ -156,7 +156,7 @@
         ],
         flops=2 * d * ff * cols,
         moved_bytes=d * ff * 2,
-        name="forward_part",
+        limit=20,
     )
 
 
@@ -220,7 +220,7 @@
         ],
         flops=2 * d * ff * cols,
         moved_bytes=d * ff * 2,
-        name="backward_part",
+        limit=20,
     )
 
 
@@ -255,7 +255,7 @@
         [pltpu.VMEM((4, pair, ff), BF16), pltpu.SemaphoreType.DMA((4,))],
         flops=2 * d * ff * cols,
         moved_bytes=d * ff * 2,
-        name="normed_part",
+        limit=20,
     )
 
 
@@ -275,7 +275,6 @@
         body,
         [((width, cols), F32), ((8, cols), F32)] + [((width + EXTRA, cols), BF16)] * 3,
         [(pown, V), (psib, V), (rd, V)],
-        name="pair_sum",
     )
 
 
@@ -306,7 +305,6 @@
         body,
         [((micro, width, tok), BF16), ((width, 1), F32)],
         [(sc, S)] + [(a, V) for a in (q0, rd0, *recv, hidden_t, out_t, gain_mat, inv, inv_count)],
-        name="input_grad",
     )
 
 
@@ -341,7 +339,7 @@
             pltpu.VMEM((pair, ff), F32),
         ],
         flops=2 * pair * ff * cols * 4,
-        name="up_part",
+        limit=20,
     )
 
 
@@ -377,7 +375,7 @@
             pltpu.VMEM((pair, ff), F32),
         ],
         flops=2 * pair * ff * cols * 4,
-        name="down_part",
+        limit=20,
     )
 
 
@@ -392,7 +390,7 @@
         total = own[...] + r1[...].astype(F32) + (r2[...].astype(F32) + r3[...].astype(F32))
         out_ref[...] = total * ic_ref[0:1, 0:1]
 
-    return call(body, [(first.shape, F32)], [(a, V) for a in (first, *rest, inv_count)], name="add_up")[0]
+    return call(body, [(first.shape, F32)], [(a, V) for a in (first, *rest, inv_count)])[0]
 
 
 def on_device(hidden_in, out_grad, pack_fill, norm_gain, up_weight, down_weight):
@@ -448,6 +446,7 @@
         P(mp, None),
     )
     out_specs = (P(None, dp, mp), P(dp, mp), P(mp, dp), P(mp))
+
     return jax.shard_map(
         on_device, mesh=split, in_specs=in_specs, out_specs=out_specs, check_vma=False
     )

time: 167 us -> 173 us (1.036)
  local copies, waits for them, and re-layouts: 10 us -> 18.5 us
  Pallas kernels: 30.4 us -> 28 us
    unnamed x48 -> x56, local copies, waits for them, and re-layouts: 8.42 us -> 16.9 us
    pallas_call x10, Pallas kernels: 30.4 us -> 28 us  [call(): pl.pallas_call(body, out_shape=[jax.ShapeDtypeStruct(s, d) for s, d in ou...]
where the time goes in v2:
time: 173 us; the launch traced here: 172 us
  starting transfers between devices  63.4 us (37%)
  waiting for transfers between devices  59.6 us (34%)
  Pallas kernels  28 us (16%)
  local copies, waits for them, and re-layouts  18.5 us (11%)
    ppermute x54, starting transfers between devices, moved(): lax.ppermute(value, axis, [(i, (i + step) % size) for i in range(size)])  63.4 us
    ppermute x54, waiting for transfers between devices, moved(): lax.ppermute(value, axis, [(i, (i + step) % size) for i in range(size)])  59.6 us
    pallas_call x10, Pallas kernels, call(): pl.pallas_call(body, out_shape=[jax.ShapeDtypeStruct(s, d) for s, d in ou...  28 us
    unnamed x56, local copies, waits for them, and re-layouts  16.9 us
  transfers between devices with their start and end apart: 54, of which 17 were waited for; matrix products, arithmetic and copies ran while one was open for 1% of the time, Pallas kernels for 10%

profile of v2, /device:TPU:0, one launch (start us, length us, event | category | flops | bytes accessed | tf_op | source)
XLA Modules:
  0.0 172.4 jit_solution(13858947832039791578)
XLA Ops:
  2.5 1.8 %collective-permute-start.7 = (bf16[2,464,128]{2,1,0:T(8,128)(2,1)S(1)}, bf16[2,464,128]{2,1,0:T(8,128)(2,1)S(1)}, u32[]{:S(2)}, u32[]{:S(2)}) collective-permute-start(bf16[2,464,128]{2,1,0:T(8,128)(2,1)S(1)} %shard_map.93.refs_0_), channel_id=1, source_target_pairs={{0,2},{2,4},{4,6},{6,0},{1,3},{3,5},{5,7},{7,1},{8,10},{10,12},{12... | collective-permute-start | bytes 712712 | tf_op jit(solution)/shard_map/ppermute | solution.py:22
  4.3 2.9 %collective-permute-start.8 = (bf16[2,464,128]{2,1,0:T(8,128)(2,1)S(1)}, bf16[2,464,128]{2,1,0:T(8,128)(2,1)S(1)}, u32[]{:S(2)}, u32[]{:S(2)}) collective-permute-start(bf16[2,464,128]{2,1,0:T(8,128)(2,1)S(1)} %shard_map.93.refs_0_), channel_id=1, source_target_pairs={{0,4},{2,6},{4,0},{6,2},{1,5},{3,7},{5,1},{7,3},{8,12},{10,14},{12... | collective-permute-start | bytes 712712 | tf_op jit(solution)/shard_map/ppermute | solution.py:22
  7.2 2.8 %collective-permute-start.1 = (bf16[2,448,128]{2,1,0:T(8,128)(2,1)}, bf16[2,448,128]{2,1,0:T(8,128)(2,1)S(1)}, u32[]{:S(2)}, u32[]{:S(2)}) collective-permute-start(bf16[2,448,128]{2,1,0:T(8,128)(2,1)} %bitcast.12), channel_id=1, source_target_pairs={{0,4},{2,6},{4,0},{6,2},{1,5},{3,7},{5,1},{7,3},{8,12},{10,14},{12... | collective-permute-start | bytes 688136 | tf_op jit(solution)/shard_map/ppermute | solution.py:22
  10.4 11.1 %collective-permute-done.refs_1_ = bf16[2,448,128]{2,1,0:T(8,128)(2,1)S(1)} collective-permute-done((bf16[2,448,128]{2,1,0:T(8,128)(2,1)}, bf16[2,448,128]{2,1,0:T(8,128)(2,1)S(1)}, u32[]{:S(2)}, u32[]{:S(2)}) %collective-permute-start) | collective-permute-done | bytes 229408 | tf_op jit(solution)/shard_map/ppermute | solution.py:22
  22.1 5.5 %collective-permute-done.1.refs_2_ = bf16[2,448,128]{2,1,0:T(8,128)(2,1)S(1)} collective-permute-done((bf16[2,448,128]{2,1,0:T(8,128)(2,1)}, bf16[2,448,128]{2,1,0:T(8,128)(2,1)S(1)}, u32[]{:S(2)}, u32[]{:S(2)}) %collective-permute-start.1) | collective-permute-done | bytes 229408 | tf_op jit(solution)/shard_map/ppermute | solution.py:22
  27.7 6.7 %collective-permute-done.2.refs_3_ = bf16[2,448,128]{2,1,0:T(8,128)(2,1)S(1)} collective-permute-done((bf16[2,448,128]{2,1,0:T(8,128)(2,1)}, bf16[2,448,128]{2,1,0:T(8,128)(2,1)S(1)}, u32[]{:S(2)}, u32[]{:S(2)}) %collective-permute-start.2) | collective-permute-done | bytes 229408 | tf_op jit(solution)/shard_map/ppermute | solution.py:22
  36.1 2.8 %copy-done = bf16[3584,896]{1,0:T(8,128)(2,1)S(1)} copy-done((bf16[3584,896]{1,0:T(8,128)(2,1)S(1)}, bf16[3584,896]{1,0:T(8,128)(2,1)}, u32[]{:S(2)}) %copy-start) | copy-done | bytes 6422552
  38.9 4.7 %shard_map.94 = (bf16[896,256]{1,0:T(8,128)(2,1)S(1)}, f32[896,256]{1,0:T(8,128)S(1)}, f32[8,256]{1,0:T(8,128)S(1)}, bf16[896,256]{1,0:T(8,128)(2,1)S(1)}, bf16[...) custom-call(s32[8]{0:T(128)S(1)} %concatenate.3.sc, ...), custom_call_target="tpu_custom_call" | custom-call | flops 1644167168 | bytes 6422528 | tf_op jit(solution)/shard_map/pallas_call | solution.py:41
  47.3 2.8 %copy-done.1 = bf16[896,3584]{1,0:T(8,128)(2,1)S(1)} copy-done((bf16[896,3584]{1,0:T(8,128)(2,1)S(1)}, bf16[896,3584]{1,0:T(8,128)(2,1)}, u32[]{:S(2)}) %copy-start.1) | copy-done | bytes 6422552
  50.2 6.6 %shard_map.95 = (bf16[896,256]{1,0:T(8,128)(2,1)S(1)}, f32[8,256]{1,0:T(8,128)S(1)}, bf16[4,224,256]{2,1,0:T(8,128)(2,1)S(1)}, bf16[4,224,128]{2,1,0:T(8,128)(2,...) custom-call(s32[8]{0:T(128)S(1)} %concatenate.3.sc, bf16[896,3584]{1,0:T(8,128)(2,1)S(1)} %copy-done.1, ...), custom_call_target="tpu_custom_call" | custom-call | flops 1644167168 | bytes 6422528 | tf_op jit(solution)/shard_map/pallas_call | solution.py:41
  59.6 4.8 %shard_map.96 = (f32[4,448,256]{2,1,0:T(8,128)S(1)}, bf16[4,464,256]{2,1,0:T(8,128)(2,1)}) custom-call(s32[8]{0:T(128)S(1)} %concatenate.3.sc, bf16[3584,896]{1,0:T(8,128)(2,1)S(1)} %bitcast.10, bf16[896,256]{1,0:T(8,128)(2,1)S(1)} %get-tuple-element.36.gp_ref.g0, f32[8,256]{1,0:T(8,128)S(1)} %get-tuple-element.37.rd_ref), custom_call_target="tpu_custom_call" | custom-call | flops 1644167168 | bytes 6422528 | tf_op jit(solution)/shard_map/pallas_call | solution.py:41
  66.0 3.1 %collective-permute-start.18 = (f32[8,128]{1,0:T(8,128)S(1)}, f32[8,128]{1,0:T(8,128)S(1)}, u32[]{:S(2)}, u32[]{:S(2)}) collective-permute-start(f32[8,128]{1,0:T(8,128)S(1)} %broadcast_in_dim.10), channel_id=1, source_target_pairs={{0,64},{32,96},{64,0},{96,32},{1,65},{33,97},{65,1},{97,33},{2,66}... | collective-permute-start | bytes 12296 | tf_op jit(solution)/shard_map/ppermute | solution.py:22
  69.8 2.6 %collective-permute-start.20 = (f32[8,128]{1,0:T(8,128)S(1)}, f32[8,128]{1,0:T(8,128)S(1)}, u32[]{:S(2)}, u32[]{:S(2)}) collective-permute-start(f32[8,128]{1,0:T(8,128)S(1)} %broadcast_in_dim.10), channel_id=1, source_target_pairs={{0,96},{32,0},{64,32},{96,64},{1,97},{33,1},{65,33},{97,65},{2,98}... | collective-permute-start | bytes 12296 | tf_op jit(solution)/shard_map/ppermute | solution.py:22
  72.4 1.9 %collective-permute-start.36 = (bf16[4,224,128]{2,1,0:T(8,128)(2,1)}, bf16[4,224,128]{2,1,0:T(8,128)(2,1)S(1)}, u32[]{:S(2)}, u32[]{:S(2)}) collective-permute-start(bf16[4,224,128]{2,1,0:T(8,128)(2,1)} %copy-done.24), channel_id=1, source_target_pairs={{0,8},{8,16},{16,24},{24,0},{1,9},{9,17},{17,25},{25,1},{2,10},{10... | collective-permute-start | bytes 688136 | tf_op jit(solution)/shard_map/ppermute | solution.py:22
  74.3 3.7 %collective-permute-start.21 = (f32[8,128]{1,0:T(8,128)S(1)}, f32[8,128]{1,0:T(8,128)S(1)}, u32[]{:S(2)}, u32[]{:S(2)}) collective-permute-start(f32[8,128]{1,0:T(8,128)S(1)} %add_add_fusion), channel_id=1, source_target_pairs={{0,16},{8,24},{16,0},{24,8},{1,17},{9,25},{17,1},{25,9},{2,18},{10... | collective-permute-start | bytes 12296 | tf_op jit(solution)/shard_map/ppermute | solution.py:22
  79.0 2.3 %collective-permute-start.23 = (f32[8,128]{1,0:T(8,128)S(1)}, f32[8,128]{1,0:T(8,128)S(1)}, u32[]{:S(2)}, u32[]{:S(2)}) collective-permute-start(f32[8,128]{1,0:T(8,128)S(1)} %add_add_fusion), channel_id=1, source_target_pairs={{0,24},{8,0},{16,8},{24,16},{1,25},{9,1},{17,9},{25,17},{2,26},{10... | collective-permute-start | bytes 12296 | tf_op jit(solution)/shard_map/ppermute | solution.py:22
  81.2 1.9 %collective-permute-done.21 = f32[8,128]{1,0:T(8,128)S(1)} collective-permute-done((f32[8,128]{1,0:T(8,128)S(1)}, f32[8,128]{1,0:T(8,128)S(1)}, u32[]{:S(2)}, u32[]{:S(2)}) %collective-permute-start.21) | collective-permute-done | bytes 4128 | tf_op jit(solution)/shard_map/ppermute | solution.py:22
  84.2 4.2 %collective-permute-start.25 = (bf16[448,256]{1,0:T(8,128)(2,1)}, bf16[448,256]{1,0:T(8,128)(2,1)}, u32[]{:S(2)}, u32[]{:S(2)}) collective-permute-start(bf16[448,256]{1,0:T(8,128)(2,1)} %copy-done.20), channel_id=1, source_target_pairs={{0,64},{32,96},{64,0},{96,32},{1,65},{33,97},{65,1},{97,33},{2,66}... | collective-permute-start | bytes 688136 | tf_op jit(solution)/shard_map/ppermute | solution.py:22
  88.4 2.5 %collective-permute-done.37.m2 = bf16[4,224,128]{2,1,0:T(8,128)(2,1)S(1)} collective-permute-done((bf16[4,224,128]{2,1,0:T(8,128)(2,1)}, bf16[4,224,128]{2,1,0:T(8,128)(2,1)S(1)}, u32[]{:S(2)}, u32[]{:S(2)}) %collective-permute-start.37) | collective-permute-done | bytes 229408 | tf_op jit(solution)/shard_map/ppermute | solution.py:22
  90.9 1.2 collective-permute-start.26
  92.4 1.3 collective-permute-done.24.m1
  93.7 2.5 %collective-permute-done.25.m2 = bf16[448,256]{1,0:T(8,128)(2,1)} collective-permute-done((bf16[448,256]{1,0:T(8,128)(2,1)}, bf16[448,256]{1,0:T(8,128)(2,1)}, u32[]{:S(2)}, u32[]{:S(2)}) %collective-permute-start.25) | collective-permute-done | bytes 229408 | tf_op jit(solution)/shard_map/ppermute | solution.py:22
  96.1 1.3 collective-permute-done.26.m3
  97.9 3.0 %collective-permute-start.43 = (bf16[896,256]{1,0:T(8,128)(2,1)}, bf16[896,256]{1,0:T(8,128)(2,1)S(1)}, u32[]{:S(2)}, u32[]{:S(2)}) collective-permute-start(bf16[896,256]{1,0:T(8,128)(2,1)} %copy-done.9), channel_id=1, source_target_pairs={{0,16},{8,24},{16,0},{24,8},{1,17},{9,25},{17,1},{25,9},{2,18},{10... | collective-permute-start | bytes 1376264 | tf_op jit(solution)/shard_map/ppermute | solution.py:22
  102.1 3.9 %collective-permute-start.31 = (bf16[896,256]{1,0:T(8,128)(2,1)}, bf16[896,256]{1,0:T(8,128)(2,1)S(1)}, u32[]{:S(2)}, u32[]{:S(2)}) collective-permute-start(bf16[896,256]{1,0:T(8,128)(2,1)} %copy-done.5), channel_id=1, source_target_pairs={{0,64},{32,96},{64,0},{96,32},{1,65},{33,97},{65,1},{97,33},{2,66}... | collective-permute-start | bytes 1376264 | tf_op jit(solution)/shard_map/ppermute | solution.py:22
  106.2 4.3 %collective-permute-done.42.a1 = bf16[896,256]{1,0:T(8,128)(2,1)S(1)} collective-permute-done((bf16[896,256]{1,0:T(8,128)(2,1)}, bf16[896,256]{1,0:T(8,128)(2,1)S(1)}, u32[]{:S(2)}, u32[]{:S(2)}) %collective-permute-start.42) | collective-permute-done | bytes 458784 | tf_op jit(solution)/shard_map/ppermute | solution.py:22
  110.5 10.8 %collective-permute-done.43.a2 = bf16[896,256]{1,0:T(8,128)(2,1)S(1)} collective-permute-done((bf16[896,256]{1,0:T(8,128)(2,1)}, bf16[896,256]{1,0:T(8,128)(2,1)S(1)}, u32[]{:S(2)}, u32[]{:S(2)}) %collective-permute-start.43) | collective-permute-done | bytes 458784 | tf_op jit(solution)/shard_map/ppermute | solution.py:22
  122.0 1.7 collective-permute-start.17
  123.7 1.0 collective-permute-done.30.g1
  125.5 1.0 copy-done.10
  126.5 1.0 copy-done.12
  127.5 3.6 %shard_map.101 = (f32[224,896]{1,0:T(8,128)S(1)}, bf16[224,896]{1,0:T(8,128)(2,1)}, bf16[224,896]{1,0:T(8,128)(2,1)S(1)}, bf16[224,896]{1,0:T(8,128)(2,1)S(1)}) custom-call(s32[8]{0:T(128)S(1)} %concatenate.3.sc, bf16[4,224,256]{2,1,0:T(8,128)(2,1)S(1)} %copy-done.12, bf16[4,224,128]{2,1,0:T(8,128)(2,1)S(1)} %collective-permute-done.36.m1, ...), custom_call_target="tpu_custom_call" | custom-call | flops 1644167168 | tf_op jit(solution)/shard_map/pallas_call | solution.py:41
  131.1 2.1 %collective-permute-start.45 = (bf16[224,896]{1,0:T(8,128)(2,1)}, bf16[224,896]{1,0:T(8,128)(2,1)S(1)}, u32[]{:S(2)}, u32[]{:S(2)}) collective-permute-start(bf16[224,896]{1,0:T(8,128)(2,1)} %get-tuple-element.60), channel_id=1, source_target_pairs={{0,32},{32,64},{64,96},{96,0},{1,33},{33,65},{65,97},{97,1},{2,34}... | collective-permute-start | bytes 1204232 | tf_op jit(solution)/shard_map/ppermute | solution.py:22
  133.8 1.5 shard_map.98
  136.1 3.2 %collective-permute-start.48 = (f32[448]{0:T(512)S(1)}, f32[448]{0:T(512)S(1)}, u32[]{:S(2)}, u32[]{:S(2)}) collective-permute-start(f32[448]{0:T(512)S(1)} %reduce.1), channel_id=1, source_target_pairs={{0,64},{32,96},{64,0},{96,32},{1,65},{33,97},{65,1},{97,33},{2,66}... | collective-permute-start | bytes 5384 | tf_op jit(solution)/shard_map/ppermute | solution.py:22
  140.4 4.1 %shard_map.99 = (f32[224,896]{1,0:T(8,128)S(1)}, bf16[224,896]{1,0:T(8,128)(2,1)S(1)}, bf16[224,896]{1,0:T(8,128)(2,1)S(1)}, bf16[224,896]{1,0:T(8,128)(2,1)S(1)}) custom-call(s32[8]{0:T(128)S(1)} %concatenate.3.sc, bf16[896,256]{1,0:T(8,128)(2,1)S(1)} %copy-done.8, bf16[448,256]{1,0:T(8,128)(2,1)} %collective-permute-done.24.m1, ...), custom_call_target="tpu_custom_call" | custom-call | flops 1644167168 | tf_op jit(solution)/shard_map/pallas_call | solution.py:41
  144.5 3.3 %collective-permute-start.50 = (f32[448]{0:T(512)S(1)}, f32[448]{0:T(512)S(1)}, u32[]{:S(2)}, u32[]{:S(2)}) collective-permute-start(f32[448]{0:T(512)S(1)} %reduce.1), channel_id=1, source_target_pairs={{0,96},{32,0},{64,32},{96,64},{1,97},{33,1},{65,33},{97,65},{2,98}... | collective-permute-start | bytes 5384 | tf_op jit(solution)/shard_map/ppermute | solution.py:22
  147.8 2.5 %collective-permute-done.45.r1 = bf16[224,896]{1,0:T(8,128)(2,1)S(1)} collective-permute-done((bf16[224,896]{1,0:T(8,128)(2,1)}, bf16[224,896]{1,0:T(8,128)(2,1)S(1)}, u32[]{:S(2)}, u32[]{:S(2)}) %collective-permute-start.45) | collective-permute-done | bytes 401440 | tf_op jit(solution)/shard_map/ppermute | solution.py:22
  150.3 2.0 %collective-permute-start.33 = (bf16[224,896]{1,0:T(8,128)(2,1)S(1)}, bf16[224,896]{1,0:T(8,128)(2,1)S(1)}, u32[]{:S(2)}, u32[]{:S(2)}) collective-permute-start(bf16[224,896]{1,0:T(8,128)(2,1)S(1)} %get-tuple-element.51), channel_id=1, source_target_pairs={{0,8},{8,16},{16,24},{24,0},{1,9},{9,17},{17,25},{25,1},{2,10},{10... | collective-permute-start | bytes 1204232 | tf_op jit(solution)/shard_map/ppermute | solution.py:22
  152.3 3.1 %collective-permute-start.34 = (bf16[224,896]{1,0:T(8,128)(2,1)S(1)}, bf16[224,896]{1,0:T(8,128)(2,1)S(1)}, u32[]{:S(2)}, u32[]{:S(2)}) collective-permute-start(bf16[224,896]{1,0:T(8,128)(2,1)S(1)} %get-tuple-element.52), channel_id=1, source_target_pairs={{0,16},{8,24},{16,0},{24,8},{1,17},{9,25},{17,1},{25,9},{2,18},{10... | collective-permute-start | bytes 1204232 | tf_op jit(solution)/shard_map/ppermute | solution.py:22
  155.4 1.6 collective-permute-start.51
  157.0 1.4 collective-permute-done.47.r3
  158.4 2.0 %collective-permute-start.52 = (f32[448]{0:T(512)S(1)}, f32[448]{0:T(512)S(1)}, u32[]{:S(2)}, u32[]{:S(2)}) collective-permute-start(f32[448]{0:T(512)S(1)} %add_add_fusion.2), channel_id=1, source_target_pairs={{0,8},{8,16},{16,24},{24,0},{1,9},{9,17},{17,25},{25,1},{2,10},{10... | collective-permute-start | bytes 5384 | tf_op jit(solution)/shard_map/ppermute | solution.py:22
  160.4 2.8 %collective-permute-done.33.r1 = bf16[224,896]{1,0:T(8,128)(2,1)S(1)} collective-permute-done((bf16[224,896]{1,0:T(8,128)(2,1)S(1)}, bf16[224,896]{1,0:T(8,128)(2,1)S(1)}, u32[]{:S(2)}, u32[]{:S(2)}) %collective-permute-start.33) | collective-permute-done | bytes 401440 | tf_op jit(solution)/shard_map/ppermute | solution.py:22
  163.2 2.9 %collective-permute-start.53 = (f32[448]{0:T(512)S(1)}, f32[448]{0:T(512)S(1)}, u32[]{:S(2)}, u32[]{:S(2)}) collective-permute-start(f32[448]{0:T(512)S(1)} %add_add_fusion.2), channel_id=1, source_target_pairs={{0,24},{8,0},{16,8},{24,16},{1,25},{9,1},{17,9},{25,17},{2,26},{10... | collective-permute-start | bytes 5384 | tf_op jit(solution)/shard_map/ppermute | solution.py:22
  166.1 1.2 shard_map.102
  167.3 3.3 %collective-permute-done.34.r2 = bf16[224,896]{1,0:T(8,128)(2,1)S(1)} collective-permute-done((bf16[224,896]{1,0:T(8,128)(2,1)S(1)}, bf16[224,896]{1,0:T(8,128)(2,1)S(1)}, u32[]{:S(2)}, u32[]{:S(2)}) %collective-permute-start.34) | collective-permute-done | bytes 401440 | tf_op jit(solution)/shard_map/ppermute | solution.py:22
  170.6 1.3 shard_map.100
  (137 shorter events, 21.4 us)
Async XLA Ops:
  2.5 19.0 %collective-permute-start.7 = (bf16[2,464,128]{2,1,0:T(8,128)(2,1)S(1)}, bf16[2,464,128]{2,1,0:T(8,128)(2,1)S(1)}, u32[]{:S(2)}, u32[]{:S(2)}) collective-permute-start(bf16[2,464,128]{2,1,0:T(8,128)(2,1)S(1)} %shard_map.93.refs_0_), channel_id=1, source_target_pairs={{0,2},{2,4},{4,6},{6,0},{1,3},{3,5},{5,7},{7,1},{8,10},{10,12},{12... | collective-permute-start | bytes 712712 | tf_op jit(solution)/shard_map/ppermute | solution.py:22
  4.3 17.7 %collective-permute-start.8 = (bf16[2,464,128]{2,1,0:T(8,128)(2,1)S(1)}, bf16[2,464,128]{2,1,0:T(8,128)(2,1)S(1)}, u32[]{:S(2)}, u32[]{:S(2)}) collective-permute-start(bf16[2,464,128]{2,1,0:T(8,128)(2,1)S(1)} %shard_map.93.refs_0_), channel_id=1, source_target_pairs={{0,4},{2,6},{4,0},{6,2},{1,5},{3,7},{5,1},{7,3},{8,12},{10,14},{12... | collective-permute-start | bytes 712712 | tf_op jit(solution)/shard_map/ppermute | solution.py:22
  7.2 14.3 %collective-permute-start = (bf16[2,448,128]{2,1,0:T(8,128)(2,1)}, bf16[2,448,128]{2,1,0:T(8,128)(2,1)S(1)}, u32[]{:S(2)}, u32[]{:S(2)}) collective-permute-start(bf16[2,448,128]{2,1,0:T(8,128)(2,1)} %bitcast.11), channel_id=1, source_target_pairs={{0,2},{2,4},{4,6},{6,0},{1,3},{3,5},{5,7},{7,1},{8,10},{10,12},{12... | collective-permute-start | bytes 688136 | tf_op jit(solution)/shard_map/ppermute | solution.py:22
  7.2 20.5 %collective-permute-start.1 = (bf16[2,448,128]{2,1,0:T(8,128)(2,1)}, bf16[2,448,128]{2,1,0:T(8,128)(2,1)S(1)}, u32[]{:S(2)}, u32[]{:S(2)}) collective-permute-start(bf16[2,448,128]{2,1,0:T(8,128)(2,1)} %bitcast.12), channel_id=1, source_target_pairs={{0,4},{2,6},{4,0},{6,2},{1,5},{3,7},{5,1},{7,3},{8,12},{10,14},{12... | collective-permute-start | bytes 688136 | tf_op jit(solution)/shard_map/ppermute | solution.py:22
  10.0 17.7 %collective-permute-start.9 = (bf16[2,464,128]{2,1,0:T(8,128)(2,1)S(1)}, bf16[2,464,128]{2,1,0:T(8,128)(2,1)S(1)}, u32[]{:S(2)}, u32[]{:S(2)}) collective-permute-start(bf16[2,464,128]{2,1,0:T(8,128)(2,1)S(1)} %shard_map.93.refs_0_), channel_id=1, source_target_pairs={{0,6},{2,0},{4,2},{6,4},{1,7},{3,1},{5,3},{7,5},{8,14},{10,8},{12,... | collective-permute-start | bytes 712712 | tf_op jit(solution)/shard_map/ppermute | solution.py:22
  21.5 12.8 %collective-permute-start.10 = (bf16[2,464,128]{2,1,0:T(8,128)(2,1)S(1)}, bf16[2,464,128]{2,1,0:T(8,128)(2,1)S(1)}, u32[]{:S(2)}, u32[]{:S(2)}) collective-permute-start(bf16[2,464,128]{2,1,0:T(8,128)(2,1)S(1)} %shard_map.93.refs_0_), channel_id=1, source_target_pairs={{0,1},{1,0},{2,3},{3,2},{4,5},{5,4},{6,7},{7,6},{8,9},{9,8},{10,11... | collective-permute-start | bytes 712712 | tf_op jit(solution)/shard_map/ppermute | solution.py:22
  21.5 13.3 %collective-permute-start.11 = (bf16[2,464,128]{2,1,0:T(8,128)(2,1)S(1)}, bf16[2,464,128]{2,1,0:T(8,128)(2,1)S(1)}, u32[]{:S(2)}, u32[]{:S(2)}) collective-permute-start(bf16[2,464,128]{2,1,0:T(8,128)(2,1)S(1)} %collective-permute-done.7.refs_1_), channel_id=1, source_target_pairs={{0,1},{1,0},{2,3},{3,2},{4,5},{5,4},{6,7},{7,6},{8,9},{9,8},{10,11... | collective-permute-start | bytes 712712 | tf_op jit(solution)/shard_map/ppermute | solution.py:22
  22.0 12.9 %collective-permute-start.12 = (bf16[2,464,128]{2,1,0:T(8,128)(2,1)S(1)}, bf16[2,464,128]{2,1,0:T(8,128)(2,1)S(1)}, u32[]{:S(2)}, u32[]{:S(2)}) collective-permute-start(bf16[2,464,128]{2,1,0:T(8,128)(2,1)S(1)} %collective-permute-done.8.refs_2_), channel_id=1, source_target_pairs={{0,1},{1,0},{2,3},{3,2},{4,5},{5,4},{6,7},{7,6},{8,9},{9,8},{10,11... | collective-permute-start | bytes 712712 | tf_op jit(solution)/shard_map/ppermute | solution.py:22
  27.6 6.7 %collective-permute-start.2 = (bf16[2,448,128]{2,1,0:T(8,128)(2,1)}, bf16[2,448,128]{2,1,0:T(8,128)(2,1)S(1)}, u32[]{:S(2)}, u32[]{:S(2)}) collective-permute-start(bf16[2,448,128]{2,1,0:T(8,128)(2,1)} %bitcast.13), channel_id=1, source_target_pairs={{0,6},{2,0},{4,2},{6,4},{1,7},{3,1},{5,3},{7,5},{8,14},{10,8},{12,... | collective-permute-start | bytes 688136 | tf_op jit(solution)/shard_map/ppermute | solution.py:22
  27.7 8.5 %collective-permute-start.13 = (bf16[2,464,128]{2,1,0:T(8,128)(2,1)S(1)}, bf16[2,464,128]{2,1,0:T(8,128)(2,1)S(1)}, u32[]{:S(2)}, u32[]{:S(2)}) collective-permute-start(bf16[2,464,128]{2,1,0:T(8,128)(2,1)S(1)} %collective-permute-done.9.refs_3_), channel_id=1, source_target_pairs={{0,1},{1,0},{2,3},{3,2},{4,5},{5,4},{6,7},{7,6},{8,9},{9,8},{10,11... | collective-permute-start | bytes 712712 | tf_op jit(solution)/shard_map/ppermute | solution.py:22
  34.3 12.9 %collective-permute-start.3 = (bf16[2,448,128]{2,1,0:T(8,128)(2,1)}, bf16[2,448,128]{2,1,0:T(8,128)(2,1)S(1)}, u32[]{:S(2)}, u32[]{:S(2)}) collective-permute-start(bf16[2,448,128]{2,1,0:T(8,128)(2,1)} %bitcast.14), channel_id=1, source_target_pairs={{0,1},{1,0},{2,3},{3,2},{4,5},{5,4},{6,7},{7,6},{8,9},{9,8},{10,11... | collective-permute-start | bytes 688136 | tf_op jit(solution)/shard_map/ppermute | solution.py:22
  34.4 12.9 %collective-permute-start.4 = (bf16[2,448,128]{2,1,0:T(8,128)(2,1)S(1)}, bf16[2,448,128]{2,1,0:T(8,128)(2,1)S(1)}, u32[]{:S(2)}, u32[]{:S(2)}) collective-permute-start(bf16[2,448,128]{2,1,0:T(8,128)(2,1)S(1)} %collective-permute-done.refs_1_), channel_id=1, source_target_pairs={{0,1},{1,0},{2,3},{3,2},{4,5},{5,4},{6,7},{7,6},{8,9},{9,8},{10,11... | collective-permute-start | bytes 688136 | tf_op jit(solution)/shard_map/ppermute | solution.py:22
  34.9 12.4 %collective-permute-start.5 = (bf16[2,448,128]{2,1,0:T(8,128)(2,1)S(1)}, bf16[2,448,128]{2,1,0:T(8,128)(2,1)}, u32[]{:S(2)}, u32[]{:S(2)}) collective-permute-start(bf16[2,448,128]{2,1,0:T(8,128)(2,1)S(1)} %collective-permute-done.1.refs_2_), channel_id=1, source_target_pairs={{0,1},{1,0},{2,3},{3,2},{4,5},{5,4},{6,7},{7,6},{8,9},{9,8},{10,11... | collective-permute-start | bytes 688136 | tf_op jit(solution)/shard_map/ppermute | solution.py:22
  35.0 12.4 %collective-permute-start.6 = (bf16[2,448,128]{2,1,0:T(8,128)(2,1)S(1)}, bf16[2,448,128]{2,1,0:T(8,128)(2,1)}, u32[]{:S(2)}, u32[]{:S(2)}) collective-permute-start(bf16[2,448,128]{2,1,0:T(8,128)(2,1)S(1)} %collective-permute-done.2.refs_3_), channel_id=1, source_target_pairs={{0,1},{1,0},{2,3},{3,2},{4,5},{5,4},{6,7},{7,6},{8,9},{9,8},{10,11... | collective-permute-start | bytes 688136 | tf_op jit(solution)/shard_map/ppermute | solution.py:22
  64.4 37.7 %collective-permute-start.14 = (bf16[4,464,256]{2,1,0:T(8,128)(2,1)}, bf16[4,464,256]{2,1,0:T(8,128)(2,1)S(1)}, u32[]{:S(2)}, u32[]{:S(2)}) collective-permute-start(bf16[4,464,256]{2,1,0:T(8,128)(2,1)} %get-tuple-element.39), channel_id=1, source_target_pairs={{0,1},{1,0},{2,3},{3,2},{4,5},{5,4},{6,7},{7,6},{8,9},{9,8},{10,11... | collective-permute-start | bytes 2850824 | tf_op jit(solution)/shard_map/ppermute | solution.py:22
  66.0 8.3 %collective-permute-start.18 = (f32[8,128]{1,0:T(8,128)S(1)}, f32[8,128]{1,0:T(8,128)S(1)}, u32[]{:S(2)}, u32[]{:S(2)}) collective-permute-start(f32[8,128]{1,0:T(8,128)S(1)} %broadcast_in_dim.10), channel_id=1, source_target_pairs={{0,64},{32,96},{64,0},{96,32},{1,65},{33,97},{65,1},{97,33},{2,66}... | collective-permute-start | bytes 12296 | tf_op jit(solution)/shard_map/ppermute | solution.py:22
  72.4 11.8 %collective-permute-start.36 = (bf16[4,224,128]{2,1,0:T(8,128)(2,1)}, bf16[4,224,128]{2,1,0:T(8,128)(2,1)S(1)}, u32[]{:S(2)}, u32[]{:S(2)}) collective-permute-start(bf16[4,224,128]{2,1,0:T(8,128)(2,1)} %copy-done.24), channel_id=1, source_target_pairs={{0,8},{8,16},{16,24},{24,0},{1,9},{9,17},{17,25},{25,1},{2,10},{10... | collective-permute-start | bytes 688136 | tf_op jit(solution)/shard_map/ppermute | solution.py:22
  74.3 8.8 %collective-permute-start.21 = (f32[8,128]{1,0:T(8,128)S(1)}, f32[8,128]{1,0:T(8,128)S(1)}, u32[]{:S(2)}, u32[]{:S(2)}) collective-permute-start(f32[8,128]{1,0:T(8,128)S(1)} %add_add_fusion), channel_id=1, source_target_pairs={{0,16},{8,24},{16,0},{24,8},{1,17},{9,25},{17,1},{25,9},{2,18},{10... | collective-permute-start | bytes 12296 | tf_op jit(solution)/shard_map/ppermute | solution.py:22
  83.1 7.7 %collective-permute-start.37 = (bf16[4,224,128]{2,1,0:T(8,128)(2,1)}, bf16[4,224,128]{2,1,0:T(8,128)(2,1)S(1)}, u32[]{:S(2)}, u32[]{:S(2)}) collective-permute-start(bf16[4,224,128]{2,1,0:T(8,128)(2,1)} %copy-done.23), channel_id=1, source_target_pairs={{0,16},{8,24},{16,0},{24,8},{1,17},{9,25},{17,1},{25,9},{2,18},{10... | collective-permute-start | bytes 688136 | tf_op jit(solution)/shard_map/ppermute | solution.py:22
  83.2 9.2 %collective-permute-start.38 = (bf16[4,224,128]{2,1,0:T(8,128)(2,1)}, bf16[4,224,128]{2,1,0:T(8,128)(2,1)S(1)}, u32[]{:S(2)}, u32[]{:S(2)}) collective-permute-start(bf16[4,224,128]{2,1,0:T(8,128)(2,1)} %copy-done.22), channel_id=1, source_target_pairs={{0,24},{8,0},{16,8},{24,16},{1,25},{9,1},{17,9},{25,17},{2,26},{10... | collective-permute-start | bytes 688136 | tf_op jit(solution)/shard_map/ppermute | solution.py:22
  84.1 9.5 %collective-permute-start.24 = (bf16[448,256]{1,0:T(8,128)(2,1)}, bf16[448,256]{1,0:T(8,128)(2,1)}, u32[]{:S(2)}, u32[]{:S(2)}) collective-permute-start(bf16[448,256]{1,0:T(8,128)(2,1)} %copy-done.21), channel_id=1, source_target_pairs={{0,32},{32,64},{64,96},{96,0},{1,33},{33,65},{65,97},{97,1},{2,34}... | collective-permute-start | bytes 688136 | tf_op jit(solution)/shard_map/ppermute | solution.py:22
  84.2 12.0 %collective-permute-start.25 = (bf16[448,256]{1,0:T(8,128)(2,1)}, bf16[448,256]{1,0:T(8,128)(2,1)}, u32[]{:S(2)}, u32[]{:S(2)}) collective-permute-start(bf16[448,256]{1,0:T(8,128)(2,1)} %copy-done.20), channel_id=1, source_target_pairs={{0,64},{32,96},{64,0},{96,32},{1,65},{33,97},{65,1},{97,33},{2,66}... | collective-permute-start | bytes 688136 | tf_op jit(solution)/shard_map/ppermute | solution.py:22
  90.9 6.6 %collective-permute-start.26 = (bf16[448,256]{1,0:T(8,128)(2,1)}, bf16[448,256]{1,0:T(8,128)(2,1)}, u32[]{:S(2)}, u32[]{:S(2)}) collective-permute-start(bf16[448,256]{1,0:T(8,128)(2,1)} %copy-done.19), channel_id=1, source_target_pairs={{0,96},{32,0},{64,32},{96,64},{1,97},{33,1},{65,33},{97,65},{2,98}... | collective-permute-start | bytes 688136 | tf_op jit(solution)/shard_map/ppermute | solution.py:22
  93.7 7.2 %collective-permute-start.40 = (bf16[4,224,128]{2,1,0:T(8,128)(2,1)S(1)}, bf16[4,224,128]{2,1,0:T(8,128)(2,1)S(1)}, u32[]{:S(2)}, u32[]{:S(2)}) collective-permute-start(bf16[4,224,128]{2,1,0:T(8,128)(2,1)S(1)} %collective-permute-done.37.m2), channel_id=1, source_target_pairs={{0,1},{1,0},{2,3},{3,2},{4,5},{5,4},{6,7},{7,6},{8,9},{9,8},{10,11... | collective-permute-start | bytes 688136 | tf_op jit(solution)/shard_map/ppermute | solution.py:22
  96.1 5.7 %collective-permute-start.41 = (bf16[4,224,128]{2,1,0:T(8,128)(2,1)S(1)}, bf16[4,224,128]{2,1,0:T(8,128)(2,1)S(1)}, u32[]{:S(2)}, u32[]{:S(2)}) collective-permute-start(bf16[4,224,128]{2,1,0:T(8,128)(2,1)S(1)} %collective-permute-done.38.m3), channel_id=1, source_target_pairs={{0,1},{1,0},{2,3},{3,2},{4,5},{5,4},{6,7},{7,6},{8,9},{9,8},{10,11... | collective-permute-start | bytes 688136 | tf_op jit(solution)/shard_map/ppermute | solution.py:22
  97.5 13.0 %collective-permute-start.42 = (bf16[896,256]{1,0:T(8,128)(2,1)}, bf16[896,256]{1,0:T(8,128)(2,1)S(1)}, u32[]{:S(2)}, u32[]{:S(2)}) collective-permute-start(bf16[896,256]{1,0:T(8,128)(2,1)} %copy-done.9), channel_id=1, source_target_pairs={{0,8},{8,16},{16,24},{24,0},{1,9},{9,17},{17,25},{25,1},{2,10},{10... | collective-permute-start | bytes 1376264 | tf_op jit(solution)/shard_map/ppermute | solution.py:22
  97.9 23.4 %collective-permute-start.43 = (bf16[896,256]{1,0:T(8,128)(2,1)}, bf16[896,256]{1,0:T(8,128)(2,1)S(1)}, u32[]{:S(2)}, u32[]{:S(2)}) collective-permute-start(bf16[896,256]{1,0:T(8,128)(2,1)} %copy-done.9), channel_id=1, source_target_pairs={{0,16},{8,24},{16,0},{24,8},{1,17},{9,25},{17,1},{25,9},{2,18},{10... | collective-permute-start | bytes 1376264 | tf_op jit(solution)/shard_map/ppermute | solution.py:22
  100.9 21.1 %collective-permute-start.44 = (bf16[896,256]{1,0:T(8,128)(2,1)}, bf16[896,256]{1,0:T(8,128)(2,1)S(1)}, u32[]{:S(2)}, u32[]{:S(2)}) collective-permute-start(bf16[896,256]{1,0:T(8,128)(2,1)} %copy-done.9), channel_id=1, source_target_pairs={{0,24},{8,0},{16,8},{24,16},{1,25},{9,1},{17,9},{25,17},{2,26},{10... | collective-permute-start | bytes 1376264 | tf_op jit(solution)/shard_map/ppermute | solution.py:22
  101.9 22.8 %collective-permute-start.30 = (bf16[896,256]{1,0:T(8,128)(2,1)}, bf16[896,256]{1,0:T(8,128)(2,1)S(1)}, u32[]{:S(2)}, u32[]{:S(2)}) collective-permute-start(bf16[896,256]{1,0:T(8,128)(2,1)} %copy-done.5), channel_id=1, source_target_pairs={{0,32},{32,64},{64,96},{96,0},{1,33},{33,65},{65,97},{97,1},{2,34}... | collective-permute-start | bytes 1376264 | tf_op jit(solution)/shard_map/ppermute | solution.py:22
  102.1 29.0 %collective-permute-start.31 = (bf16[896,256]{1,0:T(8,128)(2,1)}, bf16[896,256]{1,0:T(8,128)(2,1)S(1)}, u32[]{:S(2)}, u32[]{:S(2)}) collective-permute-start(bf16[896,256]{1,0:T(8,128)(2,1)} %copy-done.5), channel_id=1, source_target_pairs={{0,64},{32,96},{64,0},{96,32},{1,65},{33,97},{65,1},{97,33},{2,66}... | collective-permute-start | bytes 1376264 | tf_op jit(solution)/shard_map/ppermute | solution.py:22
  110.5 22.7 %collective-permute-start.15 = (bf16[464,256]{1,0:T(8,128)(2,1)S(1)}, bf16[464,256]{1,0:T(8,128)(2,1)S(1)}, u32[]{:S(2)}, u32[]{:S(2)}) collective-permute-start(bf16[464,256]{1,0:T(8,128)(2,1)S(1)} %get-tuple-element.42), channel_id=1, source_target_pairs={{0,2},{2,4},{4,6},{6,0},{1,3},{3,5},{5,7},{7,1},{8,10},{10,12},{12... | collective-permute-start | bytes 712712 | tf_op jit(solution)/shard_map/ppermute | solution.py:22
  121.4 11.9 %collective-permute-start.16 = (bf16[464,256]{1,0:T(8,128)(2,1)S(1)}, bf16[464,256]{1,0:T(8,128)(2,1)S(1)}, u32[]{:S(2)}, u32[]{:S(2)}) collective-permute-start(bf16[464,256]{1,0:T(8,128)(2,1)S(1)} %get-tuple-element.43), channel_id=1, source_target_pairs={{0,4},{2,6},{4,0},{6,2},{1,5},{3,7},{5,1},{7,3},{8,12},{10,14},{12... | collective-permute-start | bytes 712712 | tf_op jit(solution)/shard_map/ppermute | solution.py:22
  122.0 11.7 %collective-permute-start.17 = (bf16[464,256]{1,0:T(8,128)(2,1)S(1)}, bf16[464,256]{1,0:T(8,128)(2,1)S(1)}, u32[]{:S(2)}, u32[]{:S(2)}) collective-permute-start(bf16[464,256]{1,0:T(8,128)(2,1)S(1)} %get-tuple-element.44), channel_id=1, source_target_pairs={{0,6},{2,0},{4,2},{6,4},{1,7},{3,1},{5,3},{7,5},{8,14},{10,8},{12,... | collective-permute-start | bytes 712712 | tf_op jit(solution)/shard_map/ppermute | solution.py:22
  125.5 10.3 %collective-permute-start.32 = (bf16[896,256]{1,0:T(8,128)(2,1)}, bf16[896,256]{1,0:T(8,128)(2,1)}, u32[]{:S(2)}, u32[]{:S(2)}) collective-permute-start(bf16[896,256]{1,0:T(8,128)(2,1)} %copy-done.5), channel_id=1, source_target_pairs={{0,96},{32,0},{64,32},{96,64},{1,97},{33,1},{65,33},{97,65},{2,98}... | collective-permute-start | bytes 1376264 | tf_op jit(solution)/shard_map/ppermute | solution.py:22
  131.1 19.2 %collective-permute-start.45 = (bf16[224,896]{1,0:T(8,128)(2,1)}, bf16[224,896]{1,0:T(8,128)(2,1)S(1)}, u32[]{:S(2)}, u32[]{:S(2)}) collective-permute-start(bf16[224,896]{1,0:T(8,128)(2,1)} %get-tuple-element.60), channel_id=1, source_target_pairs={{0,32},{32,64},{64,96},{96,0},{1,33},{33,65},{65,97},{97,1},{2,34}... | collective-permute-start | bytes 1204232 | tf_op jit(solution)/shard_map/ppermute | solution.py:22
  133.2 6.1 %collective-permute-start.28 = (bf16[448,256]{1,0:T(8,128)(2,1)}, bf16[448,256]{1,0:T(8,128)(2,1)}, u32[]{:S(2)}, u32[]{:S(2)}) collective-permute-start(bf16[448,256]{1,0:T(8,128)(2,1)} %collective-permute-done.25.m2), channel_id=1, source_target_pairs={{0,1},{1,0},{2,3},{3,2},{4,5},{5,4},{6,7},{7,6},{8,9},{9,8},{10,11... | collective-permute-start | bytes 688136 | tf_op jit(solution)/shard_map/ppermute | solution.py:22
  133.7 5.6 %collective-permute-start.29 = (bf16[448,256]{1,0:T(8,128)(2,1)}, bf16[448,256]{1,0:T(8,128)(2,1)}, u32[]{:S(2)}, u32[]{:S(2)}) collective-permute-start(bf16[448,256]{1,0:T(8,128)(2,1)} %collective-permute-done.26.m3), channel_id=1, source_target_pairs={{0,1},{1,0},{2,3},{3,2},{4,5},{5,4},{6,7},{7,6},{8,9},{9,8},{10,11... | collective-permute-start | bytes 688136 | tf_op jit(solution)/shard_map/ppermute | solution.py:22
  135.8 19.6 %collective-permute-start.46 = (bf16[224,896]{1,0:T(8,128)(2,1)}, bf16[224,896]{1,0:T(8,128)(2,1)S(1)}, u32[]{:S(2)}, u32[]{:S(2)}) collective-permute-start(bf16[224,896]{1,0:T(8,128)(2,1)} %copy-done.18), channel_id=1, source_target_pairs={{0,64},{32,96},{64,0},{96,32},{1,65},{33,97},{65,1},{97,33},{2,66}... | collective-permute-start | bytes 1204232 | tf_op jit(solution)/shard_map/ppermute | solution.py:22
  136.1 14.2 %collective-permute-start.48 = (f32[448]{0:T(512)S(1)}, f32[448]{0:T(512)S(1)}, u32[]{:S(2)}, u32[]{:S(2)}) collective-permute-start(f32[448]{0:T(512)S(1)} %reduce.1), channel_id=1, source_target_pairs={{0,64},{32,96},{64,0},{96,32},{1,65},{33,97},{65,1},{97,33},{2,66}... | collective-permute-start | bytes 5384 | tf_op jit(solution)/shard_map/ppermute | solution.py:22
  139.4 12.9 %collective-permute-start.49 = (f32[448]{0:T(512)S(1)}, f32[448]{0:T(512)S(1)}, u32[]{:S(2)}, u32[]{:S(2)}) collective-permute-start(f32[448]{0:T(512)S(1)} %reduce.1), channel_id=1, source_target_pairs={{0,32},{32,64},{64,96},{96,0},{1,33},{33,65},{65,97},{97,1},{2,34}... | collective-permute-start | bytes 5384 | tf_op jit(solution)/shard_map/ppermute | solution.py:22
  144.5 10.9 %collective-permute-start.50 = (f32[448]{0:T(512)S(1)}, f32[448]{0:T(512)S(1)}, u32[]{:S(2)}, u32[]{:S(2)}) collective-permute-start(f32[448]{0:T(512)S(1)} %reduce.1), channel_id=1, source_target_pairs={{0,96},{32,0},{64,32},{96,64},{1,97},{33,1},{65,33},{97,65},{2,98}... | collective-permute-start | bytes 5384 | tf_op jit(solution)/shard_map/ppermute | solution.py:22
  150.3 8.1 %collective-permute-start.47 = (bf16[224,896]{1,0:T(8,128)(2,1)}, bf16[224,896]{1,0:T(8,128)(2,1)S(1)}, u32[]{:S(2)}, u32[]{:S(2)}) collective-permute-start(bf16[224,896]{1,0:T(8,128)(2,1)} %copy-done.17), channel_id=1, source_target_pairs={{0,96},{32,0},{64,32},{96,64},{1,97},{33,1},{65,33},{97,65},{2,98}... | collective-permute-start | bytes 1204232 | tf_op jit(solution)/shard_map/ppermute | solution.py:22
  150.3 12.9 %collective-permute-start.33 = (bf16[224,896]{1,0:T(8,128)(2,1)S(1)}, bf16[224,896]{1,0:T(8,128)(2,1)S(1)}, u32[]{:S(2)}, u32[]{:S(2)}) collective-permute-start(bf16[224,896]{1,0:T(8,128)(2,1)S(1)} %get-tuple-element.51), channel_id=1, source_target_pairs={{0,8},{8,16},{16,24},{24,0},{1,9},{9,17},{17,25},{25,1},{2,10},{10... | collective-permute-start | bytes 1204232 | tf_op jit(solution)/shard_map/ppermute | solution.py:22
  152.3 18.3 %collective-permute-start.34 = (bf16[224,896]{1,0:T(8,128)(2,1)S(1)}, bf16[224,896]{1,0:T(8,128)(2,1)S(1)}, u32[]{:S(2)}, u32[]{:S(2)}) collective-permute-start(bf16[224,896]{1,0:T(8,128)(2,1)S(1)} %get-tuple-element.52), channel_id=1, source_target_pairs={{0,16},{8,24},{16,0},{24,8},{1,17},{9,25},{17,1},{25,9},{2,18},{10... | collective-permute-start | bytes 1204232 | tf_op jit(solution)/shard_map/ppermute | solution.py:22
  155.4 15.2 %collective-permute-start.35 = (bf16[224,896]{1,0:T(8,128)(2,1)S(1)}, bf16[224,896]{1,0:T(8,128)(2,1)S(1)}, u32[]{:S(2)}, u32[]{:S(2)}) collective-permute-start(bf16[224,896]{1,0:T(8,128)(2,1)S(1)} %get-tuple-element.53), channel_id=1, source_target_pairs={{0,24},{8,0},{16,8},{24,16},{1,25},{9,1},{17,9},{25,17},{2,26},{10... | collective-permute-start | bytes 1204232 | tf_op jit(solution)/shard_map/ppermute | solution.py:22
  155.4 16.5 %collective-permute-start.51 = (f32[448]{0:T(512)S(1)}, f32[448]{0:T(512)S(1)}, u32[]{:S(2)}, u32[]{:S(2)}) collective-permute-start(f32[448]{0:T(512)S(1)} %add_add_fusion.2), channel_id=1, source_target_pairs={{0,16},{8,24},{16,0},{24,8},{1,17},{9,25},{17,1},{25,9},{2,18},{10... | collective-permute-start | bytes 5384 | tf_op jit(solution)/shard_map/ppermute | solution.py:22
  158.4 13.5 %collective-permute-start.52 = (f32[448]{0:T(512)S(1)}, f32[448]{0:T(512)S(1)}, u32[]{:S(2)}, u32[]{:S(2)}) collective-permute-start(f32[448]{0:T(512)S(1)} %add_add_fusion.2), channel_id=1, source_target_pairs={{0,8},{8,16},{16,24},{24,0},{1,9},{9,17},{17,25},{25,1},{2,10},{10... | collective-permute-start | bytes 5384 | tf_op jit(solution)/shard_map/ppermute | solution.py:22
  163.2 8.7 %collective-permute-start.53 = (f32[448]{0:T(512)S(1)}, f32[448]{0:T(512)S(1)}, u32[]{:S(2)}, u32[]{:S(2)}) collective-permute-start(f32[448]{0:T(512)S(1)} %add_add_fusion.2), channel_id=1, source_target_pairs={{0,24},{8,0},{16,8},{24,16},{1,25},{9,1},{17,9},{25,17},{2,26},{10... | collective-permute-start | bytes 5384 | tf_op jit(solution)/shard_map/ppermute | solution.py:22
  (34 other events, 306.8 us)

commit v3 on v2

v3 whole, which is shorter than its diff:
```python
import jax
import jax.numpy as jnp
from jax import lax
from jax.experimental import pallas as pl
from jax.experimental.pallas import tpu as pltpu
from jax.sharding import Mesh
from jax.sharding import PartitionSpec as P

INTERPRET = False
MIB = 1024 * 1024
EPS = 1e-06
EXTRA = 16
STAGE_LIMIT = 44
GELU_A = 0.7978845608028654
GELU_B = 0.044715

F32 = jnp.float32
BF16 = jnp.bfloat16


def moved(value, axis, step):
    size = lax.axis_size(axis)
    return lax.ppermute(value, axis, [(i, (i + step) % size) for i in range(size)])


def led(value, axis, sign):
    size = lax.axis_size(axis)
    pairs = [
        (2 * i + c, 2 * ((i + sign * (1 - 2 * c)) % size) + c) for i in range(size) for c in (0, 1)
    ]
    return lax.ppermute(value, (axis, "c"), pairs)


def gathered(value, axis):
    behind = led(value, axis, 1)
    ahead = led(value, axis, -1)
    return behind, ahead, led(behind, axis, 1)


def sibling(value):
    return moved(value, "c", 1)


def total_over(value, axes):
    for axis in axes:
        a, b, c = (moved(value, axis, step) for step in (1, 2, 3))
        value = (value + b) + (a + c)
    return value


def spec(space=pltpu.VMEM):
    return pl.BlockSpec(memory_space=space)


def call(body, outs, ins, scratch=(), flops=0, moved_bytes=0, limit=8):
    return pl.pallas_call(
        body,
        out_shape=[jax.ShapeDtypeStruct(s, d) for s, d in outs],
        in_specs=[spec(space) for _, space in ins],
        out_specs=[spec() for _ in outs],
        scratch_shapes=list(scratch),
        cost_estimate=pl.CostEstimate(flops=flops, bytes_accessed=moved_bytes, transcendentals=0),
        compiler_params=pltpu.CompilerParams(vmem_limit_bytes=limit * MIB),
        interpret=INTERPRET,
    )(*[a for a, _ in ins])


V, S, H = pltpu.VMEM, pltpu.SMEM, pltpu.HBM


def split3(value):
    hi = value.astype(BF16)
    rest = value - hi.astype(F32)
    mid = rest.astype(BF16)
    return hi, mid, (rest - mid.astype(F32)).astype(BF16)


def extra_rows(value):
    parts = [p.astype(F32) for p in split3(value)]
    row = lax.broadcasted_iota(jnp.int32, (EXTRA, value.shape[-1]), 0)
    out = jnp.where(row == 0, parts[0], 0.0)
    out = jnp.where(row == 1, parts[1], out)
    return jnp.where(row == 2, parts[2], out).astype(BF16)


def sum_extra(rows):
    return jnp.sum(rows.astype(F32), axis=0, keepdims=True)


def dot(left, right, dims):
    return lax.dot_general(left, right, (dims, ((), ())), preferred_element_type=F32)


def live_row(sc, tok):
    pos = lax.broadcasted_iota(jnp.int32, (1, 2 * tok), 1)
    in_first = pos < tok
    limit = jnp.where(in_first, sc[4], sc[5] + tok)
    return (pos < limit).astype(F32)


def gain_columns(g_ref, tok):
    return jnp.broadcast_to(g_ref[...], (tok, g_ref.shape[1])).T


OTHER = (0, 2, 1, 3)


def listed(target, here, c):
    delta = (target - here + 8) % 4
    return jnp.where(delta == 0, 0, jnp.where(delta == 2, 3, jnp.where((delta == 3) == (c == 0), 1, 2)))


def prepare(fill, hidden_t, out_t, gain):
    micro, width, tok = hidden_t.shape
    body_rows = width + EXTRA

    def body(fill_ref, h_ref, o_ref, g_ref, out_ref, count_ref):
        g = gain_columns(g_ref, tok)
        for m in range(micro):
            h = h_ref[m].astype(F32)
            out_ref[m, :width, :] = (h * g).astype(BF16)
            out_ref[m, width:body_rows, :] = extra_rows(jnp.sum(h * h, axis=0, keepdims=True))
            out_ref[m, body_rows:, :] = o_ref[m]
        count_ref[...] = jnp.full(count_ref.shape, (fill_ref[0, 0] + fill_ref[1, 0]).astype(F32))

    return call(
        body,
        [((micro, body_rows + width, tok), BF16), ((8, 128), F32)],
        [(fill, S), (hidden_t, V), (out_t, V), (gain, V)],
    )


def stage_weights(sc, up, down):
    d, ff = up.shape
    pair = d // 4

    def body(sc, up_ref, down_ref, upv, downv, sem):
        y, c = sc[1], sc[3]
        s = 1 - 2 * c
        copies = []
        for k, chip in enumerate((y, y - s, y + s, y + 2)):
            start = pl.multiple_of(((chip + 4) % 4) * pair, pair)
            copies.append(
                pltpu.make_async_copy(up_ref.at[pl.ds(start, pair), :], upv.at[k], sem.at[k])
            )
            copies.append(
                pltpu.make_async_copy(down_ref.at[:, pl.ds(start, pair)], downv.at[k], sem.at[4 + k])
            )
        for copy in copies:
            copy.start()
        for copy in copies:
            copy.wait()

    return call(
        body,
        [((4, pair, ff), BF16), ((4, ff, pair), BF16)],
        [(sc, S), (up, H), (down, H)],
        [pltpu.SemaphoreType.DMA((8,))],
        flops=10**9,
        moved_bytes=4 * d * ff,
        limit=STAGE_LIMIT,
    )


def mlp(sc, upv, downv, own, other):
    micro, padded, tok = own[0].shape
    width = (padded - EXTRA) // 2
    below = width + EXTRA
    pair = 2 * width
    quarter = pair // 4
    ff = upv.shape[2]
    d = 4 * pair
    cols = micro * tok

    def body(sc, up_ref, down_ref, *refs):
        r, t = refs[0:4], refs[4:8]
        act_ref, gp_ref, inv_ref, rd_ref, hown, ha, h2, oown, oa, o2, hbuf, obuf = refs[8:]
        x, y, z, c = sc[0], sc[1], sc[2], sc[3]
        s = 1 - 2 * c
        mine = pl.multiple_of(c * width, width)
        its = pl.multiple_of((1 - c) * width, width)
        squares = []
        for m in range(micro):
            cut = slice(m * tok, (m + 1) * tok)
            total = jnp.zeros((1, tok), F32)
            for k in range(4):
                a, b = r[k], t[OTHER[k]]
                hbuf[k, pl.ds(mine, width), cut] = a[m, :width, :]
                hbuf[k, pl.ds(its, width), cut] = b[m, :width, :]
                obuf[k, pl.ds(mine, width), cut] = a[m, below:, :]
                obuf[k, pl.ds(its, width), cut] = b[m, below:, :]
                total = total + sum_extra(a[m, width:below, :]) + sum_extra(b[m, width:below, :])
            squares.append(total)
        inv = lax.rsqrt(jnp.concatenate(squares, axis=1) / d + EPS)
        inv_ref[...] = jnp.broadcast_to(inv, inv_ref.shape)
        hown[...] = hbuf[listed(x, y, c)]
        ha[...] = hbuf[listed(x + s, y, c)]
        h2[...] = hbuf[listed(x + 2, y, c), pl.ds(mine, width), :]
        for ref, place in ((oown, z), (oa, z + s), (o2, z + 2)):
            row = pl.multiple_of(((place + 4) % 4) * quarter, quarter)
            for j in range(4):
                block = obuf[j, pl.ds(row, quarter), :]
                if ref is o2:
                    block = jnp.where(c == 0, block[:, :tok], block[:, tok:])
                ref[j] = block
        acc = dot(hbuf[0].T, up_ref[0], ((1,), (0,)))
        for k in range(1, 4):
            acc = acc + dot(hbuf[k].T, up_ref[k], ((1,), (0,)))
        pre = acc.T * inv
        live = live_row(sc, tok)
        cube = GELU_B * pre * pre
        th = jnp.tanh(GELU_A * (pre + cube * pre))
        act_ref[...] = (0.5 * pre * (1.0 + th) * live).astype(BF16)
        slope = 0.5 * (1.0 + th) + 0.5 * pre * (1.0 - th * th) * (GELU_A * (1.0 + 3.0 * cube))
        acc = dot(down_ref[0], obuf[0], ((1,), (0,)))
        for k in range(1, 4):
            acc = acc + dot(down_ref[k], obuf[k], ((1,), (0,)))
        gp = (acc * slope * (inv * live)).astype(BF16)
        gp_ref[...] = gp
        rd = jnp.sum(gp.astype(F32) * pre, axis=0, keepdims=True)
        rd_ref[...] = jnp.broadcast_to(rd, rd_ref.shape)

    return call(
        body,
        [
            ((ff, cols), BF16),
            ((ff, cols), BF16),
            ((8, cols), F32),
            ((8, cols), F32),
            ((pair, cols), BF16),
            ((pair, cols), BF16),
            ((width, cols), BF16),
            ((4, quarter, cols), BF16),
            ((4, quarter, cols), BF16),
            ((4, quarter, tok), BF16),
        ],
        [(sc, S), (upv, V), (downv, V)] + [(a, V) for a in (*own, *other)],
        [pltpu.VMEM((4, pair, cols), BF16), pltpu.VMEM((4, pair, cols), BF16)],
        flops=4 * d * ff * cols,
        moved_bytes=d * ff * 4,
        limit=16,
    )


def normed_part(sc, upv, gp, rd):
    _, pair, ff = upv.shape
    width = pair // 2
    cols = gp.shape[1]

    def body(sc, up_ref, gp_ref, rd_ref, pown_ref, psib_ref):
        c = sc[3]
        mine = pl.multiple_of(c * width, width)
        its = pl.multiple_of((1 - c) * width, width)
        gp = gp_ref[...]
        tail = extra_rows(rd_ref[0:1, :])
        for k in range(4):
            j = OTHER[k]
            psib_ref[j, :width, :] = dot(up_ref[k, pl.ds(its, width), :], gp, ((1,), (0,))).astype(BF16)
            psib_ref[j, width:, :] = tail
            pown_ref[k] = dot(up_ref[k, pl.ds(mine, width), :], gp, ((1,), (0,)))

    return call(
        body,
        [((4, width, cols), F32), ((4, width + EXTRA, cols), BF16)],
        [(sc, S), (upv, V), (gp, V), (rd, V)],
        flops=8 * pair * ff * cols,
        moved_bytes=8 * pair * ff,
    )


def pair_sum(pown, psib, rd):
    width, cols = pown.shape[1:]

    def body(p_ref, s_ref, rd_ref, q0, rd0, q1, q2, q3):
        total = rd_ref[0:1, :] + sum_extra(s_ref[0, width:, :])
        q0[...] = p_ref[0] + s_ref[0, :width, :].astype(F32)
        rd0[...] = jnp.broadcast_to(total, rd0.shape)
        tail = extra_rows(total)
        for k, ref in ((1, q1), (2, q2), (3, q3)):
            ref[:width, :] = (p_ref[k] + s_ref[k, :width, :].astype(F32)).astype(BF16)
            ref[width:, :] = tail

    return call(
        body,
        [((width, cols), F32), ((8, cols), F32)] + [((width + EXTRA, cols), BF16)] * 3,
        [(pown, V), (psib, V), (rd, V)],
    )


def input_grad(sc, q0, rd0, recv, hidden_t, out_t, gain, inv, inv_count):
    micro, width, tok = hidden_t.shape

    def body(sc, q0, rd0, r1, r2, r3, h_ref, o_ref, g_ref, inv_ref, ic_ref, out_ref, gain_ref):
        d = 8 * width
        grad = q0[...]
        rd = rd0[0:1, :]
        for ref in (r1, r2, r3):
            grad = grad + ref[:width, :].astype(F32)
            rd = rd + sum_extra(ref[width:, :])
        live = live_row(sc, tok)
        ic = ic_ref[0:1, :]
        g = gain_columns(g_ref, tok)
        factor = inv_ref[0:1, :] * rd / d
        total = jnp.zeros((width, tok), F32)
        for m in range(micro):
            cut = slice(m * tok, (m + 1) * tok)
            h = h_ref[m].astype(F32)
            scaled = (o_ref[m].astype(F32) * (live[:, cut] * ic)).astype(BF16).astype(F32)
            rest = g * grad[:, cut] - h * factor[:, cut]
            out_ref[m] = (scaled + rest * ic).astype(BF16)
            total = total + grad[:, cut] * h
        gain_ref[...] = jnp.sum(total, axis=1, keepdims=True) * ic[:, :1]

    return call(
        body,
        [((micro, width, tok), BF16), ((width, 1), F32)],
        [(sc, S)] + [(a, V) for a in (q0, rd0, *recv, hidden_t, out_t, gain, inv, inv_count)],
    )


def gradient_start(lefts, rights, micro_rows=False):
    rows = lefts[0].shape[0] * (lefts[0].shape[1] if micro_rows else 1)
    cols = rights[0].shape[1]
    ff = rights[0].shape[0]

    def body(l0, l1, l2, r0, r1, r2, acc_ref, lbuf, rbuf):
        for k, (left, right) in enumerate(((l0, r0), (l1, r1), (l2, r2))):
            cut = slice(k * cols, (k + 1) * cols)
            rbuf[:, cut] = right[...]
            if micro_rows:
                size = left.shape[1]
                for j in range(4):
                    lbuf[j * size : (j + 1) * size, cut] = left[OTHER[j] if k == 2 else j]
            else:
                lbuf[:, cut] = left[...]
        acc_ref[...] = dot(lbuf[...], rbuf[...], ((1,), (1,)))

    return call(
        body,
        [((rows, ff), F32)],
        [(a, V) for a in (*lefts, *rights)],
        [pltpu.VMEM((rows, 3 * cols), BF16), pltpu.VMEM((ff, 3 * cols), BF16)],
        flops=2 * rows * ff * cols * 3,
        limit=12,
    )[0]


def up_finish(sc, acc, mine, its, gp):
    width, cols = mine.shape
    ff = gp.shape[0]
    rows = width // 2

    def body(sc, acc_ref, m_ref, i_ref, g_ref, b0, b1, b2, b3, lbuf, total):
        z, c = sc[2], sc[3]
        lbuf[pl.ds(pl.multiple_of(c * width, width), width), :] = m_ref[...]
        lbuf[pl.ds(pl.multiple_of((1 - c) * width, width), width), :] = i_ref[...]
        total[...] = acc_ref[...] + dot(lbuf[...], g_ref[...], ((1,), (1,)))
        for k, ref in enumerate((b0, b1, b2, b3)):
            start = pl.multiple_of(((z + k) % 4) * rows, rows)
            ref[...] = total[pl.ds(start, rows), :].astype(ref.dtype)

    return call(
        body,
        [((rows, ff), F32)] + [((rows, ff), BF16)] * 3,
        [(sc, S)] + [(a, V) for a in (acc, mine, its, gp)],
        [pltpu.VMEM((2 * width, cols), BF16), pltpu.VMEM((2 * width, ff), F32)],
        flops=4 * width * ff * cols,
        limit=12,
    )


def down_finish(sc, acc, mine, its, act):
    _, rows, tok = mine.shape
    ff, cols = act.shape

    def body(sc, acc_ref, m_ref, i_ref, a_ref, b0, b1, b2, b3, lbuf, total):
        x, y, c = sc[0], sc[1], sc[3]
        for j in range(4):
            cut = slice(j * rows, (j + 1) * rows)
            left, right = m_ref[j], i_ref[OTHER[j]]
            lbuf[cut, :tok] = jnp.where(c == 0, left, right)
            lbuf[cut, tok:] = jnp.where(c == 0, right, left)
        total[...] = acc_ref[...] + dot(lbuf[...], a_ref[...], ((1,), (1,)))
        for k, ref in enumerate((b0, b1, b2, b3)):
            start = pl.multiple_of(listed(x + k, y, c) * rows, rows)
            ref[...] = total[pl.ds(start, rows), :].astype(ref.dtype)

    return call(
        body,
        [((rows, ff), F32)] + [((rows, ff), BF16)] * 3,
        [(sc, S)] + [(a, V) for a in (acc, mine, its, act)],
        [pltpu.VMEM((4 * rows, cols), BF16), pltpu.VMEM((4 * rows, ff), F32)],
        flops=8 * rows * ff * cols,
        limit=12,
    )


def at_owner(blocks, axis):
    return (blocks[0],) + tuple(moved(blocks[k], axis, k) for k in (1, 2, 3))


def add_up(blocks, inv_count):
    first, *rest = blocks

    def body(own, r1, r2, r3, ic_ref, out_ref):
        total = own[...] + r1[...].astype(F32) + (r2[...].astype(F32) + r3[...].astype(F32))
        out_ref[...] = total * ic_ref[0:1, 0:1]

    return call(body, [(first.shape, F32)], [(a, V) for a in (first, *rest, inv_count)])[0]


def on_device(hidden_in, out_grad, pack_fill, norm_gain, up_weight, down_weight):
    hidden_t = jnp.swapaxes(hidden_in, 1, 2)
    out_t = jnp.swapaxes(out_grad, 1, 2)
    gain_row = norm_gain[None, :]
    place = [lax.axis_index(a) for a in ("x", "y", "z", "c")]
    sc = jnp.concatenate(
        [jnp.stack(place).astype(jnp.int32), pack_fill[:, 0], jnp.zeros((2,), jnp.int32)]
    )

    payload, count = prepare(pack_fill, hidden_t, out_t, gain_row)
    own = (payload, *gathered(payload, "y"))
    other = tuple(sibling(a) for a in own)
    upv, downv = stage_weights(sc, up_weight, down_weight)
    inv_count = 1.0 / total_over(count, ("x", "z"))

    act, gp, inv, rd, h_own, h_a, h_2, o_own, o_a, o_2 = mlp(sc, upv, downv, own, other)
    gps = gathered(gp, "x")
    acts = gathered(act, "z")
    h_a = led(h_a, "x", 1)
    o_a = led(o_a, "z", 1)
    h_2 = moved(h_2, "x", 2)
    o_2 = moved(o_2, "z", 2)

    pown, psib = normed_part(sc, upv, gp, rd)
    q0, rd0, *q_send = pair_sum(pown, sibling(psib), rd)
    q_recv = (led(q_send[0], "y", -1), led(q_send[1], "y", 1), moved(q_send[2], "y", 2))

    up_acc = gradient_start((h_own, h_a, sibling(h_a)), (gp, *gps[:2]))
    down_acc = gradient_start((o_own, o_a, sibling(o_a)), (act, *acts[:2]), True)
    up_blocks = at_owner(up_finish(sc, up_acc, h_2, sibling(h_2), gps[2]), "z")
    down_blocks = at_owner(down_finish(sc, down_acc, o_2, sibling(o_2), acts[2]), "x")

    in_t, gain = input_grad(sc, q0, rd0, q_recv, hidden_t, out_t, gain_row, inv, inv_count)
    gain_grad = total_over(gain[:, 0], ("x", "z"))
    up_grad = add_up(up_blocks, inv_count)
    down_grad = add_up(down_blocks, inv_count).T
    return (jnp.swapaxes(in_t, 1, 2), up_grad, down_grad, gain_grad)


def solution(mesh):
    split = Mesh(mesh.devices.reshape(4, 4, 4, 2), ("x", "z", "y", "c"))
    dp, mp = ("x", "z"), ("y", "c")
    in_specs = (
        P(None, dp, mp),
        P(None, dp, mp),
        P(None, dp),
        P(mp),
        P(None, mp),
        P(mp, None),
    )
    out_specs = (P(None, dp, mp), P(dp, mp), P(mp, dp), P(mp))

    return jax.shard_map(
        on_device, mesh=split, in_specs=in_specs, out_specs=out_specs, check_vma=False
    )
```

time: 173 us -> 166 us (0.960)
  waiting for transfers between devices: 59.6 us -> 69.9 us
  local copies, waits for them, and re-layouts: 18.5 us -> 8.59 us
  starting transfers between devices: 63.4 us -> 53.5 us
  Pallas kernels: 28 us -> 31.2 us
    ppermute x0 -> x13, waiting for transfers between devices: none -> 28.4 us  [led(): return lax.ppermute(value, (axis, 'c'), pairs)]
    ppermute x54 -> x30, starting transfers between devices: 63.4 us -> 41.6 us  [moved(): lax.ppermute(value, axis, [(i, (i + step) % size) for i in range(size)])]
    ppermute x54 -> x30, waiting for transfers between devices: 59.6 us -> 41.5 us  [moved(): lax.ppermute(value, axis, [(i, (i + step) % size) for i in range(size)])]
    ppermute x0 -> x13, starting transfers between devices: none -> 11.9 us  [led(): return lax.ppermute(value, (axis, 'c'), pairs)]
    unnamed x56 -> x27, local copies, waits for them, and re-layouts: 16.9 us -> 7.85 us
    pallas_call x10 -> x12, Pallas kernels: 28 us -> 31.2 us  [call(): pl.pallas_call(body, out_shape=[jax.ShapeDtypeStruct(s, d) for s, d in ou...]
  transfers between devices with their start and end apart: 54 -> 43, of which waited for: 17 -> 17; matrix products, arithmetic and copies ran while one was open for 1% -> 1% of each run, Pallas kernels for 10% -> 12%
where the time goes in v3:
time: 166 us
  waiting for transfers between devices  69.9 us (42%)
  starting transfers between devices  53.5 us (32%)
  Pallas kernels  31.2 us (19%)
  local copies, waits for them, and re-layouts  8.59 us (5%)
  other arithmetic  1.68 us (1%)
    ppermute x30, starting transfers between devices, moved(): lax.ppermute(value, axis, [(i, (i + step) % size) for i in range(size)])  41.6 us
    ppermute x30, waiting for transfers between devices, moved(): lax.ppermute(value, axis, [(i, (i + step) % size) for i in range(size)])  41.5 us
    pallas_call x12, Pallas kernels, call(): pl.pallas_call(body, out_shape=[jax.ShapeDtypeStruct(s, d) for s, d in ou...  31.2 us
    ppermute x13, waiting for transfers between devices, led(): return lax.ppermute(value, (axis, 'c'), pairs)  28.4 us
    ppermute x13, starting transfers between devices, led(): return lax.ppermute(value, (axis, 'c'), pairs)  11.9 us
    unnamed x27, local copies, waits for them, and re-layouts  7.85 us
  transfers between devices with their start and end apart: 43, of which 17 were waited for; matrix products, arithmetic and copies ran while one was open for 1% of the time, Pallas kernels for 12%

profile of v3, /device:TPU:0, one launch (start us, length us, event | category | flops | bytes accessed | tf_op | source)
XLA Modules:
  0.0 165.7 jit_solution(5413875817149590955)
XLA Ops:
  4.6 1.8 %collective-permute-start = (bf16[2,912,128]{2,1,0:T(8,128)(2,1)S(1)}, bf16[2,912,128]{2,1,0:T(8,128)(2,1)S(1)}, u32[]{:S(2)}, u32[]{:S(2)}) collective-permute-start(bf16[2,912,128]{2,1,0:T(8,128)(2,1)S(1)} %get-tuple-element.37.refs_0_), channel_id=1, source_target_pairs={{0,2},{1,7},{2,4},{3,1},{4,6},{5,3},{6,0},{7,5},{8,10},{9,15},{10,... | collective-permute-start | bytes 1400840 | tf_op jit(solution)/shard_map/ppermute | solution.py:31
  6.4 1.5 collective-permute-start.1
  7.9 9.8 %collective-permute-done.refs_1_ = bf16[2,912,128]{2,1,0:T(8,128)(2,1)S(1)} collective-permute-done((bf16[2,912,128]{2,1,0:T(8,128)(2,1)S(1)}, bf16[2,912,128]{2,1,0:T(8,128)(2,1)S(1)}, u32[]{:S(2)}, u32[]{:S(2)}) %collective-permute-start) | collective-permute-done | bytes 466976 | tf_op jit(solution)/shard_map/ppermute | solution.py:31
  17.8 1.9 %collective-permute-start.2 = (bf16[2,912,128]{2,1,0:T(8,128)(2,1)S(1)}, bf16[2,912,128]{2,1,0:T(8,128)(2,1)S(1)}, u32[]{:S(2)}, u32[]{:S(2)}) collective-permute-start(bf16[2,912,128]{2,1,0:T(8,128)(2,1)S(1)} %collective-permute-done.refs_1_), channel_id=1, source_target_pairs={{0,2},{1,7},{2,4},{3,1},{4,6},{5,3},{6,0},{7,5},{8,10},{9,15},{10,... | collective-permute-start | bytes 1400840 | tf_op jit(solution)/shard_map/ppermute | solution.py:31
  20.6 7.0 %collective-permute-done.2.refs_3_ = bf16[2,912,128]{2,1,0:T(8,128)(2,1)S(1)} collective-permute-done((bf16[2,912,128]{2,1,0:T(8,128)(2,1)S(1)}, bf16[2,912,128]{2,1,0:T(8,128)(2,1)S(1)}, u32[]{:S(2)}, u32[]{:S(2)}) %collective-permute-start.2) | collective-permute-done | bytes 466976 | tf_op jit(solution)/shard_map/ppermute | solution.py:31
  28.3 8.0 %shard_map.93 = (bf16[4,896,896]{2,1,0:T(8,128)(2,1)S(1)}, bf16[4,896,896]{2,1,0:T(8,128)(2,1)}) custom-call(s32[8]{0:T(128)S(1)} %concatenate.3.sc, bf16[3584,896]{1,0:T(8,128)(2,1)} %up_ref.1, bf16[896,3584]{1,0:T(8,128)(2,1)} %down_ref.1), custom_call_target="tpu_custom_call" | custom-call | flops 1000000000 | bytes 12845056 | tf_op jit(solution)/shard_map/pallas_call | solution.py:56
  36.3 2.8 %copy-done = bf16[4,896,896]{2,1,0:T(8,128)(2,1)S(1)} copy-done((bf16[4,896,896]{2,1,0:T(8,128)(2,1)S(1)}, bf16[4,896,896]{2,1,0:T(8,128)(2,1)}, u32[]{:S(2)}) %copy-start) | copy-done | bytes 6422552
  39.2 7.3 %shard_map.95 = (bf16[896,256]{1,0:T(8,128)(2,1)}, bf16[896,256]{1,0:T(8,128)(2,1)S(1)}, f32[8,256]{1,0:T(8,128)S(1)}, f32[8,256]{1,0:T(8,128)S(1)}, bf16[896,25...) custom-call(s32[8]{0:T(128)S(1)} %concatenate.3.sc, ...), custom_call_target="tpu_custom_call" | custom-call | flops 3288334336 | bytes 12845056 | tf_op jit(solution)/shard_map/pallas_call | solution.py:56
  46.5 2.6 %shard_map.96 = (f32[4,448,256]{2,1,0:T(8,128)S(1)}, bf16[4,464,256]{2,1,0:T(8,128)(2,1)S(1)}) custom-call(s32[8]{0:T(128)S(1)} %concatenate.3.sc, bf16[4,896,896]{2,1,0:T(8,128)(2,1)S(1)} %get-tuple-element.35.up_ref, bf16[896,256]{1,0:T(8,128)(2,1)S(1)} %get-tuple-element.38.gp_ref.r0, f32[8,256]{1,0:T(8,128)S(1)} %get-tuple-element.39.rd_ref), custom_call_target="tpu_custom_call" | custom-call | flops 1644167168 | bytes 6422528 | tf_op jit(solution)/shard_map/pallas_call | solution.py:56
  49.7 3.2 %collective-permute-start.21 = (bf16[448,256]{1,0:T(8,128)(2,1)S(1)}, bf16[448,256]{1,0:T(8,128)(2,1)S(1)}, u32[]{:S(2)}, u32[]{:S(2)}) collective-permute-start(bf16[448,256]{1,0:T(8,128)(2,1)S(1)} %get-tuple-element.52), channel_id=1, source_target_pairs={{0,64},{32,96},{64,0},{96,32},{1,65},{33,97},{65,1},{97,33},{2,66}... | collective-permute-start | bytes 688136 | tf_op jit(solution)/shard_map/ppermute | solution.py:23
  53.6 3.2 %collective-permute-start.13 = (f32[8,128]{1,0:T(8,128)S(1)}, f32[8,128]{1,0:T(8,128)S(1)}, u32[]{:S(2)}, u32[]{:S(2)}) collective-permute-start(f32[8,128]{1,0:T(8,128)S(1)} %get-tuple-element.48), channel_id=1, source_target_pairs={{0,96},{32,0},{64,32},{96,64},{1,97},{33,1},{65,33},{97,65},{2,98}... | collective-permute-start | bytes 12296 | tf_op jit(solution)/shard_map/ppermute | solution.py:23
  56.8 3.3 %collective-permute-done.13 = f32[8,128]{1,0:T(8,128)S(1)} collective-permute-done((f32[8,128]{1,0:T(8,128)S(1)}, f32[8,128]{1,0:T(8,128)S(1)}, u32[]{:S(2)}, u32[]{:S(2)}) %collective-permute-start.13) | collective-permute-done | bytes 4128 | tf_op jit(solution)/shard_map/ppermute | solution.py:23
  60.1 8.6 %collective-permute-done.12 = f32[8,128]{1,0:T(8,128)S(1)} collective-permute-done((f32[8,128]{1,0:T(8,128)S(1)}, f32[8,128]{1,0:T(8,128)S(1)}, u32[]{:S(2)}, u32[]{:S(2)}) %collective-permute-start.12) | collective-permute-done | bytes 4128 | tf_op jit(solution)/shard_map/ppermute | solution.py:23
  68.7 3.2 %collective-permute-start.11 = (f32[8,128]{1,0:T(8,128)S(1)}, f32[8,128]{1,0:T(8,128)S(1)}, u32[]{:S(2)}, u32[]{:S(2)}) collective-permute-start(f32[8,128]{1,0:T(8,128)S(1)} %get-tuple-element.48), channel_id=1, source_target_pairs={{0,64},{32,96},{64,0},{96,32},{1,65},{33,97},{65,1},{97,33},{2,66}... | collective-permute-start | bytes 12296 | tf_op jit(solution)/shard_map/ppermute | solution.py:23
  71.9 1.4 collective-permute-start.22
  73.8 4.3 %collective-permute-start.16 = (f32[8,128]{1,0:T(8,128)S(1)}, f32[8,128]{1,0:T(8,128)S(1)}, u32[]{:S(2)}, u32[]{:S(2)}) collective-permute-start(f32[8,128]{1,0:T(8,128)S(1)} %add_add_fusion), channel_id=1, source_target_pairs={{0,24},{8,0},{16,8},{24,16},{1,25},{9,1},{17,9},{25,17},{2,26},{10... | collective-permute-start | bytes 12296 | tf_op jit(solution)/shard_map/ppermute | solution.py:23
  78.1 1.3 collective-permute-done.16
  79.5 4.9 %collective-permute-done.15 = f32[8,128]{1,0:T(8,128)S(1)} collective-permute-done((f32[8,128]{1,0:T(8,128)S(1)}, f32[8,128]{1,0:T(8,128)S(1)}, u32[]{:S(2)}, u32[]{:S(2)}) %collective-permute-start.15) | collective-permute-done | bytes 4128 | tf_op jit(solution)/shard_map/ppermute | solution.py:23
  84.5 1.2 collective-permute-start.14
  85.7 3.9 %collective-permute-done.14 = f32[8,128]{1,0:T(8,128)S(1)} collective-permute-done((f32[8,128]{1,0:T(8,128)S(1)}, f32[8,128]{1,0:T(8,128)S(1)}, u32[]{:S(2)}, u32[]{:S(2)}) %collective-permute-start.14) | collective-permute-done | bytes 4128 | tf_op jit(solution)/shard_map/ppermute | solution.py:23
  89.6 1.2 collective-permute-start.29
  90.7 1.5 collective-permute-start.20
  93.0 6.2 %collective-permute-done.27.l1 = bf16[4,224,256]{2,1,0:T(8,128)(2,1)S(1)} collective-permute-done((bf16[4,224,256]{2,1,0:T(8,128)(2,1)S(1)}, bf16[4,224,256]{2,1,0:T(8,128)(2,1)S(1)}, u32[]{:S(2)}, u32[]{:S(2)}) %collective-permute-start.27) | collective-permute-done | bytes 458784 | tf_op jit(solution)/shard_map/ppermute | solution.py:31
  99.3 1.5 collective-permute-start.8
  100.8 3.4 %collective-permute-done.29.r1 = bf16[896,256]{1,0:T(8,128)(2,1)S(1)} collective-permute-done((bf16[896,256]{1,0:T(8,128)(2,1)}, bf16[896,256]{1,0:T(8,128)(2,1)S(1)}, u32[]{:S(2)}, u32[]{:S(2)}) %collective-permute-start.29) | collective-permute-done | bytes 458784 | tf_op jit(solution)/shard_map/ppermute | solution.py:31
  104.6 2.5 %collective-permute-start.10 = (bf16[464,256]{1,0:T(8,128)(2,1)S(1)}, bf16[464,256]{1,0:T(8,128)(2,1)S(1)}, u32[]{:S(2)}, u32[]{:S(2)}) collective-permute-start(bf16[464,256]{1,0:T(8,128)(2,1)S(1)} %get-tuple-element.46), channel_id=1, source_target_pairs={{0,4},{2,6},{4,0},{6,2},{1,5},{3,7},{5,1},{7,3},{8,12},{10,14},{12... | collective-permute-start | bytes 712712 | tf_op jit(solution)/shard_map/ppermute | solution.py:23
  108.0 1.6 shard_map.99.acc_ref
  110.6 2.1 %shard_map.100 = (f32[224,896]{1,0:T(8,128)S(1)}, bf16[224,896]{1,0:T(8,128)(2,1)}, bf16[224,896]{1,0:T(8,128)(2,1)S(1)}, bf16[224,896]{1,0:T(8,128)(2,1)S(1)}) custom-call(s32[8]{0:T(128)S(1)} %concatenate.3.sc, f32[896,896]{1,0:T(8,128)S(1)} %shard_map.99.acc_ref, bf16[448,256]{1,0:T(8,128)(2,1)S(1)} %collective-permute-done.21.m_ref, ...), custom_call_target="tpu_custom_call" | custom-call | flops 411041792 | tf_op jit(solution)/shard_map/pallas_call | solution.py:56
  112.8 1.9 %collective-permute-done.9.r2 = bf16[464,256]{1,0:T(8,128)(2,1)S(1)} collective-permute-done((bf16[464,256]{1,0:T(8,128)(2,1)S(1)}, bf16[464,256]{1,0:T(8,128)(2,1)S(1)}, u32[]{:S(2)}, u32[]{:S(2)}) %collective-permute-start.9) | collective-permute-done | bytes 237600 | tf_op jit(solution)/shard_map/ppermute | solution.py:31
  114.7 1.4 collective-permute-start.24
  116.1 1.5 shard_map.98
  118.4 1.1 reduce
  120.0 1.5 collective-permute-start.39
  122.1 1.5 collective-permute-done.39
  123.6 3.0 %collective-permute-start.37 = (f32[448]{0:T(512)S(1)}, f32[448]{0:T(512)S(1)}, u32[]{:S(2)}, u32[]{:S(2)}) collective-permute-start(f32[448]{0:T(512)S(1)} %reduce), channel_id=1, source_target_pairs={{0,64},{32,96},{64,0},{96,32},{1,65},{33,97},{65,1},{97,33},{2,66}... | collective-permute-start | bytes 5384 | tf_op jit(solution)/shard_map/ppermute | solution.py:23
  126.6 1.0 copy-done.6
  127.6 2.7 %shard_map.102.acc_ref = f32[896,896]{1,0:T(8,128)S(1)} custom-call(bf16[4,224,256]{2,1,0:T(8,128)(2,1)S(1)} %copy-done.6, bf16[4,224,256]{2,1,0:T(8,128)(2,1)S(1)} %collective-permute-done.27.l1, bf16[4,224,256]{2,1,0:T(8,128)(2,1)S(1)} %collective-permute-done.28.l2, bf16[896,256]{1,0:T(8,128)(2,1)} %get-tuple-element.59.r0, ...), custom_call_target="tpu_custom_call" | custom-call | flops 1233125376 | tf_op jit(solution)/shard_map/pallas_call | solution.py:56
  130.3 2.2 %collective-permute-start.25 = (bf16[224,896]{1,0:T(8,128)(2,1)}, bf16[224,896]{1,0:T(8,128)(2,1)S(1)}, u32[]{:S(2)}, u32[]{:S(2)}) collective-permute-start(bf16[224,896]{1,0:T(8,128)(2,1)} %copy-done.12), channel_id=1, source_target_pairs={{0,16},{8,24},{16,0},{24,8},{1,17},{9,25},{17,1},{25,9},{2,18},{10... | collective-permute-start | bytes 1204232 | tf_op jit(solution)/shard_map/ppermute | solution.py:23
  132.6 4.0 %collective-permute-start.42 = (f32[448]{0:T(512)S(1)}, f32[448]{0:T(512)S(1)}, u32[]{:S(2)}, u32[]{:S(2)}) collective-permute-start(f32[448]{0:T(512)S(1)} %add_add_fusion.2), channel_id=1, source_target_pairs={{0,24},{8,0},{16,8},{24,16},{1,25},{9,1},{17,9},{25,17},{2,26},{10... | collective-permute-start | bytes 5384 | tf_op jit(solution)/shard_map/ppermute | solution.py:23
  137.5 2.1 %collective-permute-start.40 = (f32[448]{0:T(512)S(1)}, f32[448]{0:T(512)S(1)}, u32[]{:S(2)}, u32[]{:S(2)}) collective-permute-start(f32[448]{0:T(512)S(1)} %add_add_fusion.2), channel_id=1, source_target_pairs={{0,16},{8,24},{16,0},{24,8},{1,17},{9,25},{17,1},{25,9},{2,18},{10... | collective-permute-start | bytes 5384 | tf_op jit(solution)/shard_map/ppermute | solution.py:23
  139.6 1.9 %shard_map.103 = (f32[224,896]{1,0:T(8,128)S(1)}, bf16[224,896]{1,0:T(8,128)(2,1)S(1)}, bf16[224,896]{1,0:T(8,128)(2,1)S(1)}, bf16[224,896]{1,0:T(8,128)(2,1)S(1)}) custom-call(s32[8]{0:T(128)S(1)} %concatenate.3.sc, f32[896,896]{1,0:T(8,128)S(1)} %shard_map.102.acc_ref, bf16[4,224,128]{2,1,0:T(8,128)(2,1)} %collective-permute-done.31.m_ref, ...), custom_call_target="tpu_custom_call" | custom-call | flops 411041792 | tf_op jit(solution)/shard_map/pallas_call | solution.py:56
  141.5 3.7 %collective-permute-done.42 = f32[448]{0:T(512)S(1)} collective-permute-done((f32[448]{0:T(512)S(1)}, f32[448]{0:T(512)S(1)}, u32[]{:S(2)}, u32[]{:S(2)}) %collective-permute-start.42) | collective-permute-done | bytes 1824 | tf_op jit(solution)/shard_map/ppermute | solution.py:23
  146.1 1.7 %collective-permute-start.35 = (bf16[224,896]{1,0:T(8,128)(2,1)S(1)}, bf16[224,896]{1,0:T(8,128)(2,1)S(1)}, u32[]{:S(2)}, u32[]{:S(2)}) collective-permute-start(bf16[224,896]{1,0:T(8,128)(2,1)S(1)} %get-tuple-element.63), channel_id=1, source_target_pairs={{0,64},{32,96},{64,0},{96,32},{1,65},{33,97},{65,1},{97,33},{2,66}... | collective-permute-start | bytes 1204232 | tf_op jit(solution)/shard_map/ppermute | solution.py:23
  147.8 1.5 collective-permute-start.36
  149.8 4.1 %collective-permute-done.26.r3 = bf16[224,896]{1,0:T(8,128)(2,1)S(1)} collective-permute-done((bf16[224,896]{1,0:T(8,128)(2,1)S(1)}, bf16[224,896]{1,0:T(8,128)(2,1)S(1)}, u32[]{:S(2)}, u32[]{:S(2)}) %collective-permute-start.26) | collective-permute-done | bytes 401440 | tf_op jit(solution)/shard_map/ppermute | solution.py:23
  153.9 1.2 shard_map.101
  155.1 8.6 %collective-permute-done.34.r1 = bf16[224,896]{1,0:T(8,128)(2,1)S(1)} collective-permute-done((bf16[224,896]{1,0:T(8,128)(2,1)S(1)}, bf16[224,896]{1,0:T(8,128)(2,1)S(1)}, u32[]{:S(2)}, u32[]{:S(2)}) %collective-permute-start.34) | collective-permute-done | bytes 401440 | tf_op jit(solution)/shard_map/ppermute | solution.py:23
  164.4 1.2 shard_map.104
  (84 shorter events, 15.4 us)
Async XLA Ops:
  4.6 13.1 %collective-permute-start = (bf16[2,912,128]{2,1,0:T(8,128)(2,1)S(1)}, bf16[2,912,128]{2,1,0:T(8,128)(2,1)S(1)}, u32[]{:S(2)}, u32[]{:S(2)}) collective-permute-start(bf16[2,912,128]{2,1,0:T(8,128)(2,1)S(1)} %get-tuple-element.37.refs_0_), channel_id=1, source_target_pairs={{0,2},{1,7},{2,4},{3,1},{4,6},{5,3},{6,0},{7,5},{8,10},{9,15},{10,... | collective-permute-start | bytes 1400840 | tf_op jit(solution)/shard_map/ppermute | solution.py:31
  6.4 13.8 %collective-permute-start.1 = (bf16[2,912,128]{2,1,0:T(8,128)(2,1)S(1)}, bf16[2,912,128]{2,1,0:T(8,128)(2,1)S(1)}, u32[]{:S(2)}, u32[]{:S(2)}) collective-permute-start(bf16[2,912,128]{2,1,0:T(8,128)(2,1)S(1)} %get-tuple-element.37.refs_0_), channel_id=1, source_target_pairs={{0,6},{1,3},{2,0},{3,5},{4,2},{5,7},{6,4},{7,1},{8,14},{9,11},{10,... | collective-permute-start | bytes 1400840 | tf_op jit(solution)/shard_map/ppermute | solution.py:31
  17.8 9.8 %collective-permute-start.2 = (bf16[2,912,128]{2,1,0:T(8,128)(2,1)S(1)}, bf16[2,912,128]{2,1,0:T(8,128)(2,1)S(1)}, u32[]{:S(2)}, u32[]{:S(2)}) collective-permute-start(bf16[2,912,128]{2,1,0:T(8,128)(2,1)S(1)} %collective-permute-done.refs_1_), channel_id=1, source_target_pairs={{0,2},{1,7},{2,4},{3,1},{4,6},{5,3},{6,0},{7,5},{8,10},{9,15},{10,... | collective-permute-start | bytes 1400840 | tf_op jit(solution)/shard_map/ppermute | solution.py:31
  19.6 16.7 %collective-permute-start.3 = (bf16[2,912,128]{2,1,0:T(8,128)(2,1)S(1)}, bf16[2,912,128]{2,1,0:T(8,128)(2,1)S(1)}, u32[]{:S(2)}, u32[]{:S(2)}) collective-permute-start(bf16[2,912,128]{2,1,0:T(8,128)(2,1)S(1)} %get-tuple-element.37.refs_0_), channel_id=1, source_target_pairs={{0,1},{1,0},{2,3},{3,2},{4,5},{5,4},{6,7},{7,6},{8,9},{9,8},{10,11... | collective-permute-start | bytes 1400840 | tf_op jit(solution)/shard_map/ppermute | solution.py:23
  20.0 16.3 %collective-permute-start.4 = (bf16[2,912,128]{2,1,0:T(8,128)(2,1)S(1)}, bf16[2,912,128]{2,1,0:T(8,128)(2,1)S(1)}, u32[]{:S(2)}, u32[]{:S(2)}) collective-permute-start(bf16[2,912,128]{2,1,0:T(8,128)(2,1)S(1)} %collective-permute-done.refs_1_), channel_id=1, source_target_pairs={{0,1},{1,0},{2,3},{3,2},{4,5},{5,4},{6,7},{7,6},{8,9},{9,8},{10,11... | collective-permute-start | bytes 1400840 | tf_op jit(solution)/shard_map/ppermute | solution.py:23
  20.2 16.2 %collective-permute-start.5 = (bf16[2,912,128]{2,1,0:T(8,128)(2,1)S(1)}, bf16[2,912,128]{2,1,0:T(8,128)(2,1)S(1)}, u32[]{:S(2)}, u32[]{:S(2)}) collective-permute-start(bf16[2,912,128]{2,1,0:T(8,128)(2,1)S(1)} %collective-permute-done.1.refs_2_), channel_id=1, source_target_pairs={{0,1},{1,0},{2,3},{3,2},{4,5},{5,4},{6,7},{7,6},{8,9},{9,8},{10,11... | collective-permute-start | bytes 1400840 | tf_op jit(solution)/shard_map/ppermute | solution.py:23
  27.5 8.8 %collective-permute-start.6 = (bf16[2,912,128]{2,1,0:T(8,128)(2,1)S(1)}, bf16[2,912,128]{2,1,0:T(8,128)(2,1)}, u32[]{:S(2)}, u32[]{:S(2)}) collective-permute-start(bf16[2,912,128]{2,1,0:T(8,128)(2,1)S(1)} %collective-permute-done.2.refs_3_), channel_id=1, source_target_pairs={{0,1},{1,0},{2,3},{3,2},{4,5},{5,4},{6,7},{7,6},{8,9},{9,8},{10,11... | collective-permute-start | bytes 1400840 | tf_op jit(solution)/shard_map/ppermute | solution.py:23
  46.5 63.2 %copy-start.5 = (bf16[4,224,256]{2,1,0:T(8,128)(2,1)}, bf16[4,224,256]{2,1,0:T(8,128)(2,1)S(1)}, u32[]{:S(2)}) copy-start(bf16[4,224,256]{2,1,0:T(8,128)(2,1)S(1)} %get-tuple-element.57.l0) | copy-start | bytes 1376260
  49.1 43.1 %collective-permute-start.7 = (bf16[4,464,256]{2,1,0:T(8,128)(2,1)S(1)}, bf16[4,464,256]{2,1,0:T(8,128)(2,1)S(1)}, u32[]{:S(2)}, u32[]{:S(2)}) collective-permute-start(bf16[4,464,256]{2,1,0:T(8,128)(2,1)S(1)} %get-tuple-element.41), channel_id=1, source_target_pairs={{0,1},{1,0},{2,3},{3,2},{4,5},{5,4},{6,7},{7,6},{8,9},{9,8},{10,11... | collective-permute-start | bytes 2850824 | tf_op jit(solution)/shard_map/ppermute | solution.py:23
  49.7 22.2 %collective-permute-start.21 = (bf16[448,256]{1,0:T(8,128)(2,1)S(1)}, bf16[448,256]{1,0:T(8,128)(2,1)S(1)}, u32[]{:S(2)}, u32[]{:S(2)}) collective-permute-start(bf16[448,256]{1,0:T(8,128)(2,1)S(1)} %get-tuple-element.52), channel_id=1, source_target_pairs={{0,64},{32,96},{64,0},{96,32},{1,65},{33,97},{65,1},{97,33},{2,66}... | collective-permute-start | bytes 688136 | tf_op jit(solution)/shard_map/ppermute | solution.py:23
  52.9 37.8 %collective-permute-start.17 = (bf16[896,256]{1,0:T(8,128)(2,1)S(1)}, bf16[896,256]{1,0:T(8,128)(2,1)S(1)}, u32[]{:S(2)}, u32[]{:S(2)}) collective-permute-start(bf16[896,256]{1,0:T(8,128)(2,1)S(1)} %get-tuple-element.51), channel_id=1, source_target_pairs={{0,32},{1,97},{32,64},{33,1},{64,96},{65,33},{96,0},{97,65},{2,34}... | collective-permute-start | bytes 1376264 | tf_op jit(solution)/shard_map/ppermute | solution.py:31
  53.5 38.7 %collective-permute-start.19 = (bf16[896,256]{1,0:T(8,128)(2,1)S(1)}, bf16[896,256]{1,0:T(8,128)(2,1)S(1)}, u32[]{:S(2)}, u32[]{:S(2)}) collective-permute-start(bf16[896,256]{1,0:T(8,128)(2,1)S(1)} %get-tuple-element.38.gp_ref.r0), channel_id=1, source_target_pairs={{0,32},{1,97},{32,64},{33,1},{64,96},{65,33},{96,0},{97,65},{2,34}... | collective-permute-start | bytes 1376264 | tf_op jit(solution)/shard_map/ppermute | solution.py:31
  53.6 6.6 %collective-permute-start.13 = (f32[8,128]{1,0:T(8,128)S(1)}, f32[8,128]{1,0:T(8,128)S(1)}, u32[]{:S(2)}, u32[]{:S(2)}) collective-permute-start(f32[8,128]{1,0:T(8,128)S(1)} %get-tuple-element.48), channel_id=1, source_target_pairs={{0,96},{32,0},{64,32},{96,64},{1,97},{33,1},{65,33},{97,65},{2,98}... | collective-permute-start | bytes 12296 | tf_op jit(solution)/shard_map/ppermute | solution.py:23
  60.1 8.6 %collective-permute-start.12 = (f32[8,128]{1,0:T(8,128)S(1)}, f32[8,128]{1,0:T(8,128)S(1)}, u32[]{:S(2)}, u32[]{:S(2)}) collective-permute-start(f32[8,128]{1,0:T(8,128)S(1)} %get-tuple-element.48), channel_id=1, source_target_pairs={{0,32},{32,64},{64,96},{96,0},{1,33},{33,65},{65,97},{97,1},{2,34}... | collective-permute-start | bytes 12296 | tf_op jit(solution)/shard_map/ppermute | solution.py:23
  68.7 5.1 %collective-permute-start.11 = (f32[8,128]{1,0:T(8,128)S(1)}, f32[8,128]{1,0:T(8,128)S(1)}, u32[]{:S(2)}, u32[]{:S(2)}) collective-permute-start(f32[8,128]{1,0:T(8,128)S(1)} %get-tuple-element.48), channel_id=1, source_target_pairs={{0,64},{32,96},{64,0},{96,32},{1,65},{33,97},{65,1},{97,33},{2,66}... | collective-permute-start | bytes 12296 | tf_op jit(solution)/shard_map/ppermute | solution.py:23
  71.9 17.6 %collective-permute-start.22 = (bf16[448,256]{1,0:T(8,128)(2,1)S(1)}, bf16[448,256]{1,0:T(8,128)(2,1)S(1)}, u32[]{:S(2)}, u32[]{:S(2)}) collective-permute-start(bf16[448,256]{1,0:T(8,128)(2,1)S(1)} %collective-permute-done.21.m_ref), channel_id=1, source_target_pairs={{0,1},{1,0},{2,3},{3,2},{4,5},{5,4},{6,7},{7,6},{8,9},{9,8},{10,11... | collective-permute-start | bytes 688136 | tf_op jit(solution)/shard_map/ppermute | solution.py:23
  73.8 5.6 %collective-permute-start.16 = (f32[8,128]{1,0:T(8,128)S(1)}, f32[8,128]{1,0:T(8,128)S(1)}, u32[]{:S(2)}, u32[]{:S(2)}) collective-permute-start(f32[8,128]{1,0:T(8,128)S(1)} %add_add_fusion), channel_id=1, source_target_pairs={{0,24},{8,0},{16,8},{24,16},{1,25},{9,1},{17,9},{25,17},{2,26},{10... | collective-permute-start | bytes 12296 | tf_op jit(solution)/shard_map/ppermute | solution.py:23
  79.4 5.1 %collective-permute-start.15 = (f32[8,128]{1,0:T(8,128)S(1)}, f32[8,128]{1,0:T(8,128)S(1)}, u32[]{:S(2)}, u32[]{:S(2)}) collective-permute-start(f32[8,128]{1,0:T(8,128)S(1)} %add_add_fusion), channel_id=1, source_target_pairs={{0,8},{8,16},{16,24},{24,0},{1,9},{9,17},{17,25},{25,1},{2,10},{10... | collective-permute-start | bytes 12296 | tf_op jit(solution)/shard_map/ppermute | solution.py:23
  84.5 5.1 %collective-permute-start.14 = (f32[8,128]{1,0:T(8,128)S(1)}, f32[8,128]{1,0:T(8,128)S(1)}, u32[]{:S(2)}, u32[]{:S(2)}) collective-permute-start(f32[8,128]{1,0:T(8,128)S(1)} %add_add_fusion), channel_id=1, source_target_pairs={{0,16},{8,24},{16,0},{24,8},{1,17},{9,25},{17,1},{25,9},{2,18},{10... | collective-permute-start | bytes 12296 | tf_op jit(solution)/shard_map/ppermute | solution.py:23
  89.6 9.7 %collective-permute-start.27 = (bf16[4,224,256]{2,1,0:T(8,128)(2,1)S(1)}, bf16[4,224,256]{2,1,0:T(8,128)(2,1)S(1)}, u32[]{:S(2)}, u32[]{:S(2)}) collective-permute-start(bf16[4,224,256]{2,1,0:T(8,128)(2,1)S(1)} %get-tuple-element.58), channel_id=1, source_target_pairs={{0,8},{1,25},{8,16},{9,1},{16,24},{17,9},{24,0},{25,17},{2,10},{3,... | collective-permute-start | bytes 1376264 | tf_op jit(solution)/shard_map/ppermute | solution.py:31
  89.6 14.6 %collective-permute-start.29 = (bf16[896,256]{1,0:T(8,128)(2,1)}, bf16[896,256]{1,0:T(8,128)(2,1)S(1)}, u32[]{:S(2)}, u32[]{:S(2)}) collective-permute-start(bf16[896,256]{1,0:T(8,128)(2,1)} %get-tuple-element.59.r0), channel_id=1, source_target_pairs={{0,8},{1,25},{8,16},{9,1},{16,24},{17,9},{24,0},{25,17},{2,10},{3,... | collective-permute-start | bytes 1376264 | tf_op jit(solution)/shard_map/ppermute | solution.py:31
  90.7 13.9 %collective-permute-start.20 = (bf16[896,256]{1,0:T(8,128)(2,1)S(1)}, bf16[896,256]{1,0:T(8,128)(2,1)S(1)}, u32[]{:S(2)}, u32[]{:S(2)}) collective-permute-start(bf16[896,256]{1,0:T(8,128)(2,1)S(1)} %get-tuple-element.38.gp_ref.r0), channel_id=1, source_target_pairs={{0,96},{1,33},{32,0},{33,65},{64,32},{65,97},{96,64},{97,1},{2,98}... | collective-permute-start | bytes 1376264 | tf_op jit(solution)/shard_map/ppermute | solution.py:31
  92.2 15.0 %collective-permute-start.18 = (bf16[896,256]{1,0:T(8,128)(2,1)S(1)}, bf16[896,256]{1,0:T(8,128)(2,1)S(1)}, u32[]{:S(2)}, u32[]{:S(2)}) collective-permute-start(bf16[896,256]{1,0:T(8,128)(2,1)S(1)} %collective-permute-done.17.l1), channel_id=1, source_target_pairs={{0,1},{1,0},{2,3},{3,2},{4,5},{5,4},{6,7},{7,6},{8,9},{9,8},{10,11... | collective-permute-start | bytes 1376264 | tf_op jit(solution)/shard_map/ppermute | solution.py:23
  92.2 15.8 %collective-permute-start.23 = (bf16[896,256]{1,0:T(8,128)(2,1)S(1)}, bf16[896,256]{1,0:T(8,128)(2,1)S(1)}, u32[]{:S(2)}, u32[]{:S(2)}) collective-permute-start(bf16[896,256]{1,0:T(8,128)(2,1)S(1)} %collective-permute-done.19.r1), channel_id=1, source_target_pairs={{0,32},{1,97},{32,64},{33,1},{64,96},{65,33},{96,0},{97,65},{2,34}... | collective-permute-start | bytes 1376264 | tf_op jit(solution)/shard_map/ppermute | solution.py:31
  92.9 23.3 %copy-start.2 = (bf16[2,128,448]{1,2,0:T(8,128)(2,1)S(1)}, bf16[2,128,448]{1,2,0:T(8,128)(2,1)}, u32[]{:S(2)}) copy-start(bf16[2,128,448]{1,2,0:T(8,128)(2,1)} %param.6) | copy-start | bytes 688132
  92.9 23.3 %copy-start.4 = (bf16[2,128,448]{1,2,0:T(8,128)(2,1)S(1)}, bf16[2,128,448]{1,2,0:T(8,128)(2,1)}, u32[]{:S(2)}) copy-start(bf16[2,128,448]{1,2,0:T(8,128)(2,1)} %param.7) | copy-start | bytes 688132
  92.9 23.3 %copy-start.9 = (f32[448]{0:T(512)S(1)}, f32[448]{0:T(512)}, u32[]{:S(2)}) copy-start(f32[448]{0:T(512)} %param.9) | copy-start | bytes 5380
  99.3 10.4 %collective-permute-start.8 = (bf16[464,256]{1,0:T(8,128)(2,1)S(1)}, bf16[464,256]{1,0:T(8,128)(2,1)S(1)}, u32[]{:S(2)}, u32[]{:S(2)}) collective-permute-start(bf16[464,256]{1,0:T(8,128)(2,1)S(1)} %get-tuple-element.44), channel_id=1, source_target_pairs={{0,6},{1,3},{2,0},{3,5},{4,2},{5,7},{6,4},{7,1},{8,14},{9,11},{10,... | collective-permute-start | bytes 712712 | tf_op jit(solution)/shard_map/ppermute | solution.py:31
  104.2 10.5 %collective-permute-start.9 = (bf16[464,256]{1,0:T(8,128)(2,1)S(1)}, bf16[464,256]{1,0:T(8,128)(2,1)S(1)}, u32[]{:S(2)}, u32[]{:S(2)}) collective-permute-start(bf16[464,256]{1,0:T(8,128)(2,1)S(1)} %get-tuple-element.45), channel_id=1, source_target_pairs={{0,2},{1,7},{2,4},{3,1},{4,6},{5,3},{6,0},{7,5},{8,10},{9,15},{10,... | collective-permute-start | bytes 712712 | tf_op jit(solution)/shard_map/ppermute | solution.py:31
  104.6 10.1 %collective-permute-start.10 = (bf16[464,256]{1,0:T(8,128)(2,1)S(1)}, bf16[464,256]{1,0:T(8,128)(2,1)S(1)}, u32[]{:S(2)}, u32[]{:S(2)}) collective-permute-start(bf16[464,256]{1,0:T(8,128)(2,1)S(1)} %get-tuple-element.46), channel_id=1, source_target_pairs={{0,4},{2,6},{4,0},{6,2},{1,5},{3,7},{5,1},{7,3},{8,12},{10,14},{12... | collective-permute-start | bytes 712712 | tf_op jit(solution)/shard_map/ppermute | solution.py:23
  107.2 14.3 %collective-permute-start.30 = (bf16[896,256]{1,0:T(8,128)(2,1)}, bf16[896,256]{1,0:T(8,128)(2,1)S(1)}, u32[]{:S(2)}, u32[]{:S(2)}) collective-permute-start(bf16[896,256]{1,0:T(8,128)(2,1)} %get-tuple-element.59.r0), channel_id=1, source_target_pairs={{0,24},{1,9},{8,0},{9,17},{16,8},{17,25},{24,16},{25,1},{2,26},{3,... | collective-permute-start | bytes 1376264 | tf_op jit(solution)/shard_map/ppermute | solution.py:31
  108.0 13.5 %collective-permute-start.28 = (bf16[4,224,256]{2,1,0:T(8,128)(2,1)S(1)}, bf16[4,224,256]{2,1,0:T(8,128)(2,1)S(1)}, u32[]{:S(2)}, u32[]{:S(2)}) collective-permute-start(bf16[4,224,256]{2,1,0:T(8,128)(2,1)S(1)} %collective-permute-done.27.l1), channel_id=1, source_target_pairs={{0,1},{1,0},{2,3},{3,2},{4,5},{5,4},{6,7},{7,6},{8,9},{9,8},{10,11... | collective-permute-start | bytes 1376264 | tf_op jit(solution)/shard_map/ppermute | solution.py:23
  109.6 10.4 %collective-permute-start.31 = (bf16[4,224,128]{2,1,0:T(8,128)(2,1)}, bf16[4,224,128]{2,1,0:T(8,128)(2,1)}, u32[]{:S(2)}, u32[]{:S(2)}) collective-permute-start(bf16[4,224,128]{2,1,0:T(8,128)(2,1)} %get-tuple-element.60), channel_id=1, source_target_pairs={{0,16},{8,24},{16,0},{24,8},{1,17},{9,25},{17,1},{25,9},{2,18},{10... | collective-permute-start | bytes 688136 | tf_op jit(solution)/shard_map/ppermute | solution.py:23
  114.7 22.8 %collective-permute-start.33 = (bf16[896,256]{1,0:T(8,128)(2,1)S(1)}, bf16[896,256]{1,0:T(8,128)(2,1)S(1)}, u32[]{:S(2)}, u32[]{:S(2)}) collective-permute-start(bf16[896,256]{1,0:T(8,128)(2,1)S(1)} %collective-permute-done.29.r1), channel_id=1, source_target_pairs={{0,8},{1,25},{8,16},{9,1},{16,24},{17,9},{24,0},{25,17},{2,10},{3,... | collective-permute-start | bytes 1376264 | tf_op jit(solution)/shard_map/ppermute | solution.py:31
  114.7 33.1 %collective-permute-start.24 = (bf16[224,896]{1,0:T(8,128)(2,1)}, bf16[224,896]{1,0:T(8,128)(2,1)S(1)}, u32[]{:S(2)}, u32[]{:S(2)}) collective-permute-start(bf16[224,896]{1,0:T(8,128)(2,1)} %get-tuple-element.54), channel_id=1, source_target_pairs={{0,8},{8,16},{16,24},{24,0},{1,9},{9,17},{17,25},{25,1},{2,10},{10... | collective-permute-start | bytes 1204232 | tf_op jit(solution)/shard_map/ppermute | solution.py:23
  120.0 3.6 %collective-permute-start.39 = (f32[448]{0:T(512)S(1)}, f32[448]{0:T(512)S(1)}, u32[]{:S(2)}, u32[]{:S(2)}) collective-permute-start(f32[448]{0:T(512)S(1)} %reduce), channel_id=1, source_target_pairs={{0,96},{32,0},{64,32},{96,64},{1,97},{33,1},{65,33},{97,65},{2,98}... | collective-permute-start | bytes 5384 | tf_op jit(solution)/shard_map/ppermute | solution.py:23
  121.5 15.1 %collective-permute-start.32 = (bf16[4,224,128]{2,1,0:T(8,128)(2,1)}, bf16[4,224,128]{2,1,0:T(8,128)(2,1)S(1)}, u32[]{:S(2)}, u32[]{:S(2)}) collective-permute-start(bf16[4,224,128]{2,1,0:T(8,128)(2,1)} %collective-permute-done.31.m_ref), channel_id=1, source_target_pairs={{0,1},{1,0},{2,3},{3,2},{4,5},{5,4},{6,7},{7,6},{8,9},{9,8},{10,11... | collective-permute-start | bytes 688136 | tf_op jit(solution)/shard_map/ppermute | solution.py:23
  121.5 8.9 %collective-permute-start.38 = (f32[448]{0:T(512)S(1)}, f32[448]{0:T(512)S(1)}, u32[]{:S(2)}, u32[]{:S(2)}) collective-permute-start(f32[448]{0:T(512)S(1)} %reduce), channel_id=1, source_target_pairs={{0,32},{32,64},{64,96},{96,0},{1,33},{33,65},{65,97},{97,1},{2,34}... | collective-permute-start | bytes 5384 | tf_op jit(solution)/shard_map/ppermute | solution.py:23
  123.6 9.0 %collective-permute-start.37 = (f32[448]{0:T(512)S(1)}, f32[448]{0:T(512)S(1)}, u32[]{:S(2)}, u32[]{:S(2)}) collective-permute-start(f32[448]{0:T(512)S(1)} %reduce), channel_id=1, source_target_pairs={{0,64},{32,96},{64,0},{96,32},{1,65},{33,97},{65,1},{97,33},{2,66}... | collective-permute-start | bytes 5384 | tf_op jit(solution)/shard_map/ppermute | solution.py:23
  127.6 17.5 %copy-start.11 = (bf16[224,896]{1,0:T(8,128)(2,1)S(1)}, bf16[224,896]{1,0:T(8,128)(2,1)}, u32[]{:S(2)}) copy-start(bf16[224,896]{1,0:T(8,128)(2,1)} %copy-done.10) | copy-start | bytes 1204228
  130.3 19.5 %collective-permute-start.25 = (bf16[224,896]{1,0:T(8,128)(2,1)}, bf16[224,896]{1,0:T(8,128)(2,1)S(1)}, u32[]{:S(2)}, u32[]{:S(2)}) collective-permute-start(bf16[224,896]{1,0:T(8,128)(2,1)} %copy-done.12), channel_id=1, source_target_pairs={{0,16},{8,24},{16,0},{24,8},{1,17},{9,25},{17,1},{25,9},{2,18},{10... | collective-permute-start | bytes 1204232 | tf_op jit(solution)/shard_map/ppermute | solution.py:23
  132.6 12.6 %collective-permute-start.42 = (f32[448]{0:T(512)S(1)}, f32[448]{0:T(512)S(1)}, u32[]{:S(2)}, u32[]{:S(2)}) collective-permute-start(f32[448]{0:T(512)S(1)} %add_add_fusion.2), channel_id=1, source_target_pairs={{0,24},{8,0},{16,8},{24,16},{1,25},{9,1},{17,9},{25,17},{2,26},{10... | collective-permute-start | bytes 5384 | tf_op jit(solution)/shard_map/ppermute | solution.py:23
  136.6 8.6 %collective-permute-start.41 = (f32[448]{0:T(512)S(1)}, f32[448]{0:T(512)S(1)}, u32[]{:S(2)}, u32[]{:S(2)}) collective-permute-start(f32[448]{0:T(512)S(1)} %add_add_fusion.2), channel_id=1, source_target_pairs={{0,8},{8,16},{16,24},{24,0},{1,9},{9,17},{17,25},{25,1},{2,10},{10... | collective-permute-start | bytes 5384 | tf_op jit(solution)/shard_map/ppermute | solution.py:23
  137.5 8.6 %collective-permute-start.40 = (f32[448]{0:T(512)S(1)}, f32[448]{0:T(512)S(1)}, u32[]{:S(2)}, u32[]{:S(2)}) collective-permute-start(f32[448]{0:T(512)S(1)} %add_add_fusion.2), channel_id=1, source_target_pairs={{0,16},{8,24},{16,0},{24,8},{1,17},{9,25},{17,1},{25,9},{2,18},{10... | collective-permute-start | bytes 5384 | tf_op jit(solution)/shard_map/ppermute | solution.py:23
  145.2 8.7 %collective-permute-start.26 = (bf16[224,896]{1,0:T(8,128)(2,1)S(1)}, bf16[224,896]{1,0:T(8,128)(2,1)S(1)}, u32[]{:S(2)}, u32[]{:S(2)}) collective-permute-start(bf16[224,896]{1,0:T(8,128)(2,1)S(1)} %copy-done.11), channel_id=1, source_target_pairs={{0,24},{8,0},{16,8},{24,16},{1,25},{9,1},{17,9},{25,17},{2,26},{10... | collective-permute-start | bytes 1204232 | tf_op jit(solution)/shard_map/ppermute | solution.py:23
  145.2 18.6 %collective-permute-start.34 = (bf16[224,896]{1,0:T(8,128)(2,1)S(1)}, bf16[224,896]{1,0:T(8,128)(2,1)S(1)}, u32[]{:S(2)}, u32[]{:S(2)}) collective-permute-start(bf16[224,896]{1,0:T(8,128)(2,1)S(1)} %get-tuple-element.62), channel_id=1, source_target_pairs={{0,32},{32,64},{64,96},{96,0},{1,33},{33,65},{65,97},{97,1},{2,34}... | collective-permute-start | bytes 1204232 | tf_op jit(solution)/shard_map/ppermute | solution.py:23
  146.1 17.7 %collective-permute-start.35 = (bf16[224,896]{1,0:T(8,128)(2,1)S(1)}, bf16[224,896]{1,0:T(8,128)(2,1)S(1)}, u32[]{:S(2)}, u32[]{:S(2)}) collective-permute-start(bf16[224,896]{1,0:T(8,128)(2,1)S(1)} %get-tuple-element.63), channel_id=1, source_target_pairs={{0,64},{32,96},{64,0},{96,32},{1,65},{33,97},{65,1},{97,33},{2,66}... | collective-permute-start | bytes 1204232 | tf_op jit(solution)/shard_map/ppermute | solution.py:23
  147.8 16.6 %collective-permute-start.36 = (bf16[224,896]{1,0:T(8,128)(2,1)S(1)}, bf16[224,896]{1,0:T(8,128)(2,1)S(1)}, u32[]{:S(2)}, u32[]{:S(2)}) collective-permute-start(bf16[224,896]{1,0:T(8,128)(2,1)S(1)} %get-tuple-element.64), channel_id=1, source_target_pairs={{0,96},{32,0},{64,32},{96,64},{1,97},{33,1},{65,33},{97,65},{2,98}... | collective-permute-start | bytes 1204232 | tf_op jit(solution)/shard_map/ppermute | solution.py:23
  (8 other events, 17.0 us)

commit v4 on v3

--- a/solution.py
+++ b/solution.py
@@ -10,7 +10,7 @@
 MIB = 1024 * 1024
 EPS = 1e-06
 EXTRA = 16
-STAGE_LIMIT = 44
+STAGE_LIMIT = 41
 GELU_A = 0.7978845608028654
 GELU_B = 0.044715
 
@@ -31,9 +31,9 @@
     return lax.ppermute(value, (axis, "c"), pairs)
 
 
-def gathered(value, axis):
-    behind = led(value, axis, 1)
-    ahead = led(value, axis, -1)
+def gathered(forward, back, axis):
+    behind = led(forward, axis, 1)
+    ahead = led(back, axis, -1)
     return behind, ahead, led(behind, axis, 1)
 
 
@@ -110,24 +110,28 @@
     return jnp.where(delta == 0, 0, jnp.where(delta == 2, 3, jnp.where((delta == 3) == (c == 0), 1, 2)))
 
 
-def prepare(fill, hidden_t, out_t, gain):
+def prepare(hidden_t, out_t, gain):
     micro, width, tok = hidden_t.shape
     body_rows = width + EXTRA
 
-    def body(fill_ref, h_ref, o_ref, g_ref, out_ref, count_ref):
+    def body(h_ref, o_ref, g_ref, out_ref):
         g = gain_columns(g_ref, tok)
         for m in range(micro):
             h = h_ref[m].astype(F32)
             out_ref[m, :width, :] = (h * g).astype(BF16)
             out_ref[m, width:body_rows, :] = extra_rows(jnp.sum(h * h, axis=0, keepdims=True))
             out_ref[m, body_rows:, :] = o_ref[m]
-        count_ref[...] = jnp.full(count_ref.shape, (fill_ref[0, 0] + fill_ref[1, 0]).astype(F32))
-
-    return call(
-        body,
-        [((micro, body_rows + width, tok), BF16), ((8, 128), F32)],
-        [(fill, S), (hidden_t, V), (out_t, V), (gain, V)],
-    )
+
+    return call(
+        body, [((micro, body_rows + width, tok), BF16)], [(hidden_t, V), (out_t, V), (gain, V)]
+    )[0]
+
+
+def own_count(sc):
+    def body(sc, count_ref):
+        count_ref[...] = jnp.full(count_ref.shape, (sc[4] + sc[5]).astype(F32))
+
+    return call(body, [((8, 128), F32)], [(sc, S)])[0]
 
 
 def stage_weights(sc, up, down):
@@ -174,7 +178,7 @@
 
     def body(sc, up_ref, down_ref, *refs):
         r, t = refs[0:4], refs[4:8]
-        act_ref, gp_ref, inv_ref, rd_ref, hown, ha, h2, oown, oa, o2, hbuf, obuf = refs[8:]
+        a1, a2, g1, g2, inv_ref, rd_ref, hown, ha, oown, oa, hbuf, obuf = refs[8:]
         x, y, z, c = sc[0], sc[1], sc[2], sc[3]
         s = 1 - 2 * c
         mine = pl.multiple_of(c * width, width)
@@ -195,14 +199,16 @@
         inv_ref[...] = jnp.broadcast_to(inv, inv_ref.shape)
         hown[...] = hbuf[listed(x, y, c)]
         ha[...] = hbuf[listed(x + s, y, c)]
-        h2[...] = hbuf[listed(x + 2, y, c), pl.ds(mine, width), :]
-        for ref, place in ((oown, z), (oa, z + s), (o2, z + 2)):
+        g1[ff:, :] = hbuf[listed(x + 2, y, c), pl.ds(mine, width), :]
+        for ref, place in ((oown, z), (oa, z + s)):
             row = pl.multiple_of(((place + 4) % 4) * quarter, quarter)
             for j in range(4):
-                block = obuf[j, pl.ds(row, quarter), :]
-                if ref is o2:
-                    block = jnp.where(c == 0, block[:, :tok], block[:, tok:])
-                ref[j] = block
+                ref[j] = obuf[j, pl.ds(row, quarter), :]
+        row = pl.multiple_of(((z + 2) % 4) * quarter, quarter)
+        for i, (j0, j1) in enumerate(((0, 1), (3, 2))):
+            a1[ff + i * quarter : ff + (i + 1) * quarter, :] = obuf[
+                jnp.where(c == 0, j0, j1), pl.ds(row, quarter), :
+            ]
         acc = dot(hbuf[0].T, up_ref[0], ((1,), (0,)))
         for k in range(1, 4):
             acc = acc + dot(hbuf[k].T, up_ref[k], ((1,), (0,)))
@@ -210,29 +216,32 @@
         live = live_row(sc, tok)
         cube = GELU_B * pre * pre
         th = jnp.tanh(GELU_A * (pre + cube * pre))
-        act_ref[...] = (0.5 * pre * (1.0 + th) * live).astype(BF16)
+        act = (0.5 * pre * (1.0 + th) * live).astype(BF16)
+        a1[:ff, :] = act
+        a2[...] = act
         slope = 0.5 * (1.0 + th) + 0.5 * pre * (1.0 - th * th) * (GELU_A * (1.0 + 3.0 * cube))
         acc = dot(down_ref[0], obuf[0], ((1,), (0,)))
         for k in range(1, 4):
             acc = acc + dot(down_ref[k], obuf[k], ((1,), (0,)))
         gp = (acc * slope * (inv * live)).astype(BF16)
-        gp_ref[...] = gp
+        g1[:ff, :] = gp
+        g2[...] = gp
         rd = jnp.sum(gp.astype(F32) * pre, axis=0, keepdims=True)
         rd_ref[...] = jnp.broadcast_to(rd, rd_ref.shape)
 
     return call(
         body,
         [
+            ((ff + width, cols), BF16),
             ((ff, cols), BF16),
+            ((ff + width, cols), BF16),
             ((ff, cols), BF16),
             ((8, cols), F32),
             ((8, cols), F32),
             ((pair, cols), BF16),
             ((pair, cols), BF16),
-            ((width, cols), BF16),
             ((4, quarter, cols), BF16),
             ((4, quarter, cols), BF16),
-            ((4, quarter, tok), BF16),
         ],
         [(sc, S), (upv, V), (downv, V)] + [(a, V) for a in (*own, *other)],
         [pltpu.VMEM((4, pair, cols), BF16), pltpu.VMEM((4, pair, cols), BF16)],
@@ -309,24 +318,24 @@
             rest = g * grad[:, cut] - h * factor[:, cut]
             out_ref[m] = (scaled + rest * ic).astype(BF16)
             total = total + grad[:, cut] * h
-        gain_ref[...] = jnp.sum(total, axis=1, keepdims=True) * ic[:, :1]
-
-    return call(
-        body,
-        [((micro, width, tok), BF16), ((width, 1), F32)],
+        row = jnp.sum(total.T, axis=0, keepdims=True) * ic[:, :1]
+        gain_ref[...] = jnp.broadcast_to(row, gain_ref.shape)
+
+    return call(
+        body,
+        [((micro, width, tok), BF16), ((8, width), F32)],
         [(sc, S)] + [(a, V) for a in (q0, rd0, *recv, hidden_t, out_t, gain, inv, inv_count)],
     )
 
 
 def gradient_start(lefts, rights, micro_rows=False):
     rows = lefts[0].shape[0] * (lefts[0].shape[1] if micro_rows else 1)
-    cols = rights[0].shape[1]
-    ff = rights[0].shape[0]
+    ff, cols = rights[0].shape
 
     def body(l0, l1, l2, r0, r1, r2, acc_ref, lbuf, rbuf):
         for k, (left, right) in enumerate(((l0, r0), (l1, r1), (l2, r2))):
             cut = slice(k * cols, (k + 1) * cols)
-            rbuf[:, cut] = right[...]
+            rbuf[:, cut] = right[:ff, :]
             if micro_rows:
                 size = left.shape[1]
                 for j in range(4):
@@ -345,42 +354,47 @@
     )[0]
 
 
-def up_finish(sc, acc, mine, its, gp):
-    width, cols = mine.shape
-    ff = gp.shape[0]
+def up_finish(sc, acc, mine, its, gain):
+    _, cols = mine.shape
+    pair, ff = acc.shape
+    width = pair // 2
     rows = width // 2
 
-    def body(sc, acc_ref, m_ref, i_ref, g_ref, b0, b1, b2, b3, lbuf, total):
+    def body(sc, acc_ref, m_ref, i_ref, gain_ref, b0, b1, b2, b3, lbuf, total):
         z, c = sc[2], sc[3]
-        lbuf[pl.ds(pl.multiple_of(c * width, width), width), :] = m_ref[...]
-        lbuf[pl.ds(pl.multiple_of((1 - c) * width, width), width), :] = i_ref[...]
-        total[...] = acc_ref[...] + dot(lbuf[...], g_ref[...], ((1,), (1,)))
+        lbuf[pl.ds(pl.multiple_of(c * width, width), width), :] = m_ref[ff:, :]
+        lbuf[pl.ds(pl.multiple_of((1 - c) * width, width), width), :] = i_ref[ff:, :]
+        total[...] = acc_ref[...] + dot(lbuf[...], m_ref[:ff, :], ((1,), (1,)))
+        tail = extra_rows(gain_ref[0:1, :])
         for k, ref in enumerate((b0, b1, b2, b3)):
             start = pl.multiple_of(((z + k) % 4) * rows, rows)
-            ref[...] = total[pl.ds(start, rows), :].astype(ref.dtype)
-
-    return call(
-        body,
-        [((rows, ff), F32)] + [((rows, ff), BF16)] * 3,
-        [(sc, S)] + [(a, V) for a in (acc, mine, its, gp)],
-        [pltpu.VMEM((2 * width, cols), BF16), pltpu.VMEM((2 * width, ff), F32)],
-        flops=4 * width * ff * cols,
+            ref[:rows, :] = total[pl.ds(start, rows), :].astype(ref.dtype)
+            if k:
+                ref[rows:, :] = jnp.zeros((EXTRA, ff), BF16)
+                ref[rows:, :width] = tail
+
+    return call(
+        body,
+        [((rows, ff), F32)] + [((rows + EXTRA, ff), BF16)] * 3,
+        [(sc, S)] + [(a, V) for a in (acc, mine, its, gain)],
+        [pltpu.VMEM((pair, cols), BF16), pltpu.VMEM((pair, ff), F32)],
+        flops=2 * pair * ff * cols,
         limit=12,
     )
 
 
-def down_finish(sc, acc, mine, its, act):
-    _, rows, tok = mine.shape
-    ff, cols = act.shape
-
-    def body(sc, acc_ref, m_ref, i_ref, a_ref, b0, b1, b2, b3, lbuf, total):
+def down_finish(sc, acc, mine, its):
+    _, cols = mine.shape
+    pair, ff = acc.shape
+    rows = pair // 4
+
+    def body(sc, acc_ref, m_ref, i_ref, b0, b1, b2, b3, lbuf, total):
         x, y, c = sc[0], sc[1], sc[3]
-        for j in range(4):
-            cut = slice(j * rows, (j + 1) * rows)
-            left, right = m_ref[j], i_ref[OTHER[j]]
-            lbuf[cut, :tok] = jnp.where(c == 0, left, right)
-            lbuf[cut, tok:] = jnp.where(c == 0, right, left)
-        total[...] = acc_ref[...] + dot(lbuf[...], a_ref[...], ((1,), (1,)))
+        m0, m1 = m_ref[ff : ff + rows, :], m_ref[ff + rows :, :]
+        i0, i1 = i_ref[ff : ff + rows, :], i_ref[ff + rows :, :]
+        for j, (first, second) in enumerate(((m0, i0), (i1, m0), (i0, m1), (m1, i1))):
+            lbuf[j * rows : (j + 1) * rows, :] = jnp.where(c == 0, first, second)
+        total[...] = acc_ref[...] + dot(lbuf[...], m_ref[:ff, :], ((1,), (1,)))
         for k, ref in enumerate((b0, b1, b2, b3)):
             start = pl.multiple_of(listed(x + k, y, c) * rows, rows)
             ref[...] = total[pl.ds(start, rows), :].astype(ref.dtype)
@@ -388,9 +402,9 @@
     return call(
         body,
         [((rows, ff), F32)] + [((rows, ff), BF16)] * 3,
-        [(sc, S)] + [(a, V) for a in (acc, mine, its, act)],
-        [pltpu.VMEM((4 * rows, cols), BF16), pltpu.VMEM((4 * rows, ff), F32)],
-        flops=8 * rows * ff * cols,
+        [(sc, S)] + [(a, V) for a in (acc, mine, its)],
+        [pltpu.VMEM((pair, cols), BF16), pltpu.VMEM((pair, ff), F32)],
+        flops=2 * pair * ff * cols,
         limit=12,
     )
 
@@ -401,12 +415,25 @@
 
 def add_up(blocks, inv_count):
     first, *rest = blocks
+    rows = first.shape[0]
 
     def body(own, r1, r2, r3, ic_ref, out_ref):
-        total = own[...] + r1[...].astype(F32) + (r2[...].astype(F32) + r3[...].astype(F32))
-        out_ref[...] = total * ic_ref[0:1, 0:1]
+        parts = [r[:rows, :].astype(F32) for r in (r1, r2, r3)]
+        out_ref[...] = (own[...] + parts[0] + (parts[1] + parts[2])) * ic_ref[0:1, 0:1]
 
     return call(body, [(first.shape, F32)], [(a, V) for a in (first, *rest, inv_count)])[0]
+
+
+def gain_over_z(gain, blocks):
+    width = gain.shape[1]
+
+    def body(g_ref, r1, r2, r3, out_ref):
+        total = g_ref[0:1, :]
+        for r in (r1, r2, r3):
+            total = total + sum_extra(r[-EXTRA:, :width])
+        out_ref[...] = jnp.broadcast_to(total, out_ref.shape)
+
+    return call(body, [(gain.shape, F32)], [(a, V) for a in (gain, *blocks)])[0]
 
 
 def on_device(hidden_in, out_grad, pack_fill, norm_gain, up_weight, down_weight):
@@ -418,31 +445,31 @@
         [jnp.stack(place).astype(jnp.int32), pack_fill[:, 0], jnp.zeros((2,), jnp.int32)]
     )
 
-    payload, count = prepare(pack_fill, hidden_t, out_t, gain_row)
-    own = (payload, *gathered(payload, "y"))
+    payload = prepare(hidden_t, out_t, gain_row)
+    own = (payload, *gathered(payload, payload, "y"))
     other = tuple(sibling(a) for a in own)
     upv, downv = stage_weights(sc, up_weight, down_weight)
-    inv_count = 1.0 / total_over(count, ("x", "z"))
-
-    act, gp, inv, rd, h_own, h_a, h_2, o_own, o_a, o_2 = mlp(sc, upv, downv, own, other)
-    gps = gathered(gp, "x")
-    acts = gathered(act, "z")
+    inv_count = 1.0 / total_over(own_count(sc), ("x", "z"))
+
+    act_all, act, gp_all, gp, inv, rd, h_own, h_a, o_own, o_a = mlp(sc, upv, downv, own, other)
+    gps = gathered(gp_all, gp, "x")
+    acts = gathered(act_all, act, "z")
     h_a = led(h_a, "x", 1)
     o_a = led(o_a, "z", 1)
-    h_2 = moved(h_2, "x", 2)
-    o_2 = moved(o_2, "z", 2)
 
     pown, psib = normed_part(sc, upv, gp, rd)
     q0, rd0, *q_send = pair_sum(pown, sibling(psib), rd)
     q_recv = (led(q_send[0], "y", -1), led(q_send[1], "y", 1), moved(q_send[2], "y", 2))
+    in_t, gain = input_grad(sc, q0, rd0, q_recv, hidden_t, out_t, gain_row, inv, inv_count)
 
     up_acc = gradient_start((h_own, h_a, sibling(h_a)), (gp, *gps[:2]))
     down_acc = gradient_start((o_own, o_a, sibling(o_a)), (act, *acts[:2]), True)
-    up_blocks = at_owner(up_finish(sc, up_acc, h_2, sibling(h_2), gps[2]), "z")
-    down_blocks = at_owner(down_finish(sc, down_acc, o_2, sibling(o_2), acts[2]), "x")
-
-    in_t, gain = input_grad(sc, q0, rd0, q_recv, hidden_t, out_t, gain_row, inv, inv_count)
-    gain_grad = total_over(gain[:, 0], ("x", "z"))
+    up_blocks = up_finish(sc, up_acc, gps[2], sibling(gps[2]), gain)
+    up_blocks = at_owner(up_blocks, "z")
+    down_blocks = down_finish(sc, down_acc, acts[2], sibling(acts[2]))
+    down_blocks = at_owner(down_blocks, "x")
+
+    gain_grad = total_over(gain_over_z(gain, up_blocks[1:]), ("x",))[0]
     up_grad = add_up(up_blocks, inv_count)
     down_grad = add_up(down_blocks, inv_count).T
     return (jnp.swapaxes(in_t, 1, 2), up_grad, down_grad, gain_grad)

time: 166 us -> 148 us (0.89)
  starting transfers between devices: 53.5 us -> 43.7 us
  Pallas kernels: 31.2 us -> 25.8 us
  local copies, waits for them, and re-layouts: 8.59 us -> 3.3 us
  waiting for transfers between devices: 69.9 us -> 73.5 us
    ppermute x30 -> x25, starting transfers between devices: 41.6 us -> 26.2 us  [moved(): lax.ppermute(value, axis, [(i, (i + step) % size) for i in range(size)])]
    ppermute x13, waiting for transfers between devices: 28.4 us -> 34.9 us  [led(): return lax.ppermute(value, (axis, 'c'), pairs)]
    ppermute x13, starting transfers between devices: 11.9 us -> 17.5 us  [led(): return lax.ppermute(value, (axis, 'c'), pairs)]
    pallas_call x12 -> x14, Pallas kernels: 31.2 us -> 25.8 us  [call(): pl.pallas_call(body, out_shape=[jax.ShapeDtypeStruct(s, d) for s, d in ou...]
    unnamed x27 -> x12, local copies, waits for them, and re-layouts: 7.85 us -> 2.56 us
    ppermute x30 -> x25, waiting for transfers between devices: 41.5 us -> 38.6 us  [moved(): lax.ppermute(value, axis, [(i, (i + step) % size) for i in range(size)])]
  transfers between devices with their start and end apart: 43 -> 38, of which waited for: 17 -> 18; matrix products, arithmetic and copies ran while one was open for 1% -> 1% of each run, Pallas kernels for 12% -> 13%
where the time goes in v4:
time: 148 us
  waiting for transfers between devices  73.5 us (50%)
  starting transfers between devices  43.7 us (30%)
  Pallas kernels  25.8 us (17%)
  local copies, waits for them, and re-layouts  3.3 us (2%)
    ppermute x25, waiting for transfers between devices, moved(): lax.ppermute(value, axis, [(i, (i + step) % size) for i in range(size)])  38.6 us
    ppermute x13, waiting for transfers between devices, led(): return lax.ppermute(value, (axis, 'c'), pairs)  34.9 us
    ppermute x25, starting transfers between devices, moved(): lax.ppermute(value, axis, [(i, (i + step) % size) for i in range(size)])  26.2 us
    pallas_call x14, Pallas kernels, call(): pl.pallas_call(body, out_shape=[jax.ShapeDtypeStruct(s, d) for s, d in ou...  25.8 us
    ppermute x13, starting transfers between devices, led(): return lax.ppermute(value, (axis, 'c'), pairs)  17.5 us
  transfers between devices with their start and end apart: 38, of which 18 were waited for; matrix products, arithmetic and copies ran while one was open for 1% of the time, Pallas kernels for 13%

profile of v4, /device:TPU:0, one launch (start us, length us, event | category | flops | bytes accessed | tf_op | source)
XLA Modules:
  0.0 147.7 jit_solution(5988709865075432069)
XLA Ops:
  0.6 0.9 copy-done
  1.6 0.9 copy-done.2
  3.3 1.8 %collective-permute-start = (bf16[2,912,128]{2,1,0:T(8,128)(2,1)S(1)}, bf16[2,912,128]{2,1,0:T(8,128)(2,1)S(1)}, u32[]{:S(2)}, u32[]{:S(2)}) collective-permute-start(bf16[2,912,128]{2,1,0:T(8,128)(2,1)S(1)} %shard_map.94.refs_0_), channel_id=1, source_target_pairs={{0,2},{1,7},{2,4},{3,1},{4,6},{5,3},{6,0},{7,5},{8,10},{9,15},{10,... | collective-permute-start | bytes 1400840 | tf_op jit(solution)/shard_map/ppermute | solution.py:31
  5.1 1.5 %collective-permute-start.1 = (bf16[2,912,128]{2,1,0:T(8,128)(2,1)S(1)}, bf16[2,912,128]{2,1,0:T(8,128)(2,1)S(1)}, u32[]{:S(2)}, u32[]{:S(2)}) collective-permute-start(bf16[2,912,128]{2,1,0:T(8,128)(2,1)S(1)} %shard_map.94.refs_0_), channel_id=1, source_target_pairs={{0,6},{1,3},{2,0},{3,5},{4,2},{5,7},{6,4},{7,1},{8,14},{9,11},{10,... | collective-permute-start | bytes 1400840 | tf_op jit(solution)/shard_map/ppermute | solution.py:31
  6.6 9.8 %collective-permute-done.refs_1_ = bf16[2,912,128]{2,1,0:T(8,128)(2,1)S(1)} collective-permute-done((bf16[2,912,128]{2,1,0:T(8,128)(2,1)S(1)}, bf16[2,912,128]{2,1,0:T(8,128)(2,1)S(1)}, u32[]{:S(2)}, u32[]{:S(2)}) %collective-permute-start) | collective-permute-done | bytes 466976 | tf_op jit(solution)/shard_map/ppermute | solution.py:31
  16.5 1.9 %collective-permute-start.2 = (bf16[2,912,128]{2,1,0:T(8,128)(2,1)S(1)}, bf16[2,912,128]{2,1,0:T(8,128)(2,1)S(1)}, u32[]{:S(2)}, u32[]{:S(2)}) collective-permute-start(bf16[2,912,128]{2,1,0:T(8,128)(2,1)S(1)} %collective-permute-done.refs_1_), channel_id=1, source_target_pairs={{0,2},{1,7},{2,4},{3,1},{4,6},{5,3},{6,0},{7,5},{8,10},{9,15},{10,... | collective-permute-start | bytes 1400840 | tf_op jit(solution)/shard_map/ppermute | solution.py:31
  19.3 7.0 %collective-permute-done.2.refs_3_ = bf16[2,912,128]{2,1,0:T(8,128)(2,1)S(1)} collective-permute-done((bf16[2,912,128]{2,1,0:T(8,128)(2,1)S(1)}, bf16[2,912,128]{2,1,0:T(8,128)(2,1)S(1)}, u32[]{:S(2)}, u32[]{:S(2)}) %collective-permute-start.2) | collective-permute-done | bytes 466976 | tf_op jit(solution)/shard_map/ppermute | solution.py:31
  27.0 5.3 %shard_map.93 = (bf16[4,896,896]{2,1,0:T(8,128)(2,1)S(1)}, bf16[4,896,896]{2,1,0:T(8,128)(2,1)S(1)}) custom-call(s32[8]{0:T(128)S(1)} %concatenate.3.sc, bf16[3584,896]{1,0:T(8,128)(2,1)} %up_ref.1, bf16[896,3584]{1,0:T(8,128)(2,1)} %down_ref.1), custom_call_target="tpu_custom_call" | custom-call | flops 1000000000 | bytes 12845056 | tf_op jit(solution)/shard_map/pallas_call | solution.py:56
  32.4 6.7 %shard_map.95 = (bf16[1344,256]{1,0:T(8,128)(2,1)S(1)}, bf16[896,256]{1,0:T(8,128)(2,1)S(1)}, bf16[1344,256]{1,0:T(8,128)(2,1)S(1)}, bf16[896,256]{1,0:T(8,128)(...) custom-call(s32[8]{0:T(128)S(1)} %concatenate.3.sc, ...), custom_call_target="tpu_custom_call" | custom-call | flops 3288334336 | bytes 12845056 | tf_op jit(solution)/shard_map/pallas_call | solution.py:56
  39.0 1.8 %collective-permute-start.19 = (bf16[1344,256]{1,0:T(8,128)(2,1)S(1)}, bf16[1344,256]{1,0:T(8,128)(2,1)S(1)}, u32[]{:S(2)}, u32[]{:S(2)}) collective-permute-start(bf16[1344,256]{1,0:T(8,128)(2,1)S(1)} %get-tuple-element.48), channel_id=1, source_target_pairs={{0,32},{1,97},{32,64},{33,1},{64,96},{65,33},{96,0},{97,65},{2,34}... | collective-permute-start | bytes 2064392 | tf_op jit(solution)/shard_map/ppermute | solution.py:31
  40.8 2.6 %shard_map.96 = (f32[4,448,256]{2,1,0:T(8,128)S(1)}, bf16[4,464,256]{2,1,0:T(8,128)(2,1)S(1)}) custom-call(s32[8]{0:T(128)S(1)} %concatenate.3.sc, bf16[4,896,896]{2,1,0:T(8,128)(2,1)S(1)} %get-tuple-element.33.up_ref, bf16[896,256]{1,0:T(8,128)(2,1)S(1)} %get-tuple-element.35.gp_ref.r0, f32[8,256]{1,0:T(8,128)S(1)} %get-tuple-element.36.rd_ref), custom_call_target="tpu_custom_call" | custom-call | flops 1644167168 | bytes 6422528 | tf_op jit(solution)/shard_map/pallas_call | solution.py:56
  43.4 1.6 %collective-permute-start.7 = (bf16[4,464,256]{2,1,0:T(8,128)(2,1)S(1)}, bf16[4,464,256]{2,1,0:T(8,128)(2,1)S(1)}, u32[]{:S(2)}, u32[]{:S(2)}) collective-permute-start(bf16[4,464,256]{2,1,0:T(8,128)(2,1)S(1)} %get-tuple-element.38), channel_id=1, source_target_pairs={{0,1},{1,0},{2,3},{3,2},{4,5},{5,4},{6,7},{7,6},{8,9},{9,8},{10,11... | collective-permute-start | bytes 2850824 | tf_op jit(solution)/shard_map/ppermute | solution.py:23
  45.0 1.9 %collective-permute-start.28 = (bf16[1344,256]{1,0:T(8,128)(2,1)S(1)}, bf16[1344,256]{1,0:T(8,128)(2,1)S(1)}, u32[]{:S(2)}, u32[]{:S(2)}) collective-permute-start(bf16[1344,256]{1,0:T(8,128)(2,1)S(1)} %get-tuple-element.57), channel_id=1, source_target_pairs={{0,8},{1,25},{8,16},{9,1},{16,24},{17,9},{24,0},{25,17},{2,10},{3,... | collective-permute-start | bytes 2064392 | tf_op jit(solution)/shard_map/ppermute | solution.py:31
  47.0 4.3 %collective-permute-done.19.r1 = bf16[1344,256]{1,0:T(8,128)(2,1)S(1)} collective-permute-done((bf16[1344,256]{1,0:T(8,128)(2,1)S(1)}, bf16[1344,256]{1,0:T(8,128)(2,1)S(1)}, u32[]{:S(2)}, u32[]{:S(2)}) %collective-permute-start.19) | collective-permute-done | bytes 688160 | tf_op jit(solution)/shard_map/ppermute | solution.py:31
  52.3 2.8 %collective-permute-start.11 = (f32[8,128]{1,0:T(8,128)S(1)}, f32[8,128]{1,0:T(8,128)S(1)}, u32[]{:S(2)}, u32[]{:S(2)}) collective-permute-start(f32[8,128]{1,0:T(8,128)S(1)} %shard_map.98), channel_id=1, source_target_pairs={{0,64},{32,96},{64,0},{96,32},{1,65},{33,97},{65,1},{97,33},{2,66}... | collective-permute-start | bytes 12296 | tf_op jit(solution)/shard_map/ppermute | solution.py:23
  55.1 9.7 %collective-permute-done.11 = f32[8,128]{1,0:T(8,128)S(1)} collective-permute-done((f32[8,128]{1,0:T(8,128)S(1)}, f32[8,128]{1,0:T(8,128)S(1)}, u32[]{:S(2)}, u32[]{:S(2)}) %collective-permute-start.11) | collective-permute-done | bytes 4128 | tf_op jit(solution)/shard_map/ppermute | solution.py:23
  64.8 4.8 %collective-permute-done.12 = f32[8,128]{1,0:T(8,128)S(1)} collective-permute-done((f32[8,128]{1,0:T(8,128)S(1)}, f32[8,128]{1,0:T(8,128)S(1)}, u32[]{:S(2)}, u32[]{:S(2)}) %collective-permute-start.12) | collective-permute-done | bytes 4128 | tf_op jit(solution)/shard_map/ppermute | solution.py:23
  69.7 3.6 %collective-permute-done.13 = f32[8,128]{1,0:T(8,128)S(1)} collective-permute-done((f32[8,128]{1,0:T(8,128)S(1)}, f32[8,128]{1,0:T(8,128)S(1)}, u32[]{:S(2)}, u32[]{:S(2)}) %collective-permute-start.13) | collective-permute-done | bytes 4128 | tf_op jit(solution)/shard_map/ppermute | solution.py:23
  73.3 3.9 %collective-permute-start.14 = (f32[8,128]{1,0:T(8,128)S(1)}, f32[8,128]{1,0:T(8,128)S(1)}, u32[]{:S(2)}, u32[]{:S(2)}) collective-permute-start(f32[8,128]{1,0:T(8,128)S(1)} %add_add_fusion), channel_id=1, source_target_pairs={{0,16},{8,24},{16,0},{24,8},{1,17},{9,25},{17,1},{25,9},{2,18},{10... | collective-permute-start | bytes 12296 | tf_op jit(solution)/shard_map/ppermute | solution.py:23
  77.2 1.6 %collective-permute-done.14 = f32[8,128]{1,0:T(8,128)S(1)} collective-permute-done((f32[8,128]{1,0:T(8,128)S(1)}, f32[8,128]{1,0:T(8,128)S(1)}, u32[]{:S(2)}, u32[]{:S(2)}) %collective-permute-start.14) | collective-permute-done | bytes 4128 | tf_op jit(solution)/shard_map/ppermute | solution.py:23
  78.7 1.6 %collective-permute-start.15 = (f32[8,128]{1,0:T(8,128)S(1)}, f32[8,128]{1,0:T(8,128)S(1)}, u32[]{:S(2)}, u32[]{:S(2)}) collective-permute-start(f32[8,128]{1,0:T(8,128)S(1)} %add_add_fusion), channel_id=1, source_target_pairs={{0,8},{8,16},{16,24},{24,0},{1,9},{9,17},{17,25},{25,1},{2,10},{10... | collective-permute-start | bytes 12296 | tf_op jit(solution)/shard_map/ppermute | solution.py:23
  80.3 3.7 %collective-permute-done.15 = f32[8,128]{1,0:T(8,128)S(1)} collective-permute-done((f32[8,128]{1,0:T(8,128)S(1)}, f32[8,128]{1,0:T(8,128)S(1)}, u32[]{:S(2)}, u32[]{:S(2)}) %collective-permute-start.15) | collective-permute-done | bytes 4128 | tf_op jit(solution)/shard_map/ppermute | solution.py:23
  84.0 2.0 %collective-permute-start.16 = (f32[8,128]{1,0:T(8,128)S(1)}, f32[8,128]{1,0:T(8,128)S(1)}, u32[]{:S(2)}, u32[]{:S(2)}) collective-permute-start(f32[8,128]{1,0:T(8,128)S(1)} %add_add_fusion), channel_id=1, source_target_pairs={{0,24},{8,0},{16,8},{24,16},{1,25},{9,1},{17,9},{25,17},{2,26},{10... | collective-permute-start | bytes 12296 | tf_op jit(solution)/shard_map/ppermute | solution.py:23
  86.0 1.6 %collective-permute-done.16 = f32[8,128]{1,0:T(8,128)S(1)} collective-permute-done((f32[8,128]{1,0:T(8,128)S(1)}, f32[8,128]{1,0:T(8,128)S(1)}, u32[]{:S(2)}, u32[]{:S(2)}) %collective-permute-start.16) | collective-permute-done | bytes 4128 | tf_op jit(solution)/shard_map/ppermute | solution.py:23
  87.7 1.2 collective-permute-start.20
  88.9 1.8 %collective-permute-start.30 = (bf16[1344,256]{1,0:T(8,128)(2,1)S(1)}, bf16[1344,256]{1,0:T(8,128)(2,1)S(1)}, u32[]{:S(2)}, u32[]{:S(2)}) collective-permute-start(bf16[1344,256]{1,0:T(8,128)(2,1)S(1)} %collective-permute-done.28.r1), channel_id=1, source_target_pairs={{0,8},{1,25},{8,16},{9,1},{16,24},{17,9},{24,0},{25,17},{2,10},{3,... | collective-permute-start | bytes 2064392 | tf_op jit(solution)/shard_map/ppermute | solution.py:31
  91.4 4.7 %collective-permute-done.20.r2 = bf16[896,256]{1,0:T(8,128)(2,1)S(1)} collective-permute-done((bf16[896,256]{1,0:T(8,128)(2,1)S(1)}, bf16[896,256]{1,0:T(8,128)(2,1)S(1)}, u32[]{:S(2)}, u32[]{:S(2)}) %collective-permute-start.20) | collective-permute-done | bytes 458784 | tf_op jit(solution)/shard_map/ppermute | solution.py:31
  96.1 1.4 collective-permute-start.10
  97.5 2.3 %collective-permute-done.26.l1 = bf16[4,224,256]{2,1,0:T(8,128)(2,1)S(1)} collective-permute-done((bf16[4,224,256]{2,1,0:T(8,128)(2,1)S(1)}, bf16[4,224,256]{2,1,0:T(8,128)(2,1)S(1)}, u32[]{:S(2)}, u32[]{:S(2)}) %collective-permute-start.26) | collective-permute-done | bytes 458784 | tf_op jit(solution)/shard_map/ppermute | solution.py:31
  100.7 3.5 %collective-permute-start.29 = (bf16[896,256]{1,0:T(8,128)(2,1)S(1)}, bf16[896,256]{1,0:T(8,128)(2,1)S(1)}, u32[]{:S(2)}, u32[]{:S(2)}) collective-permute-start(bf16[896,256]{1,0:T(8,128)(2,1)S(1)} %get-tuple-element.56.r0), channel_id=1, source_target_pairs={{0,24},{1,9},{8,0},{9,17},{16,8},{17,25},{24,16},{25,1},{2,26},{3,... | collective-permute-start | bytes 1376264 | tf_op jit(solution)/shard_map/ppermute | solution.py:31
  104.2 1.9 %collective-permute-done.8.r1 = bf16[464,256]{1,0:T(8,128)(2,1)S(1)} collective-permute-done((bf16[464,256]{1,0:T(8,128)(2,1)S(1)}, bf16[464,256]{1,0:T(8,128)(2,1)S(1)}, u32[]{:S(2)}, u32[]{:S(2)}) %collective-permute-start.8) | collective-permute-done | bytes 237600 | tf_op jit(solution)/shard_map/ppermute | solution.py:31
  106.8 4.1 %collective-permute-done.30.m_ref = bf16[1344,256]{1,0:T(8,128)(2,1)S(1)} collective-permute-done((bf16[1344,256]{1,0:T(8,128)(2,1)S(1)}, bf16[1344,256]{1,0:T(8,128)(2,1)S(1)}, u32[]{:S(2)}, u32[]{:S(2)}) %collective-permute-start.30) | collective-permute-done | bytes 688160 | tf_op jit(solution)/shard_map/ppermute | solution.py:31
  110.9 1.6 %shard_map.100.acc_ref = f32[896,896]{1,0:T(8,128)S(1)} custom-call(bf16[896,256]{1,0:T(8,128)(2,1)S(1)} %get-tuple-element.46.l0, bf16[896,256]{1,0:T(8,128)(2,1)S(1)} %collective-permute-done.17.l1, bf16[896,256]{1,0:T(8,128)(2,1)S(1)} %collective-permute-done.18.l2, bf16[896,256]{1,0:T(8,128)(2,1)S(1)} %get-tuple-element.35.gp_ref.r0, ...), custom_call_target="tpu_custom_call" | custom-call | flops 1233125376 | tf_op jit(solution)/shard_map/pallas_call | solution.py:56
  113.3 1.5 %shard_map.99 = (bf16[2,448,128]{2,1,0:T(8,128)(2,1)}, f32[8,448]{1,0:T(8,128)S(1)}) custom-call(s32[8]{0:T(128)S(1)} %concatenate.3.sc, f32[448,256]{1,0:T(8,128)S(1)} %get-tuple-element.39.q0, f32[8,256]{1,0:T(8,128)S(1)} %get-tuple-element.40.rd0, bf16[464,256]{1,0:T(8,128)(2,1)S(1)} %collective-permute-done.8.r1, ...), custom_call_target="tpu_custom_call" | custom-call | tf_op jit(solution)/shard_map/pallas_call | solution.py:56
  114.9 1.4 shard_map.101
  116.6 1.6 %shard_map.103.acc_ref = f32[896,896]{1,0:T(8,128)S(1)} custom-call(bf16[4,224,256]{2,1,0:T(8,128)(2,1)S(1)} %get-tuple-element.54.l0, bf16[4,224,256]{2,1,0:T(8,128)(2,1)S(1)} %collective-permute-done.26.l1, bf16[4,224,256]{2,1,0:T(8,128)(2,1)S(1)} %collective-permute-done.27.l2, bf16[896,256]{1,0:T(8,128)(2,1)S(1)} %get-tuple-element.56.r0, ...), custom_call_target="tpu_custom_call" | custom-call | flops 1233125376 | tf_op jit(solution)/shard_map/pallas_call | solution.py:56
  118.2 4.8 %collective-permute-start.24 = (bf16[240,896]{1,0:T(8,128)(2,1)S(1)}, bf16[240,896]{1,0:T(8,128)(2,1)S(1)}, u32[]{:S(2)}, u32[]{:S(2)}) collective-permute-start(bf16[240,896]{1,0:T(8,128)(2,1)S(1)} %get-tuple-element.52), channel_id=1, source_target_pairs={{0,16},{8,24},{16,0},{24,8},{1,17},{9,25},{17,1},{25,9},{2,18},{10... | collective-permute-start | bytes 1290248 | tf_op jit(solution)/shard_map/ppermute | solution.py:23
  123.1 1.5 %shard_map.104 = (f32[224,896]{1,0:T(8,128)S(1)}, bf16[224,896]{1,0:T(8,128)(2,1)S(1)}, bf16[224,896]{1,0:T(8,128)(2,1)S(1)}, bf16[224,896]{1,0:T(8,128)(2,1)S(1)}) custom-call(s32[8]{0:T(128)S(1)} %concatenate.3.sc, f32[896,896]{1,0:T(8,128)S(1)} %shard_map.103.acc_ref, bf16[1344,256]{1,0:T(8,128)(2,1)S(1)} %collective-permute-done.30.m_ref, ...), custom_call_target="tpu_custom_call" | custom-call | flops 411041792 | tf_op jit(solution)/shard_map/pallas_call | solution.py:56
  124.7 1.2 collective-permute-start.32
  125.8 1.6 %collective-permute-start.33 = (bf16[224,896]{1,0:T(8,128)(2,1)S(1)}, bf16[224,896]{1,0:T(8,128)(2,1)S(1)}, u32[]{:S(2)}, u32[]{:S(2)}) collective-permute-start(bf16[224,896]{1,0:T(8,128)(2,1)S(1)} %get-tuple-element.60), channel_id=1, source_target_pairs={{0,64},{32,96},{64,0},{96,32},{1,65},{33,97},{65,1},{97,33},{2,66}... | collective-permute-start | bytes 1204232 | tf_op jit(solution)/shard_map/ppermute | solution.py:23
  127.4 4.1 %collective-permute-done.23.r1 = bf16[240,896]{1,0:T(8,128)(2,1)S(1)} collective-permute-done((bf16[240,896]{1,0:T(8,128)(2,1)S(1)}, bf16[240,896]{1,0:T(8,128)(2,1)S(1)}, u32[]{:S(2)}, u32[]{:S(2)}) %collective-permute-start.23) | collective-permute-done | bytes 430112 | tf_op jit(solution)/shard_map/ppermute | solution.py:23
  131.5 1.3 collective-permute-start.34
  132.9 5.7 %collective-permute-done.24.r2 = bf16[240,896]{1,0:T(8,128)(2,1)S(1)} collective-permute-done((bf16[240,896]{1,0:T(8,128)(2,1)S(1)}, bf16[240,896]{1,0:T(8,128)(2,1)S(1)}, u32[]{:S(2)}, u32[]{:S(2)}) %collective-permute-start.24) | collective-permute-done | bytes 430112 | tf_op jit(solution)/shard_map/ppermute | solution.py:23
  138.5 2.1 %collective-permute-done.25.r3 = bf16[240,896]{1,0:T(8,128)(2,1)S(1)} collective-permute-done((bf16[240,896]{1,0:T(8,128)(2,1)S(1)}, bf16[240,896]{1,0:T(8,128)(2,1)S(1)}, u32[]{:S(2)}, u32[]{:S(2)}) %collective-permute-start.25) | collective-permute-done | bytes 430112 | tf_op jit(solution)/shard_map/ppermute | solution.py:23
  141.6 1.7 %collective-permute-done.32.r1 = bf16[224,896]{1,0:T(8,128)(2,1)S(1)} collective-permute-done((bf16[224,896]{1,0:T(8,128)(2,1)S(1)}, bf16[224,896]{1,0:T(8,128)(2,1)S(1)}, u32[]{:S(2)}, u32[]{:S(2)}) %collective-permute-start.32) | collective-permute-done | bytes 401440 | tf_op jit(solution)/shard_map/ppermute | solution.py:23
  143.3 1.3 collective-permute-start.37
  144.6 1.3 shard_map.105
  145.8 1.3 shard_map.102
  (59 shorter events, 8.8 us)
Async XLA Ops:
  0.6 0.9 copy-start
  1.6 0.9 copy-start.2
  2.5 0.7 copy-start.4
  3.3 13.1 %collective-permute-start = (bf16[2,912,128]{2,1,0:T(8,128)(2,1)S(1)}, bf16[2,912,128]{2,1,0:T(8,128)(2,1)S(1)}, u32[]{:S(2)}, u32[]{:S(2)}) collective-permute-start(bf16[2,912,128]{2,1,0:T(8,128)(2,1)S(1)} %shard_map.94.refs_0_), channel_id=1, source_target_pairs={{0,2},{1,7},{2,4},{3,1},{4,6},{5,3},{6,0},{7,5},{8,10},{9,15},{10,... | collective-permute-start | bytes 1400840 | tf_op jit(solution)/shard_map/ppermute | solution.py:31
  5.1 13.8 %collective-permute-start.1 = (bf16[2,912,128]{2,1,0:T(8,128)(2,1)S(1)}, bf16[2,912,128]{2,1,0:T(8,128)(2,1)S(1)}, u32[]{:S(2)}, u32[]{:S(2)}) collective-permute-start(bf16[2,912,128]{2,1,0:T(8,128)(2,1)S(1)} %shard_map.94.refs_0_), channel_id=1, source_target_pairs={{0,6},{1,3},{2,0},{3,5},{4,2},{5,7},{6,4},{7,1},{8,14},{9,11},{10,... | collective-permute-start | bytes 1400840 | tf_op jit(solution)/shard_map/ppermute | solution.py:31
  16.5 9.8 %collective-permute-start.2 = (bf16[2,912,128]{2,1,0:T(8,128)(2,1)S(1)}, bf16[2,912,128]{2,1,0:T(8,128)(2,1)S(1)}, u32[]{:S(2)}, u32[]{:S(2)}) collective-permute-start(bf16[2,912,128]{2,1,0:T(8,128)(2,1)S(1)} %collective-permute-done.refs_1_), channel_id=1, source_target_pairs={{0,2},{1,7},{2,4},{3,1},{4,6},{5,3},{6,0},{7,5},{8,10},{9,15},{10,... | collective-permute-start | bytes 1400840 | tf_op jit(solution)/shard_map/ppermute | solution.py:31
  18.3 14.0 %collective-permute-start.3 = (bf16[2,912,128]{2,1,0:T(8,128)(2,1)S(1)}, bf16[2,912,128]{2,1,0:T(8,128)(2,1)S(1)}, u32[]{:S(2)}, u32[]{:S(2)}) collective-permute-start(bf16[2,912,128]{2,1,0:T(8,128)(2,1)S(1)} %shard_map.94.refs_0_), channel_id=1, source_target_pairs={{0,1},{1,0},{2,3},{3,2},{4,5},{5,4},{6,7},{7,6},{8,9},{9,8},{10,11... | collective-permute-start | bytes 1400840 | tf_op jit(solution)/shard_map/ppermute | solution.py:23
  18.8 13.6 %collective-permute-start.4 = (bf16[2,912,128]{2,1,0:T(8,128)(2,1)S(1)}, bf16[2,912,128]{2,1,0:T(8,128)(2,1)S(1)}, u32[]{:S(2)}, u32[]{:S(2)}) collective-permute-start(bf16[2,912,128]{2,1,0:T(8,128)(2,1)S(1)} %collective-permute-done.refs_1_), channel_id=1, source_target_pairs={{0,1},{1,0},{2,3},{3,2},{4,5},{5,4},{6,7},{7,6},{8,9},{9,8},{10,11... | collective-permute-start | bytes 1400840 | tf_op jit(solution)/shard_map/ppermute | solution.py:23
  18.9 13.5 %collective-permute-start.5 = (bf16[2,912,128]{2,1,0:T(8,128)(2,1)S(1)}, bf16[2,912,128]{2,1,0:T(8,128)(2,1)S(1)}, u32[]{:S(2)}, u32[]{:S(2)}) collective-permute-start(bf16[2,912,128]{2,1,0:T(8,128)(2,1)S(1)} %collective-permute-done.1.refs_2_), channel_id=1, source_target_pairs={{0,1},{1,0},{2,3},{3,2},{4,5},{5,4},{6,7},{7,6},{8,9},{9,8},{10,11... | collective-permute-start | bytes 1400840 | tf_op jit(solution)/shard_map/ppermute | solution.py:23
  26.2 6.1 %collective-permute-start.6 = (bf16[2,912,128]{2,1,0:T(8,128)(2,1)S(1)}, bf16[2,912,128]{2,1,0:T(8,128)(2,1)}, u32[]{:S(2)}, u32[]{:S(2)}) collective-permute-start(bf16[2,912,128]{2,1,0:T(8,128)(2,1)S(1)} %collective-permute-done.2.refs_3_), channel_id=1, source_target_pairs={{0,1},{1,0},{2,3},{3,2},{4,5},{5,4},{6,7},{7,6},{8,9},{9,8},{10,11... | collective-permute-start | bytes 1400840 | tf_op jit(solution)/shard_map/ppermute | solution.py:23
  39.0 12.2 %collective-permute-start.19 = (bf16[1344,256]{1,0:T(8,128)(2,1)S(1)}, bf16[1344,256]{1,0:T(8,128)(2,1)S(1)}, u32[]{:S(2)}, u32[]{:S(2)}) collective-permute-start(bf16[1344,256]{1,0:T(8,128)(2,1)S(1)} %get-tuple-element.48), channel_id=1, source_target_pairs={{0,32},{1,97},{32,64},{33,1},{64,96},{65,33},{96,0},{97,65},{2,34}... | collective-permute-start | bytes 2064392 | tf_op jit(solution)/shard_map/ppermute | solution.py:31
  40.8 72.5 %copy-start.1 = (bf16[2,128,448]{1,2,0:T(8,128)(2,1)S(1)}, bf16[2,128,448]{1,2,0:T(8,128)(2,1)}, u32[]{:S(2)}) copy-start(bf16[2,128,448]{1,2,0:T(8,128)(2,1)} %param.6) | copy-start | bytes 688132
  40.8 72.5 %copy-start.3 = (bf16[2,128,448]{1,2,0:T(8,128)(2,1)S(1)}, bf16[2,128,448]{1,2,0:T(8,128)(2,1)}, u32[]{:S(2)}) copy-start(bf16[2,128,448]{1,2,0:T(8,128)(2,1)} %param.7) | copy-start | bytes 688132
  40.8 72.5 %copy-start.5 = (f32[448]{0:T(512)S(1)}, f32[448]{0:T(512)}, u32[]{:S(2)}) copy-start(f32[448]{0:T(512)} %param.9) | copy-start | bytes 5380
  43.4 47.3 %collective-permute-start.7 = (bf16[4,464,256]{2,1,0:T(8,128)(2,1)S(1)}, bf16[4,464,256]{2,1,0:T(8,128)(2,1)S(1)}, u32[]{:S(2)}, u32[]{:S(2)}) collective-permute-start(bf16[4,464,256]{2,1,0:T(8,128)(2,1)S(1)} %get-tuple-element.38), channel_id=1, source_target_pairs={{0,1},{1,0},{2,3},{3,2},{4,5},{5,4},{6,7},{7,6},{8,9},{9,8},{10,11... | collective-permute-start | bytes 2850824 | tf_op jit(solution)/shard_map/ppermute | solution.py:23
  45.0 43.9 %collective-permute-start.28 = (bf16[1344,256]{1,0:T(8,128)(2,1)S(1)}, bf16[1344,256]{1,0:T(8,128)(2,1)S(1)}, u32[]{:S(2)}, u32[]{:S(2)}) collective-permute-start(bf16[1344,256]{1,0:T(8,128)(2,1)S(1)} %get-tuple-element.57), channel_id=1, source_target_pairs={{0,8},{1,25},{8,16},{9,1},{16,24},{17,9},{24,0},{25,17},{2,10},{3,... | collective-permute-start | bytes 2064392 | tf_op jit(solution)/shard_map/ppermute | solution.py:31
  46.9 41.9 %collective-permute-start.17 = (bf16[896,256]{1,0:T(8,128)(2,1)S(1)}, bf16[896,256]{1,0:T(8,128)(2,1)S(1)}, u32[]{:S(2)}, u32[]{:S(2)}) collective-permute-start(bf16[896,256]{1,0:T(8,128)(2,1)S(1)} %get-tuple-element.47), channel_id=1, source_target_pairs={{0,32},{1,97},{32,64},{33,1},{64,96},{65,33},{96,0},{97,65},{2,34}... | collective-permute-start | bytes 1376264 | tf_op jit(solution)/shard_map/ppermute | solution.py:31
  51.3 39.5 %collective-permute-start.21 = (bf16[1344,256]{1,0:T(8,128)(2,1)S(1)}, bf16[1344,256]{1,0:T(8,128)(2,1)S(1)}, u32[]{:S(2)}, u32[]{:S(2)}) collective-permute-start(bf16[1344,256]{1,0:T(8,128)(2,1)S(1)} %collective-permute-done.19.r1), channel_id=1, source_target_pairs={{0,32},{1,97},{32,64},{33,1},{64,96},{65,33},{96,0},{97,65},{2,34}... | collective-permute-start | bytes 2064392 | tf_op jit(solution)/shard_map/ppermute | solution.py:31
  52.3 12.5 %collective-permute-start.11 = (f32[8,128]{1,0:T(8,128)S(1)}, f32[8,128]{1,0:T(8,128)S(1)}, u32[]{:S(2)}, u32[]{:S(2)}) collective-permute-start(f32[8,128]{1,0:T(8,128)S(1)} %shard_map.98), channel_id=1, source_target_pairs={{0,64},{32,96},{64,0},{96,32},{1,65},{33,97},{65,1},{97,33},{2,66}... | collective-permute-start | bytes 12296 | tf_op jit(solution)/shard_map/ppermute | solution.py:23
  64.8 4.8 %collective-permute-start.12 = (f32[8,128]{1,0:T(8,128)S(1)}, f32[8,128]{1,0:T(8,128)S(1)}, u32[]{:S(2)}, u32[]{:S(2)}) collective-permute-start(f32[8,128]{1,0:T(8,128)S(1)} %shard_map.98), channel_id=1, source_target_pairs={{0,32},{32,64},{64,96},{96,0},{1,33},{33,65},{65,97},{97,1},{2,34}... | collective-permute-start | bytes 12296 | tf_op jit(solution)/shard_map/ppermute | solution.py:23
  69.7 3.6 %collective-permute-start.13 = (f32[8,128]{1,0:T(8,128)S(1)}, f32[8,128]{1,0:T(8,128)S(1)}, u32[]{:S(2)}, u32[]{:S(2)}) collective-permute-start(f32[8,128]{1,0:T(8,128)S(1)} %shard_map.98), channel_id=1, source_target_pairs={{0,96},{32,0},{64,32},{96,64},{1,97},{33,1},{65,33},{97,65},{2,98}... | collective-permute-start | bytes 12296 | tf_op jit(solution)/shard_map/ppermute | solution.py:23
  73.3 5.5 %collective-permute-start.14 = (f32[8,128]{1,0:T(8,128)S(1)}, f32[8,128]{1,0:T(8,128)S(1)}, u32[]{:S(2)}, u32[]{:S(2)}) collective-permute-start(f32[8,128]{1,0:T(8,128)S(1)} %add_add_fusion), channel_id=1, source_target_pairs={{0,16},{8,24},{16,0},{24,8},{1,17},{9,25},{17,1},{25,9},{2,18},{10... | collective-permute-start | bytes 12296 | tf_op jit(solution)/shard_map/ppermute | solution.py:23
  78.7 5.3 %collective-permute-start.15 = (f32[8,128]{1,0:T(8,128)S(1)}, f32[8,128]{1,0:T(8,128)S(1)}, u32[]{:S(2)}, u32[]{:S(2)}) collective-permute-start(f32[8,128]{1,0:T(8,128)S(1)} %add_add_fusion), channel_id=1, source_target_pairs={{0,8},{8,16},{16,24},{24,0},{1,9},{9,17},{17,25},{25,1},{2,10},{10... | collective-permute-start | bytes 12296 | tf_op jit(solution)/shard_map/ppermute | solution.py:23
  84.0 3.6 %collective-permute-start.16 = (f32[8,128]{1,0:T(8,128)S(1)}, f32[8,128]{1,0:T(8,128)S(1)}, u32[]{:S(2)}, u32[]{:S(2)}) collective-permute-start(f32[8,128]{1,0:T(8,128)S(1)} %add_add_fusion), channel_id=1, source_target_pairs={{0,24},{8,0},{16,8},{24,16},{1,25},{9,1},{17,9},{25,17},{2,26},{10... | collective-permute-start | bytes 12296 | tf_op jit(solution)/shard_map/ppermute | solution.py:23
  87.7 8.5 %collective-permute-start.20 = (bf16[896,256]{1,0:T(8,128)(2,1)S(1)}, bf16[896,256]{1,0:T(8,128)(2,1)S(1)}, u32[]{:S(2)}, u32[]{:S(2)}) collective-permute-start(bf16[896,256]{1,0:T(8,128)(2,1)S(1)} %get-tuple-element.35.gp_ref.r0), channel_id=1, source_target_pairs={{0,96},{1,33},{32,0},{33,65},{64,32},{65,97},{96,64},{97,1},{2,98}... | collective-permute-start | bytes 1376264 | tf_op jit(solution)/shard_map/ppermute | solution.py:31
  88.9 11.0 %collective-permute-start.26 = (bf16[4,224,256]{2,1,0:T(8,128)(2,1)S(1)}, bf16[4,224,256]{2,1,0:T(8,128)(2,1)S(1)}, u32[]{:S(2)}, u32[]{:S(2)}) collective-permute-start(bf16[4,224,256]{2,1,0:T(8,128)(2,1)S(1)} %get-tuple-element.55), channel_id=1, source_target_pairs={{0,8},{1,25},{8,16},{9,1},{16,24},{17,9},{24,0},{25,17},{2,10},{3,... | collective-permute-start | bytes 1376264 | tf_op jit(solution)/shard_map/ppermute | solution.py:31
  88.9 22.0 %collective-permute-start.30 = (bf16[1344,256]{1,0:T(8,128)(2,1)S(1)}, bf16[1344,256]{1,0:T(8,128)(2,1)S(1)}, u32[]{:S(2)}, u32[]{:S(2)}) collective-permute-start(bf16[1344,256]{1,0:T(8,128)(2,1)S(1)} %collective-permute-done.28.r1), channel_id=1, source_target_pairs={{0,8},{1,25},{8,16},{9,1},{16,24},{17,9},{24,0},{25,17},{2,10},{3,... | collective-permute-start | bytes 2064392 | tf_op jit(solution)/shard_map/ppermute | solution.py:31
  90.7 10.0 %collective-permute-start.18 = (bf16[896,256]{1,0:T(8,128)(2,1)S(1)}, bf16[896,256]{1,0:T(8,128)(2,1)S(1)}, u32[]{:S(2)}, u32[]{:S(2)}) collective-permute-start(bf16[896,256]{1,0:T(8,128)(2,1)S(1)} %collective-permute-done.17.l1), channel_id=1, source_target_pairs={{0,1},{1,0},{2,3},{3,2},{4,5},{5,4},{6,7},{7,6},{8,9},{9,8},{10,11... | collective-permute-start | bytes 1376264 | tf_op jit(solution)/shard_map/ppermute | solution.py:23
  90.7 24.1 %collective-permute-start.22 = (bf16[1344,256]{1,0:T(8,128)(2,1)S(1)}, bf16[1344,256]{1,0:T(8,128)(2,1)S(1)}, u32[]{:S(2)}, u32[]{:S(2)}) collective-permute-start(bf16[1344,256]{1,0:T(8,128)(2,1)S(1)} %collective-permute-done.21.m_ref), channel_id=1, source_target_pairs={{0,1},{1,0},{2,3},{3,2},{4,5},{5,4},{6,7},{7,6},{8,9},{9,8},{10,11... | collective-permute-start | bytes 2064392 | tf_op jit(solution)/shard_map/ppermute | solution.py:23
  96.1 8.0 %collective-permute-start.10 = (bf16[464,256]{1,0:T(8,128)(2,1)S(1)}, bf16[464,256]{1,0:T(8,128)(2,1)S(1)}, u32[]{:S(2)}, u32[]{:S(2)}) collective-permute-start(bf16[464,256]{1,0:T(8,128)(2,1)S(1)} %get-tuple-element.43), channel_id=1, source_target_pairs={{0,4},{2,6},{4,0},{6,2},{1,5},{3,7},{5,1},{7,3},{8,12},{10,14},{12... | collective-permute-start | bytes 712712 | tf_op jit(solution)/shard_map/ppermute | solution.py:23
  99.9 6.1 %collective-permute-start.8 = (bf16[464,256]{1,0:T(8,128)(2,1)S(1)}, bf16[464,256]{1,0:T(8,128)(2,1)S(1)}, u32[]{:S(2)}, u32[]{:S(2)}) collective-permute-start(bf16[464,256]{1,0:T(8,128)(2,1)S(1)} %get-tuple-element.41), channel_id=1, source_target_pairs={{0,6},{1,3},{2,0},{3,5},{4,2},{5,7},{6,4},{7,1},{8,14},{9,11},{10,... | collective-permute-start | bytes 712712 | tf_op jit(solution)/shard_map/ppermute | solution.py:31
  100.7 15.9 %collective-permute-start.29 = (bf16[896,256]{1,0:T(8,128)(2,1)S(1)}, bf16[896,256]{1,0:T(8,128)(2,1)S(1)}, u32[]{:S(2)}, u32[]{:S(2)}) collective-permute-start(bf16[896,256]{1,0:T(8,128)(2,1)S(1)} %get-tuple-element.56.r0), channel_id=1, source_target_pairs={{0,24},{1,9},{8,0},{9,17},{16,8},{17,25},{24,16},{25,1},{2,26},{3,... | collective-permute-start | bytes 1376264 | tf_op jit(solution)/shard_map/ppermute | solution.py:31
  104.1 12.4 %collective-permute-start.27 = (bf16[4,224,256]{2,1,0:T(8,128)(2,1)S(1)}, bf16[4,224,256]{2,1,0:T(8,128)(2,1)S(1)}, u32[]{:S(2)}, u32[]{:S(2)}) collective-permute-start(bf16[4,224,256]{2,1,0:T(8,128)(2,1)S(1)} %collective-permute-done.26.l1), channel_id=1, source_target_pairs={{0,1},{1,0},{2,3},{3,2},{4,5},{5,4},{6,7},{7,6},{8,9},{9,8},{10,11... | collective-permute-start | bytes 1376264 | tf_op jit(solution)/shard_map/ppermute | solution.py:23
  106.0 7.3 %collective-permute-start.9 = (bf16[464,256]{1,0:T(8,128)(2,1)S(1)}, bf16[464,256]{1,0:T(8,128)(2,1)S(1)}, u32[]{:S(2)}, u32[]{:S(2)}) collective-permute-start(bf16[464,256]{1,0:T(8,128)(2,1)S(1)} %get-tuple-element.42), channel_id=1, source_target_pairs={{0,2},{1,7},{2,4},{3,1},{4,6},{5,3},{6,0},{7,5},{8,10},{9,15},{10,... | collective-permute-start | bytes 712712 | tf_op jit(solution)/shard_map/ppermute | solution.py:31
  110.9 12.3 %collective-permute-start.31 = (bf16[1344,256]{1,0:T(8,128)(2,1)S(1)}, bf16[1344,256]{1,0:T(8,128)(2,1)S(1)}, u32[]{:S(2)}, u32[]{:S(2)}) collective-permute-start(bf16[1344,256]{1,0:T(8,128)(2,1)S(1)} %collective-permute-done.30.m_ref), channel_id=1, source_target_pairs={{0,1},{1,0},{2,3},{3,2},{4,5},{5,4},{6,7},{7,6},{8,9},{9,8},{10,11... | collective-permute-start | bytes 2064392 | tf_op jit(solution)/shard_map/ppermute | solution.py:23
  116.3 15.2 %collective-permute-start.23 = (bf16[240,896]{1,0:T(8,128)(2,1)S(1)}, bf16[240,896]{1,0:T(8,128)(2,1)S(1)}, u32[]{:S(2)}, u32[]{:S(2)}) collective-permute-start(bf16[240,896]{1,0:T(8,128)(2,1)S(1)} %get-tuple-element.51), channel_id=1, source_target_pairs={{0,8},{8,16},{16,24},{24,0},{1,9},{9,17},{17,25},{25,1},{2,10},{10... | collective-permute-start | bytes 1290248 | tf_op jit(solution)/shard_map/ppermute | solution.py:23
  118.2 20.4 %collective-permute-start.24 = (bf16[240,896]{1,0:T(8,128)(2,1)S(1)}, bf16[240,896]{1,0:T(8,128)(2,1)S(1)}, u32[]{:S(2)}, u32[]{:S(2)}) collective-permute-start(bf16[240,896]{1,0:T(8,128)(2,1)S(1)} %get-tuple-element.52), channel_id=1, source_target_pairs={{0,16},{8,24},{16,0},{24,8},{1,17},{9,25},{17,1},{25,9},{2,18},{10... | collective-permute-start | bytes 1290248 | tf_op jit(solution)/shard_map/ppermute | solution.py:23
  123.0 17.6 %collective-permute-start.25 = (bf16[240,896]{1,0:T(8,128)(2,1)S(1)}, bf16[240,896]{1,0:T(8,128)(2,1)S(1)}, u32[]{:S(2)}, u32[]{:S(2)}) collective-permute-start(bf16[240,896]{1,0:T(8,128)(2,1)S(1)} %get-tuple-element.53), channel_id=1, source_target_pairs={{0,24},{8,0},{16,8},{24,16},{1,25},{9,1},{17,9},{25,17},{2,26},{10... | collective-permute-start | bytes 1290248 | tf_op jit(solution)/shard_map/ppermute | solution.py:23
  124.7 18.6 %collective-permute-start.32 = (bf16[224,896]{1,0:T(8,128)(2,1)S(1)}, bf16[224,896]{1,0:T(8,128)(2,1)S(1)}, u32[]{:S(2)}, u32[]{:S(2)}) collective-permute-start(bf16[224,896]{1,0:T(8,128)(2,1)S(1)} %get-tuple-element.59), channel_id=1, source_target_pairs={{0,32},{32,64},{64,96},{96,0},{1,33},{33,65},{65,97},{97,1},{2,34}... | collective-permute-start | bytes 1204232 | tf_op jit(solution)/shard_map/ppermute | solution.py:23
  125.8 18.7 %collective-permute-start.33 = (bf16[224,896]{1,0:T(8,128)(2,1)S(1)}, bf16[224,896]{1,0:T(8,128)(2,1)S(1)}, u32[]{:S(2)}, u32[]{:S(2)}) collective-permute-start(bf16[224,896]{1,0:T(8,128)(2,1)S(1)} %get-tuple-element.60), channel_id=1, source_target_pairs={{0,64},{32,96},{64,0},{96,32},{1,65},{33,97},{65,1},{97,33},{2,66}... | collective-permute-start | bytes 1204232 | tf_op jit(solution)/shard_map/ppermute | solution.py:23
  131.5 13.0 %collective-permute-start.34 = (bf16[224,896]{1,0:T(8,128)(2,1)S(1)}, bf16[224,896]{1,0:T(8,128)(2,1)S(1)}, u32[]{:S(2)}, u32[]{:S(2)}) collective-permute-start(bf16[224,896]{1,0:T(8,128)(2,1)S(1)} %get-tuple-element.61), channel_id=1, source_target_pairs={{0,96},{32,0},{64,32},{96,64},{1,97},{33,1},{65,33},{97,65},{2,98}... | collective-permute-start | bytes 1204232 | tf_op jit(solution)/shard_map/ppermute | solution.py:23
  140.7 6.5 %collective-permute-start.35 = (f32[8,448]{1,0:T(8,128)S(1)}, f32[8,448]{1,0:T(8,128)S(1)}, u32[]{:S(2)}, u32[]{:S(2)}) collective-permute-start(f32[8,448]{1,0:T(8,128)S(1)} %shard_map.106), channel_id=1, source_target_pairs={{0,64},{32,96},{64,0},{96,32},{1,65},{33,97},{65,1},{97,33},{2,66}... | collective-permute-start | bytes 43016 | tf_op jit(solution)/shard_map/ppermute | solution.py:23
  141.3 5.8 %collective-permute-start.36 = (f32[8,448]{1,0:T(8,128)S(1)}, f32[8,448]{1,0:T(8,128)S(1)}, u32[]{:S(2)}, u32[]{:S(2)}) collective-permute-start(f32[8,448]{1,0:T(8,128)S(1)} %shard_map.106), channel_id=1, source_target_pairs={{0,32},{32,64},{64,96},{96,0},{1,33},{33,65},{65,97},{97,1},{2,34}... | collective-permute-start | bytes 43016 | tf_op jit(solution)/shard_map/ppermute | solution.py:23
  143.3 3.8 %collective-permute-start.37 = (f32[8,448]{1,0:T(8,128)S(1)}, f32[8,448]{1,0:T(8,128)S(1)}, u32[]{:S(2)}, u32[]{:S(2)}) collective-permute-start(f32[8,448]{1,0:T(8,128)S(1)} %shard_map.106), channel_id=1, source_target_pairs={{0,96},{32,0},{64,32},{96,64},{1,97},{33,1},{65,33},{97,65},{2,98}... | collective-permute-start | bytes 43016 | tf_op jit(solution)/shard_map/ppermute | solution.py:23
